TPU v7x, 128 devices: a whole 4x4x4 slice. The times are simulated.
128 devices in a mesh: gx: 4 (over y), gy: 8 (over z, x_lo), gz: 4 (over x_hi, core).
Axes of the slice: x: 4 (x_hi: 2, x_lo: 2; x = x_hi * 2 + x_lo), y: 4, z: 4, core: 2. Of those that a mesh axis runs over, the one named last changes fastest.
Arguments:
- node_latent: bfloat16 [64, 256, 16, 128], P('gx', 'gy', 'gz'), may hold values from -6 to 6
- edge_latent: bfloat16 [4, 8, 4, 12288, 128], P('gx', 'gy', 'gz'), may hold values from -6 to 6
- senders: int32 [4, 8, 4, 12288], P('gx', 'gy', 'gz'), may hold values from 7 to 3664, as said below
- receivers: int32 [4, 8, 4, 12288], P('gx', 'gy', 'gz'), may hold values from 0 to 2047, as said below
- w1_edge: bfloat16 [384, 128], replicated, may hold values from -0.3125 to 0.3125
- b1_edge: float32 [128], replicated, may hold values from -3 to 3
- w2_edge: bfloat16 [128, 128], replicated, may hold values from -0.5 to 0.5
- b2_edge: float32 [128], replicated, may hold values from -3 to 3
- w1_node: bfloat16 [256, 128], replicated, may hold values from -0.375 to 0.375
- b1_node: float32 [128], replicated, may hold values from -3 to 3
- w2_node: bfloat16 [128, 128], replicated, may hold values from -0.5 to 0.5
- cot_node: bfloat16 [64, 256, 16, 128], P('gx', 'gy', 'gz'), may hold values from -6 to 6
- cot_edge: bfloat16 [4, 8, 4, 12288, 128], P('gx', 'gy', 'gz'), may hold values from -8 to 8
Outputs:
- grad_node: bfloat16 [64, 256, 16, 128], P('gx', 'gy', 'gz')
- grad_edge: bfloat16 [4, 8, 4, 12288, 128], P('gx', 'gy', 'gz')
- grad_w1_edge: float32 [384, 128], replicated
- grad_w2_edge: float32 [128, 128], replicated
- grad_w1_node: float32 [256, 128], replicated
- grad_w2_node: float32 [128, 128], replicated
- grad_biases: float32 [4, 128], replicated
Inputs may be any that keep to these rules, and one draw needn't show every extreme that they name: `receivers`: in every block the list is nondecreasing; entry (i * 32 + j) * 4 + l names the block's cell at local coordinates (i, j, l). `senders`: entry (p * 34 + q) * 6 + r names the cell at local coordinates (p - 1, q - 1, r - 1) of the block extended by one cell on every side, the extension being cells of the adjacent blocks around the periodic box; it is always one of the six face neighbours of the same slot's receiver.
All inputs are finite; a program needn't handle non-finite values.
Results may differ from a plain program's by a relative error of at most 0.01.
Values may be sent and summed in bfloat16 or wider, within the bound.
No kernel may reach another device: no remote copies, remote signals or barrier semaphores. Data moves between devices by JAX's collectives and lax.ppermute only.
A program may use at most 128 MiB of HBM per device.

v0:
```python
import jax
import jax.numpy as jnp
from jax import lax
from jax.sharding import PartitionSpec as P


def with_halo(shard, sides, width):
    edges = {}
    for axis, dim in sides:
        peers, length = (lax.axis_size(axis), shard.shape[dim])
        up = [(i, (i + 1) % peers) for i in range(peers)]
        last = lax.slice_in_dim(shard, length - width, length, axis=dim)
        leading = lax.slice_in_dim(shard, 0, width, axis=dim)
        edges[dim] = (
            lax.ppermute(last, axis, up),
            lax.ppermute(leading, axis, [(b, a) for a, b in up]),
        )
    done = []
    for _, dim in sides:
        low, high = edges[dim]
        around = [(width, width) if d in done else (0, 0) for d in range(shard.ndim)]
        shard = jnp.concatenate([jnp.pad(low, around), shard, jnp.pad(high, around)], axis=dim)
        done.append(dim)
    return shard


def transposed_dot(left, right):
    return lax.dot_general(
        left, right, (((0,), (0,)), ((), ())), preferred_element_type=jnp.float32
    )


def column_sums(values):
    return jnp.sum(values.astype(jnp.float32), axis=0)


def silu_slope(values):
    sigma = jax.nn.sigmoid(values)
    return sigma * (1.0 + values * (1.0 - sigma))


def reduce_flat(flat_grads):
    return lax.psum(flat_grads, ("gx", "gy", "gz"))


def on_device(
    node_latent,
    edge_latent,
    senders,
    receivers,
    w1_edge,
    b1_edge,
    w2_edge,
    b2_edge,
    w1_node,
    b1_node,
    w2_node,
    cot_node,
    cot_edge,
):
    side_x, side_y, side_z, latent = node_latent.shape
    cell_count = side_x * side_y * side_z
    edge_count = edge_latent.shape[3]
    padded = with_halo(node_latent, (("gx", 0), ("gy", 1), ("gz", 2)), 1)
    flat_pad = padded.reshape(-1, latent)
    own_rows = node_latent.reshape(cell_count, latent)
    edge_rows = edge_latent.reshape(edge_count, latent)
    cot_rows = cot_edge.reshape(edge_count, latent)
    cot_cells = cot_node.reshape(cell_count, latent)
    sender_ids = senders.reshape(edge_count)
    receiver_ids = receivers.reshape(edge_count)
    sender_rows = jnp.take(flat_pad, sender_ids, axis=0)
    receiver_rows = jnp.take(own_rows, receiver_ids, axis=0)
    x_edge = jnp.concatenate([edge_rows, sender_rows, receiver_rows], axis=1)
    z_edge = jnp.dot(x_edge, w1_edge, preferred_element_type=jnp.float32) + b1_edge
    u_edge = jax.nn.silu(z_edge).astype(jnp.bfloat16)
    edge_new = (
        edge_rows.astype(jnp.float32)
        + jnp.dot(u_edge, w2_edge, preferred_element_type=jnp.float32)
        + b2_edge
    ).astype(jnp.bfloat16)
    aggregate = jax.ops.segment_sum(
        edge_new.astype(jnp.float32), receiver_ids, cell_count, indices_are_sorted=True
    ).astype(jnp.bfloat16)
    x_node = jnp.concatenate([own_rows, aggregate], axis=1)
    z_node = jnp.dot(x_node, w1_node, preferred_element_type=jnp.float32) + b1_node
    u_node = jax.nn.silu(z_node).astype(jnp.bfloat16)
    dz_node = (
        jnp.dot(cot_cells, w2_node.T, preferred_element_type=jnp.float32) * silu_slope(z_node)
    ).astype(jnp.bfloat16)
    dx_node = jnp.dot(dz_node, w1_node.T, preferred_element_type=jnp.float32)
    node_flat = jnp.concatenate(
        [
            transposed_dot(x_node, dz_node).reshape(-1),
            column_sums(dz_node),
            transposed_dot(u_node, cot_cells).reshape(-1),
            column_sums(cot_cells),
        ]
    )
    d_edge = (
        cot_rows.astype(jnp.float32) + jnp.take(dx_node[:, latent:], receiver_ids, axis=0)
    ).astype(jnp.bfloat16)
    dz_edge = (
        jnp.dot(d_edge, w2_edge.T, preferred_element_type=jnp.float32) * silu_slope(z_edge)
    ).astype(jnp.bfloat16)
    d_self = jnp.dot(dz_edge, w1_edge[:latent].T, preferred_element_type=jnp.float32)
    d_sender = jnp.dot(dz_edge, w1_edge[latent : 2 * latent].T, preferred_element_type=jnp.float32)
    d_receiver = jnp.dot(dz_edge, w1_edge[2 * latent :].T, preferred_element_type=jnp.float32)
    grad_edge = (
        (d_edge.astype(jnp.float32) + d_self).astype(jnp.bfloat16).reshape(edge_latent.shape)
    )
    edge_flat = jnp.concatenate(
        [
            transposed_dot(x_edge, dz_edge).reshape(-1),
            column_sums(dz_edge),
            transposed_dot(u_edge, d_edge).reshape(-1),
            column_sums(d_edge),
        ]
    )
    summed = (reduce_flat(jnp.concatenate([node_flat, edge_flat])),)
    send_grid = jax.ops.segment_sum(d_sender, sender_ids, flat_pad.shape[0]).reshape(
        side_x + 2, side_y + 2, side_z + 2, latent
    )
    receiver_sum = jax.ops.segment_sum(
        d_receiver, receiver_ids, cell_count, indices_are_sorted=True
    )
    own_terms = cot_cells.astype(jnp.float32) + dx_node[:, :latent] + receiver_sum
    interior = send_grid[1:-1, 1:-1, 1:-1] + own_terms.reshape(side_x, side_y, side_z, latent)
    extended = with_halo(
        send_grid.astype(jnp.bfloat16), (("gx", 0), ("gy", 1), ("gz", 2)), 1
    ).astype(send_grid.dtype)
    interior = interior.at[0].add(extended[0, 2:-2, 2:-2]).at[-1].add(extended[-1, 2:-2, 2:-2])
    interior = (
        interior.at[:, 0].add(extended[2:-2, 0, 2:-2]).at[:, -1].add(extended[2:-2, -1, 2:-2])
    )
    interior = (
        interior.at[:, :, 0].add(extended[2:-2, 2:-2, 0]).at[:, :, -1].add(extended[2:-2, 2:-2, -1])
    )
    grad_node = interior.astype(jnp.bfloat16)
    param_count = 7 * latent * latent + 4 * latent
    partial_value = sum((jnp.sum(portion * portion) for portion in summed))
    factor = 1.0 / jnp.maximum(1.0, jnp.sqrt(partial_value / param_count))
    scaled = [portion * factor for portion in summed]
    full_grads = scaled[0]
    square = latent * latent
    cut_a = 2 * square
    cut_b = cut_a + latent
    cut_c = cut_b + square
    cut_d = cut_c + latent
    cut_e = cut_d + 3 * square
    cut_f = cut_e + latent
    cut_g = cut_f + square
    grad_w1_node = full_grads[:cut_a].reshape(2 * latent, latent)
    bias_one_node = full_grads[cut_a:cut_b]
    grad_w2_node = full_grads[cut_b:cut_c].reshape(latent, latent)
    bias_two_node = full_grads[cut_c:cut_d]
    grad_w1_edge = full_grads[cut_d:cut_e].reshape(3 * latent, latent)
    bias_one_edge = full_grads[cut_e:cut_f]
    grad_w2_edge = full_grads[cut_f:cut_g].reshape(latent, latent)
    bias_two_edge = full_grads[cut_g:]
    grad_biases = jnp.stack([bias_one_edge, bias_two_edge, bias_one_node, bias_two_node])
    return (
        grad_node,
        grad_edge,
        grad_w1_edge,
        grad_w2_edge,
        grad_w1_node,
        grad_w2_node,
        grad_biases,
    )


def solution(mesh):
    placed = (
        P("gx", "gy", "gz", None),
        P("gx", "gy", "gz", None, None),
        P("gx", "gy", "gz", None),
        P("gx", "gy", "gz", None),
        P(),
        P(),
        P(),
        P(),
        P(),
        P(),
        P(),
        P("gx", "gy", "gz", None),
        P("gx", "gy", "gz", None, None),
    )
    return jax.shard_map(
        on_device,
        mesh=mesh,
        in_specs=placed,
        out_specs=(
            P("gx", "gy", "gz", None),
            P("gx", "gy", "gz", None, None),
            P(),
            P(),
            P(),
            P(),
            P(),
        ),
        check_vma=False,
    )
```

profile of v0, /device:TPU:1, one launch (start us, length us, event | category | flops | bytes accessed | tf_op | source)
XLA Modules:
  0.0 521.9 jit_solution(16961521660698633385)
XLA Ops:
  8.1 2.1 collective-permute-start.1
  10.2 3.6 collective-permute-start.4
  19.2 3.8 collective-permute-start
  28.0 43.3 %gather_fusion.1 = bf16[12288,128]{1,0:T(8,128)(2,1)} fusion(bf16[2048,128]{1,0:T(8,128)(2,1)S(1)} %bitcast.62, s32[12288]{0:T(1024)S(1)} %broadcast_clamp_fusion), kind=kCustom, calls=%fused_computation.1 | custom fusion | bytes 6340608 | tf_op jit(solution)/shard_map/jit(_take)/gather | solution.py:73
  71.4 2.1 fusion.34
  73.8 43.7 %gather_fusion = bf16[12288,128]{1,0:T(8,128)(2,1)} fusion(bf16[3672,128]{1,0:T(8,128)(2,1)S(1)} %reshape.366, s32[12288]{0:T(1024)S(1)} %broadcast_clamp_fusion.1), kind=kCustom, calls=%fused_computation | custom fusion | bytes 6340608 | tf_op jit(solution)/shard_map/jit(_take)/gather | solution.py:72
  117.5 9.2 %broadcast_select_fusion = (bf16[12288,128]{1,0:T(8,128)(2,1)S(1)}, bf16[12288,128]{1,0:T(8,128)(2,1)S(1)}) fusion(bf16[12288,128]{1,0:T(8,128)(2,1)} %gather_fusion, pred[12288]{0:T(1024)(128)(4,1)S(1)} %compare_and_fusion, bf16[12288,128]{1,0:T(8,128)(2,1)} %gather_fusion.1, pred[12288]{0:T(1024)(128)(4,1)S(1)} %compare_and_fusion.1), kind=kLoop, calls=%fused_computation.38 | loop fusion | flops 3145728 | bytes 12607488 | tf_op jit(solution)/shard_map/jit(_take)/select_n | solution.py:72
  126.8 3.0 convolution_add_fusion.2
  129.9 2.6 copy-done.25
  132.5 3.8 fusion.4
  136.3 76.1 %scatter_custom_fusion = f32[2048,128]{1,0:T(8,128)S(1)} fusion(s32[12288]{0:T(1024)S(1)} %bitcast.69, f32[12288,128]{1,0:T(8,128)} %fusion.4, f32[]{:T(128)} %constant.207.clone.1), kind=kCustom, calls=%fused_computation.83 | custom fusion | flops 1572864 | bytes 1049088 | tf_op jit(solution)/shard_map/scatter-add | solution.py:82
  215.6 41.2 %gather_fusion.2 = f32[12288,128]{1,0:T(8,128)} fusion(f32[2048,128]{1,0:T(8,128)S(1)} %get-tuple-element.81, s32[12288]{0:T(1024)S(1)} %broadcast_clamp_fusion), kind=kCustom, calls=%fused_computation.2 | custom fusion | bytes 12632064 | tf_op jit(solution)/shard_map/jit(_take)/gather | solution.py:101
  256.9 9.3 %convert_reduce_fusion = (f32[128]{0:T(128)S(1)}, bf16[12288,128]{1,0:T(8,128)(2,1)S(1)}) fusion(f32[12288,128]{1,0:T(8,128)} %gather_fusion.2, pred[12288]{0:T(1024)(128)(4,1)S(1)} %compare_and_fusion.1, bf16[1,1,1,12288,128]{4,3,2,1,0:T(8,128)(2,1)} %param.37), kind=kLoop, calls=%fused_computation.17 | loop fusion | flops 9437056 | bytes 12595712 | tf_op jit(solution)/shard_map/reduce_sum | solution.py:34
  266.2 5.4 %convolution_bitcast_fusion.2 = f32[16384]{0:T(1024)} fusion(bf16[12288,128]{1,0:T(8,128)(2,1)S(1)} %get-tuple-element.80, f32[12288,128]{1,0:T(8,128)} %copy-done.25), kind=kOutput, calls=%fused_computation.63 | convolution fusion | flops 410517504 | bytes 9502720 | tf_op jit(solution)/shard_map/dot_general | solution.py:28
  271.6 3.2 convert_reduce_fusion.1
  275.4 3.3 convolution_bitcast_fusion
  278.7 2.6 fusion.5
  281.3 3.6 fusion.47
  284.9 3.6 fusion.49
  288.5 66.6 %scatter_custom_fusion.1 = f32[3672,128]{1,0:T(8,128)S(1)} fusion(s32[12288]{0:T(1024)} %bitcast.74, f32[12288,128]{1,0:T(8,128)} %fusion.49, f32[]{:T(128)} %constant.207.clone.1), kind=kCustom, calls=%fused_computation.81 | custom fusion | flops 1572864 | bytes 1880576 | tf_op jit(solution)/shard_map/scatter-add | solution.py:121
  356.9 2.0 convert_element_type.85
  361.8 3.6 collective-permute-start.10
  365.5 2.6 collective-permute-start.9
  368.1 4.3 collective-permute-start.6
  372.5 76.2 %scatter_fusion = f32[2048,128]{1,0:T(8,128)S(1)} fusion(f32[2048,128]{1,0:T(8,128)S(1)} %get-tuple-element.82, s32[12288]{0:T(1024)S(1)} %bitcast.70, f32[12288,128]{1,0:T(8,128)} %fusion.47), kind=kCustom, calls=%fused_computation.5 | custom fusion | flops 1572864 | bytes 18923520 | tf_op jit(solution)/shard_map/scatter-add | solution.py:124
  449.3 2.0 slice_add_fusion.1
  451.3 5.5 %collective-permute-done.11 = bf16[18,34,1,128]{3,2,1,0:T(2,128)(2,1)S(1)} collective-permute-done((bf16[18,34,1,128]{3,2,1,0:T(2,128)(2,1)}, bf16[18,34,1,128]{3,2,1,0:T(2,128)(2,1)S(1)}, u32[]{:S(2)}, u32[]{:S(2)}) %collective-permute-start.11) | collective-permute-done | bytes 156704 | tf_op jit(solution)/shard_map/ppermute | solution.py:16
  456.8 3.4 fusion.30
  462.1 5.3 %scatter-add.58 = f32[16,32,4,128]{3,2,1,0:T(4,128)S(1)} dynamic-update-slice(f32[16,32,4,128]{3,2,1,0:T(4,128)S(1)} %fusion.44, f32[16,32,1,128]{3,2,1,0:T(1,128)S(1)} %slice_add_fusion.3, s32[]{:T(128)} %constant.208.clone.1, s32[]{:T(128)} %constant.208.clone.1, s32[]{:T(128)} %constant.208.clone.1, s32[]{:T(128)} %constant.208.clone.1) | dynamic-update-slice | bytes 524292 | tf_op jit(solution)/shard_map/scatter-add | solution.py:137
  467.4 2.1 slice_add_fusion.2
  469.5 5.3 %scatter-add.59 = f32[16,32,4,128]{3,2,1,0:T(4,128)S(1)} dynamic-update-slice(f32[16,32,4,128]{3,2,1,0:T(4,128)S(1)} %scatter-add.58, f32[16,32,1,128]{3,2,1,0:T(1,128)S(1)} %slice_add_fusion.2, s32[]{:T(128)} %constant.208.clone.1, s32[]{:T(128)} %constant.208.clone.1, s32[]{:T(128)} %constant.219.clone.1, s32[]{:T(128)} %constant.208.clone.1) | dynamic-update-slice | bytes 524292 | tf_op jit(solution)/shard_map/scatter-add | solution.py:137
  475.8 33.1 %all-reduce.10.cloned.1.call-done = f32[115200]{0:T(1024)} async-done(((f32[115200]{0:T(1024)}), f32[115200]{0:T(1024)}) %all-reduce.10.cloned.1.call-update) | async-done | bytes 460816 | tf_op jit(solution)/shard_map/psum | solution.py:43
  (117 shorter events, 29.1 us)
Async XLA Ops:
  7.2 205.3 %copy-start = (bf16[256,128]{1,0:T(8,128)(2,1)S(1)}, bf16[256,128]{1,0:T(8,128)(2,1)}, u32[]{:S(2)}) copy-start(bf16[256,128]{1,0:T(8,128)(2,1)} %param.33) | copy-start | bytes 196612
  7.2 20.8 %copy-start.2 = (bf16[16,32,4,128]{3,2,1,0:T(4,128)(2,1)S(1)}, bf16[16,32,4,128]{3,2,1,0:T(4,128)(2,1)}, u32[]{:S(2)}) copy-start(bf16[16,32,4,128]{3,2,1,0:T(4,128)(2,1)} %param.25) | copy-start | bytes 1572868
  7.2 501.7 %all-reduce.10.cloned.1.call-start = ((), (), s32[]{:S(2)}) async-start(), calls=%async_computation | async-start | bytes 925696 | tf_op jit(solution)/shard_map/psum | solution.py:43
  8.1 18.3 %collective-permute-start.1 = (bf16[16,1,4,128]{3,2,1,0:T(4,128)(2,1)S(1)}, bf16[16,1,4,128]{3,2,1,0:T(4,128)(2,1)S(1)}, u32[]{:S(2)}, u32[]{:S(2)}) collective-permute-start(bf16[16,1,4,128]{3,2,1,0:T(4,128)(2,1)S(1)} %get-tuple-element.93), channel_id=1, source_target_pairs={{0,4},{4,8},{8,12},{12,16},{16,20},{20,24},{24,28},{28,0},{1,5},{5... | collective-permute-start | bytes 49160 | tf_op jit(solution)/shard_map/ppermute | solution.py:15
  10.2 61.2 %collective-permute-start.4 = (bf16[16,1,4,128]{3,2,1,0:T(4,128)(2,1)S(1)}, bf16[16,1,4,128]{3,2,1,0:T(4,128)(2,1)S(1)}, u32[]{:S(2)}, u32[]{:S(2)}) collective-permute-start(bf16[16,1,4,128]{3,2,1,0:T(4,128)(2,1)S(1)} %get-tuple-element.94), channel_id=1, source_target_pairs={{4,0},{8,4},{12,8},{16,12},{20,16},{24,20},{28,24},{0,28},{5,1},{9... | collective-permute-start | bytes 49160 | tf_op jit(solution)/shard_map/ppermute | solution.py:16
  14.5 56.8 %collective-permute-start.2 = (bf16[1,32,4,128]{3,2,1,0:T(4,128)(2,1)S(1)}, bf16[1,32,4,128]{3,2,1,0:T(4,128)(2,1)S(1)}, u32[]{:S(2)}, u32[]{:S(2)}) collective-permute-start(bf16[1,32,4,128]{3,2,1,0:T(4,128)(2,1)S(1)} %get-tuple-element.89), channel_id=1, source_target_pairs={{0,32},{32,64},{64,96},{96,0},{1,33},{33,65},{65,97},{97,1},{2,34}... | collective-permute-start | bytes 98312 | tf_op jit(solution)/shard_map/ppermute | solution.py:15
  15.9 55.5 %collective-permute-start.3 = (bf16[1,32,4,128]{3,2,1,0:T(4,128)(2,1)S(1)}, bf16[1,32,4,128]{3,2,1,0:T(4,128)(2,1)S(1)}, u32[]{:S(2)}, u32[]{:S(2)}) collective-permute-start(bf16[1,32,4,128]{3,2,1,0:T(4,128)(2,1)S(1)} %get-tuple-element.90), channel_id=1, source_target_pairs={{32,0},{64,32},{96,64},{0,96},{33,1},{65,33},{97,65},{1,97},{34,2}... | collective-permute-start | bytes 98312 | tf_op jit(solution)/shard_map/ppermute | solution.py:16
  19.2 52.2 %collective-permute-start = (bf16[16,32,1,128]{3,2,1,0:T(2,128)(2,1)S(1)}, bf16[16,32,1,128]{3,2,1,0:T(2,128)(2,1)S(1)}, u32[]{:S(2)}, u32[]{:S(2)}) collective-permute-start(bf16[16,32,1,128]{3,2,1,0:T(2,128)(2,1)S(1)} %get-tuple-element.91), channel_id=1, source_target_pairs={{0,1},{1,2},{2,3},{3,0},{4,5},{5,6},{6,7},{7,4},{8,9},{9,10},{10,1... | collective-permute-start | bytes 393224 | tf_op jit(solution)/shard_map/ppermute | solution.py:15
  26.3 45.0 %collective-permute-start.5 = (bf16[16,32,1,128]{3,2,1,0:T(2,128)(2,1)S(1)}, bf16[16,32,1,128]{3,2,1,0:T(2,128)(2,1)S(1)}, u32[]{:S(2)}, u32[]{:S(2)}) collective-permute-start(bf16[16,32,1,128]{3,2,1,0:T(2,128)(2,1)S(1)} %get-tuple-element.92), channel_id=1, source_target_pairs={{1,0},{2,1},{3,2},{0,3},{5,4},{6,5},{7,6},{4,7},{9,8},{10,9},{11,1... | collective-permute-start | bytes 393224 | tf_op jit(solution)/shard_map/ppermute | solution.py:16
  117.5 9.3 %copy-start.12 = (bf16[384,128]{1,0:T(8,128)(2,1)S(1)}, bf16[384,128]{1,0:T(8,128)(2,1)}, u32[]{:S(2)}) copy-start(bf16[384,128]{1,0:T(8,128)(2,1)} %param.29) | copy-start | bytes 294916
  117.5 9.3 %copy-start.17 = (bf16[1,1,1,12288,128]{4,3,2,1,0:T(8,128)(2,1)S(1)}, bf16[1,1,1,12288,128]{4,3,2,1,0:T(8,128)(2,1)}, u32[]{:S(2)}) copy-start(bf16[1,1,1,12288,128]{4,3,2,1,0:T(8,128)(2,1)} %param.26) | copy-start | bytes 9437188
  117.5 9.3 %copy-start.21 = (f32[128]{0:T(128)S(1)}, f32[128]{0:T(128)}, u32[]{:S(2)}) copy-start(f32[128]{0:T(128)} %param.30) | copy-start | bytes 1540
  126.8 5.7 %copy-start.20 = (bf16[128,128]{1,0:T(8,128)(2,1)S(1)}, bf16[128,128]{1,0:T(8,128)(2,1)}, u32[]{:S(2)}) copy-start(bf16[128,128]{1,0:T(8,128)(2,1)} %param.31) | copy-start | bytes 98308
  126.8 5.7 %copy-start.22 = (f32[128]{0:T(128)S(1)}, f32[128]{0:T(128)}, u32[]{:S(2)}) copy-start(f32[128]{0:T(128)} %param.32) | copy-start | bytes 1540
  132.5 3.8 copy-start.10
  132.5 79.9 %copy-start.23 = (f32[128]{0:T(128)S(1)}, f32[128]{0:T(128)}, u32[]{:S(2)}) copy-start(f32[128]{0:T(128)} %param.34) | copy-start | bytes 1540
  136.3 76.6 %copy-start.8 = (bf16[16,32,4,128]{3,2,1,0:T(4,128)(2,1)S(1)}, bf16[16,32,4,128]{3,2,1,0:T(4,128)(2,1)}, u32[]{:S(2)}) copy-start(bf16[16,32,4,128]{3,2,1,0:T(4,128)(2,1)} %param.36) | copy-start | bytes 1572868
  256.9 14.7 %slice-start = ((s8[6291456]{0:T(1024)(128)(4,1)}), s8[4194304]{0:T(1024)(128)(4,1)S(1)}, s32[]{:S(2)}) async-start(s8[6291456]{0:T(1024)(128)(4,1)} %bitcast.77), calls=%async_computation.1 | async-start | bytes 8388608
  266.1 5.5 %slice-start.1 = ((s8[6291456]{0:T(1024)(128)(4,1)}), s8[2097152]{0:T(1024)(128)(4,1)S(1)}, s32[]{:S(2)}) async-start(s8[6291456]{0:T(1024)(128)(4,1)} %bitcast.77), calls=%async_computation.2 | async-start | bytes 4194304
  271.6 3.7 copy-start.18
  356.9 3.9 copy-start.13
  356.9 4.0 copy-start.11
  356.9 4.1 copy-start.24
  356.9 4.1 copy-start.14
  360.8 87.8 %collective-permute-start.7 = (bf16[18,1,6,128]{3,2,1,0:T(8,128)(2,1)S(1)}, bf16[18,1,6,128]{3,2,1,0:T(8,128)(2,1)S(1)}, u32[]{:S(2)}, u32[]{:S(2)}) collective-permute-start(bf16[18,1,6,128]{3,2,1,0:T(8,128)(2,1)S(1)} %get-tuple-element.87), channel_id=1, source_target_pairs={{0,4},{4,8},{8,12},{12,16},{16,20},{20,24},{24,28},{28,0},{1,5},{5... | collective-permute-start | bytes 82952 | tf_op jit(solution)/shard_map/ppermute | solution.py:15
  361.8 89.5 %collective-permute-start.10 = (bf16[18,1,6,128]{3,2,1,0:T(8,128)(2,1)S(1)}, bf16[18,1,6,128]{3,2,1,0:T(8,128)(2,1)S(1)}, u32[]{:S(2)}, u32[]{:S(2)}) collective-permute-start(bf16[18,1,6,128]{3,2,1,0:T(8,128)(2,1)S(1)} %get-tuple-element.88), channel_id=1, source_target_pairs={{4,0},{8,4},{12,8},{16,12},{20,16},{24,20},{28,24},{0,28},{5,1},{9... | collective-permute-start | bytes 82952 | tf_op jit(solution)/shard_map/ppermute | solution.py:16
  365.4 85.8 %collective-permute-start.8 = (bf16[1,34,6,128]{3,2,1,0:T(8,128)(2,1)}, bf16[1,34,6,128]{3,2,1,0:T(8,128)(2,1)}, u32[]{:S(2)}, u32[]{:S(2)}) collective-permute-start(bf16[1,34,6,128]{3,2,1,0:T(8,128)(2,1)} %get-tuple-element.83), channel_id=1, source_target_pairs={{0,32},{32,64},{64,96},{96,0},{1,33},{33,65},{65,97},{97,1},{2,34}... | collective-permute-start | bytes 156680 | tf_op jit(solution)/shard_map/ppermute | solution.py:15
  365.5 85.8 %collective-permute-start.9 = (bf16[1,34,6,128]{3,2,1,0:T(8,128)(2,1)}, bf16[1,34,6,128]{3,2,1,0:T(8,128)(2,1)}, u32[]{:S(2)}, u32[]{:S(2)}) collective-permute-start(bf16[1,34,6,128]{3,2,1,0:T(8,128)(2,1)} %get-tuple-element.84), channel_id=1, source_target_pairs={{32,0},{64,32},{96,64},{0,96},{33,1},{65,33},{97,65},{1,97},{34,2}... | collective-permute-start | bytes 156680 | tf_op jit(solution)/shard_map/ppermute | solution.py:16
  368.1 83.2 %collective-permute-start.6 = (bf16[18,34,1,128]{3,2,1,0:T(2,128)(2,1)}, bf16[18,34,1,128]{3,2,1,0:T(2,128)(2,1)}, u32[]{:S(2)}, u32[]{:S(2)}) collective-permute-start(bf16[18,34,1,128]{3,2,1,0:T(2,128)(2,1)} %get-tuple-element.85), channel_id=1, source_target_pairs={{0,1},{1,2},{2,3},{3,0},{4,5},{5,6},{6,7},{7,4},{8,9},{9,10},{10,1... | collective-permute-start | bytes 470024 | tf_op jit(solution)/shard_map/ppermute | solution.py:15
  448.6 8.1 %collective-permute-start.11 = (bf16[18,34,1,128]{3,2,1,0:T(2,128)(2,1)}, bf16[18,34,1,128]{3,2,1,0:T(2,128)(2,1)S(1)}, u32[]{:S(2)}, u32[]{:S(2)}) collective-permute-start(bf16[18,34,1,128]{3,2,1,0:T(2,128)(2,1)} %get-tuple-element.86), channel_id=1, source_target_pairs={{1,0},{2,1},{3,2},{0,3},{5,4},{6,5},{7,6},{4,7},{9,8},{10,9},{11,1... | collective-permute-start | bytes 470024 | tf_op jit(solution)/shard_map/ppermute | solution.py:16
  449.3 7.5 %copy-start.16 = (bf16[18,1,6,128]{3,2,1,0:T(8,128)(2,1)S(1)}, bf16[18,1,6,128]{3,2,1,0:T(8,128)(2,1)}, u32[]{:S(2)}) copy-start(bf16[18,1,6,128]{3,2,1,0:T(8,128)(2,1)} %copy-done.15) | copy-start | bytes 82948
  460.3 54.7 %copy-start.1 = (bf16[256,128]{1,0:T(8,128)(2,1)S(1)}, bf16[256,128]{1,0:T(8,128)(2,1)}, u32[]{:S(2)}) copy-start(bf16[256,128]{1,0:T(8,128)(2,1)} %param.33) | copy-start | bytes 196612
  (9 other events, 19.9 us)
Sparse Core Ops, SparseCore 0:
  361.9 146.8 all-reduce.9
where the time goes:
time: 523 us; the launch traced here: 522 us
  other arithmetic  259 us (50%)
  local copies, waits for them, and re-layouts  154 us (29%)
  waiting for transfers between devices  38.6 us (7%)
  matrix products  31.6 us (6%)
  starting transfers between devices  23.2 us (4%)
  between operations  15.3 us (3%)
    scatter-add x1, other arithmetic, on_device(): jax.ops.segment_sum(d_receiver, receiver_ids, cell_count, indices_are_sor...  76.2 us
    scatter-add x1, other arithmetic, on_device(): jax.ops.segment_sum(edge_new.astype(jnp.float32), receiver_ids, cell_coun...  76.1 us
    scatter-add x1, other arithmetic, on_device(): jax.ops.segment_sum(d_sender, sender_ids, flat_pad.shape[0])  66.6 us
    gather x1, local copies, waits for them, and re-layouts, on_device(): sender_rows = jnp.take(flat_pad, sender_ids, axis=0)  43.7 us
    gather x1, local copies, waits for them, and re-layouts, on_device(): receiver_rows = jnp.take(own_rows, receiver_ids, axis=0)  43.3 us
    gather x1, local copies, waits for them, and re-layouts, on_device(): jnp.take(dx_node[:, latent:], receiver_ids, axis=0)  41.2 us
    psum x1, waiting for transfers between devices, reduce_flat(): return lax.psum(flat_grads, ('gx', 'gy', 'gz'))  33.1 us
    ppermute x6, starting transfers between devices, with_halo(): lax.ppermute(last, axis, up)  11.7 us
  transfers between devices with their start and end apart: 13, of which 2 were waited for; matrix products, arithmetic and copies ran while one was open for 28% of the time, Pallas kernels for 0%

commit v1 on v0

v1 whole, which is shorter than its diff:
```python
import jax
import jax.numpy as jnp
from jax import lax
from jax.experimental import pallas as pl
from jax.experimental.pallas import tpu as pltpu
from jax.sharding import PartitionSpec as P

H = 128
PLANE = 128
N_PLANE = 16
CELLS = N_PLANE * PLANE
EDGES = 12288
TILE = 256
TILES = EDGES // TILE
WIN = 64
GROUP = 2
ROWS = CELLS + 128
PAD_ROWS = CELLS + 3 * PLANE
PARAM_ROWS = 1024
AXES = ("gx", "gy", "gz")
F32 = jnp.float32
BF16 = jnp.bfloat16


def dot(a, b):
    return lax.dot_general(a, b, (((1,), (0,)), ((), ())), preferred_element_type=F32)


def dot_first(a, b):
    return lax.dot_general(a, b, (((0,), (0,)), ((), ())), preferred_element_type=F32)


def flip(w):
    return w.astype(F32).T.astype(BF16)


def hot(mask):
    return jnp.where(mask, 1.0, 0.0).astype(BF16)


def iota(shape, dim):
    return lax.broadcasted_iota(jnp.int32, shape, dim)


def sigmoid(v):
    return 0.5 * jnp.tanh(0.5 * v) + 0.5


def layer_kernel(
    first_ref,
    last_ref,
    code_ref,
    node_ref,
    cotn_ref,
    xlo_ref,
    xhi_ref,
    ylo_ref,
    yhi_ref,
    zlo_ref,
    zhi_ref,
    e_ref,
    cot_ref,
    w1e_ref,
    b1e_ref,
    w2e_ref,
    b2e_ref,
    w1n_ref,
    b1n_ref,
    w2n_ref,
    gedge_ref,
    gown_ref,
    fx_ref,
    fy_ref,
    fz_ref,
    par_ref,
    own_ref,
    zx_ref,
    yx_ref,
    ppad_ref,
    tab_ref,
    col_ref,
    u_ref,
    slope_ref,
    eu_ref,
    deg_ref,
    dd_ref,
    spad_ref,
    acc_ref,
    wide_ref,
    zacc_ref,
    const_ref,
    flip_ref,
    sr_ref,
):
    w1a = w1e_ref[0:H]
    w1b = w1e_ref[H : 2 * H]
    w1c = w1e_ref[2 * H : 3 * H]
    par_ref[...] = jnp.zeros(par_ref.shape, F32)
    eu_ref[...] = jnp.zeros(eu_ref.shape, F32)
    deg_ref[...] = jnp.zeros(deg_ref.shape, F32)
    spad_ref[...] = jnp.zeros(spad_ref.shape, F32)
    acc_ref[...] = jnp.zeros(acc_ref.shape, F32)
    dd_ref[CELLS:ROWS] = jnp.zeros((ROWS - CELLS, 2 * H), BF16)
    tab_ref[:, CELLS:ROWS] = jnp.zeros((5, ROWS - CELLS, H), BF16)
    ppad_ref[CELLS + 2 * PLANE :] = jnp.zeros((PAD_ROWS - CELLS - 2 * PLANE, H), BF16)
    const_ref[:, 0:H] = flip(w2e_ref[...])
    const_ref[:, H:] = hot(iota((H, H), 0) == iota((H, H), 1))
    flip_ref[0:H] = flip(w1b)
    flip_ref[H : 2 * H] = flip(w1c)
    flip_ref[2 * H : 3 * H] = flip(w1a)

    ppad_ref[0:PLANE] = dot(xlo_ref[...], w1b).astype(BF16)
    ppad_ref[CELLS + PLANE : CELLS + 2 * PLANE] = dot(xhi_ref[...], w1b).astype(BF16)
    yx_ref[0:PLANE] = dot(ylo_ref[...], w1b)
    yx_ref[PLANE : 2 * PLANE] = dot(yhi_ref[...], w1b)
    zx_ref[pl.ds(0, CELLS // 4, 4), :] = dot(zlo_ref[...], w1b)
    zx_ref[pl.ds(3, CELLS // 4, 4), :] = dot(zhi_ref[...], w1b)
    w1bc = jnp.concatenate([w1b, w1c], axis=1)
    row = iota((PLANE, H), 0)
    at_low = (row & 3) == 0
    at_high = (row & 3) == 3

    def prepare(i, carry):
        base = pl.multiple_of(i * PLANE, PLANE)
        both = dot(node_ref[pl.ds(base, PLANE), :], w1bc)
        p = both[:, 0:H]
        tab_ref[4, pl.ds(base, PLANE), :] = (both[:, H:] + b1e_ref[...]).astype(BF16)
        ppad_ref[pl.ds(base + PLANE, PLANE), :] = p.astype(BF16)
        ylow = yx_ref[pl.ds(pl.multiple_of(i * 8, 8), 8), :]
        yhigh = yx_ref[pl.ds(pl.multiple_of(PLANE + i * 8, 8), 8), :]
        pad = jnp.zeros((PLANE - 8, H), F32)
        low_full = jnp.concatenate([ylow, pad], axis=0)
        high_full = jnp.concatenate([pad, yhigh], axis=0)
        up = jnp.where(row < PLANE - 4, pltpu.roll(p, PLANE - 4, 0), pltpu.roll(high_full, 4, 0))
        down = jnp.where(row >= 4, pltpu.roll(p, 4, 0), pltpu.roll(low_full, PLANE - 4, 0))
        tab_ref[0, pl.ds(base, PLANE), :] = up.astype(BF16)
        tab_ref[1, pl.ds(base, PLANE), :] = down.astype(BF16)
        zx = zx_ref[pl.ds(base, PLANE), :]
        tab_ref[2, pl.ds(base, PLANE), :] = jnp.where(
            at_high, zx, pltpu.roll(p, PLANE - 1, 0)
        ).astype(BF16)
        tab_ref[3, pl.ds(base, PLANE), :] = jnp.where(at_low, zx, pltpu.roll(p, 1, 0)).astype(BF16)
        return carry

    lax.fori_loop(0, N_PLANE, prepare, 0)

    lane = iota((TILE, H), 1)
    lane_code = (lane >> 6) * 4096 + (lane & 63)
    lane_self = jnp.where(lane < WIN, lane, -(1 << 20))
    srow = iota((H, TILE), 0)
    srow_code = (srow >> 6) * 4096 + (srow & 63)
    wrow = iota((WIN, TILE), 0)

    def start_of(t):
        return pl.multiple_of((first_ref[t] >> 4) << 4, 16)

    def windows_of(t):
        return ((last_ref[t] - start_of(t)) >> 6) + 1

    def rows_of(t):
        return pl.ds(pl.multiple_of(t * TILE, TILE), TILE)

    def columns(t):
        line = code_ref[pl.ds(t, 1), :].astype(F32)
        parts = [
            jnp.broadcast_to(line[:, k * H : (k + 1) * H], (H, H)).T for k in range(TILE // H)
        ]
        return jnp.concatenate(parts, axis=0).astype(jnp.int32)

    def gather_pre(col, w):
        shifted = col - w
        inner = (col & 4095) - w
        parts = [hot(shifted == lane_code + k * 8192) for k in range(3)]
        left = jnp.concatenate(parts + [hot(inner == lane_self)], axis=1)
        right = jnp.concatenate(
            [
                ppad_ref[pl.ds(w + 2 * PLANE, WIN), :],
                ppad_ref[pl.ds(w, WIN), :],
            ]
            + [tab_ref[k, pl.ds(w, WIN), :] for k in range(5)]
            + [jnp.zeros((WIN, H), BF16)],
            axis=0,
        )
        return dot(left, right)

    def activate(t, z):
        s = sigmoid(z)
        u = z * s
        ub = u.astype(BF16)
        u_ref[rows_of(t), :] = ub
        slope_ref[rows_of(t), :] = (s + u * (1.0 - s)).astype(BF16)
        return ub

    def collect(t, w, eu):
        picked = ((code_ref[pl.ds(t, 1), :] & 4095) - w) == wrow
        ones = jnp.where(picked, 1.0, 0.0)
        eu_ref[pl.ds(w, WIN), :] += dot(ones.astype(BF16), eu)
        deg_ref[pl.ds(w, WIN), :] += jnp.broadcast_to(
            jnp.sum(ones, axis=1, keepdims=True), (WIN, H)
        )

    def forward_fast(t):
        col = columns(t)
        col_ref[rows_of(t), :] = col
        e = e_ref[rows_of(t), :]
        w = start_of(t)
        ub = activate(t, gather_pre(col, w) + dot(e, w1a))
        collect(t, w, jnp.concatenate([e, ub], axis=1))

    def forward_slow(t):
        col_ref[rows_of(t), :] = columns(t)
        zacc_ref[:, 0:H] = dot(e_ref[rows_of(t), :], w1a)

        def more(k, carry):
            w = pl.multiple_of(start_of(t) + k * WIN, 16)
            zacc_ref[:, 0:H] += gather_pre(col_ref[rows_of(t), :], w)
            return carry

        lax.fori_loop(0, windows_of(t), more, 0)
        activate(t, zacc_ref[:, 0:H])

        def put(k, carry):
            w = pl.multiple_of(start_of(t) + k * WIN, 16)
            collect(t, w, jnp.concatenate([e_ref[rows_of(t), :], u_ref[rows_of(t), :]], axis=1))
            return carry

        lax.fori_loop(0, windows_of(t), put, 0)

    def each_group(fast, slow):
        def body(g, carry):
            tiles = [g * GROUP + k for k in range(GROUP)]
            fits = windows_of(tiles[0]) <= 1
            for t in tiles[1:]:
                fits = jnp.logical_and(fits, windows_of(t) <= 1)

            @pl.when(fits)
            def _():
                for t in tiles:
                    fast(t)

            @pl.when(jnp.logical_not(fits))
            def _():
                for t in tiles:
                    slow(t)

            return carry

        lax.fori_loop(0, TILES // GROUP, body, 0)

    each_group(forward_fast, forward_slow)

    w2n_flip = flip(w2n_ref[...])
    w1n_flip = jnp.concatenate([flip(w1n_ref[0:H]), flip(w1n_ref[H : 2 * H])], axis=1)

    def cells(k, carry):
        at = pl.ds(pl.multiple_of(k * TILE, TILE), TILE)
        eu = eu_ref[at, :]
        usum = eu[:, H:]
        uh = usum.astype(BF16)
        ul = (usum - uh.astype(F32)).astype(BF16)
        w2 = w2e_ref[...]
        agg = (eu[:, 0:H] + deg_ref[at, :] * b2e_ref[...]) + dot(
            jnp.concatenate([uh, ul], axis=1), jnp.concatenate([w2, w2], axis=0)
        )
        x = jnp.concatenate([node_ref[at, :], agg.astype(BF16)], axis=1)
        z = dot(x, w1n_ref[...]) + b1n_ref[...]
        s = sigmoid(z)
        u = z * s
        cot = cotn_ref[at, :]
        dz = (dot(cot, w2n_flip) * (s + u * (1.0 - s))).astype(BF16)
        dx = dot(dz, w1n_flip)
        cot32 = cot.astype(F32)
        gown_ref[at, :] = cot32 + dx[:, 0:H]
        dagg = dx[:, H:].astype(BF16)
        dd_ref[at, 0:H] = dot(dagg, const_ref[:, 0:H]).astype(BF16)
        dd_ref[at, H:] = dagg
        par_ref[4 * H : 6 * H, :] += dot_first(x, dz)
        par_ref[6 * H : 7 * H, :] += dot_first(u.astype(BF16), cot)
        par_ref[7 * H + 2 : 7 * H + 3, :] += jnp.sum(dz.astype(F32), axis=0, keepdims=True)
        par_ref[7 * H + 3 : 7 * H + 4, :] += jnp.sum(cot32, axis=0, keepdims=True)
        return carry

    lax.fori_loop(0, CELLS // TILE, cells, 0)

    def spread(col, w, cot):
        left = jnp.concatenate([hot((col & 4095) - w == lane), cot], axis=1)
        right = jnp.concatenate([dd_ref[pl.ds(w, H), :], const_ref[...]], axis=0)
        return dot(left, right)

    def scatter(t, w, dz):
        shifted = code_ref[pl.ds(t, 1), :] - w
        inner = (code_ref[pl.ds(t, 1), :] & 4095) - w
        parts = [hot(shifted == srow_code + k * 8192) for k in range(3)]
        sums = dot(jnp.concatenate(parts + [hot(inner == wrow)], axis=0), dz)
        spad_ref[pl.ds(w + 2 * PLANE, WIN), :] += sums[0:WIN]
        spad_ref[pl.ds(w, WIN), :] += sums[WIN : 2 * WIN]
        for k in range(5):
            acc_ref[k, pl.ds(w, WIN), :] += sums[(k + 2) * WIN : (k + 3) * WIN]

    def finish_edges(t, dd):
        d32 = dd[:, H:]
        d = d32.astype(BF16)
        d32 = d.astype(F32)
        dz = (dd[:, 0:H] * slope_ref[rows_of(t), :].astype(F32)).astype(BF16)
        gedge_ref[rows_of(t), :] = (d32 + dot(dz, flip_ref[2 * H : 3 * H])).astype(BF16)
        wide_ref[0:H, :] += dot_first(e_ref[rows_of(t), :], dz)
        wide_ref[H : 2 * H, :] += dot_first(u_ref[rows_of(t), :], d)
        wide_ref[2 * H : 2 * H + 8, :] += jnp.sum(d32.reshape(TILE // 8, 8, H), axis=0)
        return dz

    def backward_fast(t):
        w = start_of(t)
        dz = finish_edges(t, spread(col_ref[rows_of(t), :], w, cot_ref[rows_of(t), :]))
        scatter(t, w, dz)

    def backward_slow(t):
        zacc_ref[...] = dot(cot_ref[rows_of(t), :], const_ref[...])

        def more(k, carry):
            w = pl.multiple_of(start_of(t) + k * H, 16)
            zacc_ref[...] += spread(
                col_ref[rows_of(t), :], w, jnp.zeros((TILE, H), BF16)
            )
            return carry

        lax.fori_loop(0, (windows_of(t) + 1) >> 1, more, 0)
        own_ref[...] = finish_edges(t, zacc_ref[...])

        def put(k, carry):
            scatter(t, pl.multiple_of(start_of(t) + k * WIN, 16), own_ref[...])
            return carry

        lax.fori_loop(0, windows_of(t), put, 0)

    wide_ref[...] = jnp.zeros(wide_ref.shape, F32)
    each_group(backward_fast, backward_slow)

    row8 = iota((8, H), 0)

    def gather_cells(i, carry):
        base = pl.multiple_of(i * PLANE, PLANE)
        at = pl.ds(base, PLANE)
        yp = acc_ref[0, at, :]
        ym = acc_ref[1, at, :]
        zp = acc_ref[2, at, :]
        zm = acc_ref[3, at, :]
        zero = jnp.zeros((PLANE, H), F32)
        total = spad_ref[pl.ds(base + PLANE, PLANE), :]
        total += jnp.where(row >= 4, pltpu.roll(yp, 4, 0), zero)
        total += jnp.where(row < PLANE - 4, pltpu.roll(ym, PLANE - 4, 0), zero)
        total += jnp.where(at_low, zero, pltpu.roll(zp, 1, 0))
        total += jnp.where(at_high, zero, pltpu.roll(zm, PLANE - 1, 0))
        sr = jnp.concatenate([total, acc_ref[4, at, :]], axis=1)
        par_ref[7 * H : 7 * H + 1, :] += jnp.sum(acc_ref[4, at, :], axis=0, keepdims=True)
        sr16 = sr.astype(BF16)
        sr_ref[at, :] = sr16
        gown_ref[at, :] += dot(sr16, flip_ref[0 : 2 * H])
        eight = pl.multiple_of(i * 8, 8)
        yx_ref[pl.ds(eight, 8), :] = jnp.where(row8 >= 4, pltpu.roll(ym[0:8], 4, 0), 0.0)
        yx_ref[pl.ds(PLANE + eight, 8), :] = jnp.where(
            row8 < 4, pltpu.roll(yp[PLANE - 8 :], 4, 0), 0.0
        )
        return carry

    lax.fori_loop(0, N_PLANE, gather_cells, 0)
    both = dot_first(node_ref[...], sr_ref[...])
    w1b_flip = flip_ref[0:H]
    sx_lo = spad_ref[0:PLANE].astype(BF16)
    sx_hi = spad_ref[CELLS + PLANE : CELLS + 2 * PLANE].astype(BF16)
    sy_lo = yx_ref[0:PLANE].astype(BF16)
    sy_hi = yx_ref[PLANE : 2 * PLANE].astype(BF16)
    zx_ref[...] = acc_ref[3, 0:CELLS, :]
    sz_lo = zx_ref[pl.ds(0, CELLS // 4, 4), :].astype(BF16)
    zx_ref[...] = acc_ref[2, 0:CELLS, :]
    sz_hi = zx_ref[pl.ds(3, CELLS // 4, 4), :].astype(BF16)
    fx_ref[0] = dot(sx_lo, w1b_flip).astype(BF16)
    fx_ref[1] = dot(sx_hi, w1b_flip).astype(BF16)
    fy_ref[0] = dot(sy_lo, w1b_flip).astype(BF16)
    fy_ref[1] = dot(sy_hi, w1b_flip).astype(BF16)
    fz_ref[0] = dot(sz_lo, w1b_flip).astype(BF16)
    fz_ref[1] = dot(sz_hi, w1b_flip).astype(BF16)
    halo_x = dot_first(xlo_ref[...], sx_lo) + dot_first(xhi_ref[...], sx_hi)
    halo_y = dot_first(ylo_ref[...], sy_lo) + dot_first(yhi_ref[...], sy_hi)
    halo_z = dot_first(zlo_ref[...], sz_lo) + dot_first(zhi_ref[...], sz_hi)
    par_ref[0:H, :] = wide_ref[0:H, :]
    par_ref[H : 2 * H, :] = both[:, 0:H] + halo_x + halo_y + halo_z
    par_ref[2 * H : 3 * H, :] = both[:, H:]
    par_ref[3 * H : 4 * H, :] = wide_ref[H : 2 * H, :]
    par_ref[7 * H + 1 : 7 * H + 2, :] = jnp.sum(
        wide_ref[2 * H : 2 * H + 8, :], axis=0, keepdims=True
    )


def layer_call(first, last, code, *arrays):
    smem = pl.BlockSpec(memory_space=pltpu.SMEM)
    vmem = pl.BlockSpec(memory_space=pltpu.VMEM)
    return pl.pallas_call(
        layer_kernel,
        in_specs=[smem, smem] + [vmem] * 18,
        out_specs=[vmem] * 6,
        out_shape=[
            jax.ShapeDtypeStruct((EDGES, H), BF16),
            jax.ShapeDtypeStruct((CELLS, H), F32),
            jax.ShapeDtypeStruct((2, PLANE, H), BF16),
            jax.ShapeDtypeStruct((2, PLANE, H), BF16),
            jax.ShapeDtypeStruct((2, CELLS // 4, H), BF16),
            jax.ShapeDtypeStruct((PARAM_ROWS, H), F32),
        ],
        scratch_shapes=[
            pltpu.VMEM((TILE, H), BF16),
            pltpu.VMEM((CELLS, H), F32),
            pltpu.VMEM((2 * PLANE, H), F32),
            pltpu.VMEM((PAD_ROWS, H), BF16),
            pltpu.VMEM((5, ROWS, H), BF16),
            pltpu.VMEM((EDGES, H), jnp.int32),
            pltpu.VMEM((EDGES, H), BF16),
            pltpu.VMEM((EDGES, H), BF16),
            pltpu.VMEM((ROWS, 2 * H), F32),
            pltpu.VMEM((ROWS, H), F32),
            pltpu.VMEM((ROWS, 2 * H), BF16),
            pltpu.VMEM((PAD_ROWS, H), F32),
            pltpu.VMEM((5, ROWS, H), F32),
            pltpu.VMEM((2 * H + 8, H), F32),
            pltpu.VMEM((TILE, 2 * H), F32),
            pltpu.VMEM((H, 2 * H), BF16),
            pltpu.VMEM((3 * H, H), BF16),
            pltpu.VMEM((CELLS, 2 * H), BF16),
        ],
        compiler_params=pltpu.CompilerParams(vmem_limit_bytes=60 * 1024 * 1024),
        name="layer",
    )(first, last, code, *arrays)


def finish_kernel(
    gown_ref,
    xlo_ref,
    xhi_ref,
    ylo_ref,
    yhi_ref,
    zlo_ref,
    zhi_ref,
    par_ref,
    gnode_ref,
    w1e_ref,
    w2e_ref,
    w1n_ref,
    w2n_ref,
    bias_ref,
    sum_ref,
):
    par = par_ref[0 : 7 * H + 8, :]
    square = jnp.sum(par * par)
    factor = 1.0 / jnp.maximum(1.0, jnp.sqrt(jnp.full((1, H), square / (7 * H * H + 4 * H), F32)))
    w1e_ref[...] = par_ref[0 : 3 * H, :] * factor
    w2e_ref[...] = par_ref[3 * H : 4 * H, :] * factor
    w1n_ref[...] = par_ref[4 * H : 6 * H, :] * factor
    w2n_ref[...] = par_ref[6 * H : 7 * H, :] * factor
    bias_ref[...] = par_ref[7 * H : 7 * H + 4, :] * factor
    sum_ref[...] = gown_ref[...]
    sum_ref[0:PLANE] += xlo_ref[...].astype(F32)
    sum_ref[CELLS - PLANE :] += xhi_ref[...].astype(F32)
    for i in range(N_PLANE):
        low = ylo_ref[i * 8 : i * 8 + 8, :].astype(F32)
        high = yhi_ref[i * 8 : i * 8 + 8, :].astype(F32)
        sum_ref[i * PLANE : i * PLANE + 8, :] += low
        sum_ref[(i + 1) * PLANE - 8 : (i + 1) * PLANE, :] += high
    sum_ref[pl.ds(0, CELLS // 4, 4), :] += zlo_ref[...].astype(F32)
    sum_ref[pl.ds(3, CELLS // 4, 4), :] += zhi_ref[...].astype(F32)
    gnode_ref[...] = sum_ref[...].astype(BF16)


def finish_call(*arrays):
    return pl.pallas_call(
        finish_kernel,
        in_specs=[pl.BlockSpec(memory_space=pltpu.VMEM)] * 8,
        out_specs=[pl.BlockSpec(memory_space=pltpu.VMEM)] * 6,
        out_shape=[
            jax.ShapeDtypeStruct((CELLS, H), BF16),
            jax.ShapeDtypeStruct((3 * H, H), F32),
            jax.ShapeDtypeStruct((H, H), F32),
            jax.ShapeDtypeStruct((2 * H, H), F32),
            jax.ShapeDtypeStruct((H, H), F32),
            jax.ShapeDtypeStruct((4, H), F32),
        ],
        scratch_shapes=[pltpu.VMEM((CELLS, H), F32)],
        name="finish",
    )(*arrays)


def from_previous(value, axis):
    n = lax.axis_size(axis)
    return lax.ppermute(value, axis, [(k, (k + 1) % n) for k in range(n)])


def from_next(value, axis):
    n = lax.axis_size(axis)
    return lax.ppermute(value, axis, [((k + 1) % n, k) for k in range(n)])


def edge_codes(senders, receivers):
    r = receivers.reshape(TILES, TILE)
    s = senders.reshape(TILES, TILE)
    home = ((r >> 7) + 1) * 204 + (((r >> 2) & 31) + 1) * 6 + (r & 3) + 1
    delta = s - home
    size = jnp.abs(delta)
    side = jnp.where(size == 204, 0, jnp.where(size == 6, 2, 4)) + (delta < 0).astype(jnp.int32)
    return r[:, 0], r[:, -1], side * 4096 + r


def sum_over_devices(rows):
    count = 1
    for axis in AXES:
        count *= lax.axis_size(axis)
    chunks = rows.reshape(count, -1, H)
    mine = jnp.sum(lax.all_to_all(chunks, AXES, 0, 0, tiled=True), axis=0)
    copies = jnp.broadcast_to(mine[None], (count,) + mine.shape)
    return lax.all_to_all(copies, AXES, 0, 0, tiled=True).reshape(-1, H)


def on_device(
    node_latent,
    edge_latent,
    senders,
    receivers,
    w1_edge,
    b1_edge,
    w2_edge,
    b2_edge,
    w1_node,
    b1_node,
    w2_node,
    cot_node,
    cot_edge,
):
    zlo = from_previous(node_latent[:, :, 3], "gz").reshape(-1, H)
    zhi = from_next(node_latent[:, :, 0], "gz").reshape(-1, H)
    ylo = from_previous(node_latent[:, 30:32], "gy").reshape(-1, H)
    yhi = from_next(node_latent[:, 0:2], "gy").reshape(-1, H)
    xlo = from_previous(node_latent[15], "gx").reshape(-1, H)
    xhi = from_next(node_latent[0], "gx").reshape(-1, H)
    first, last, code = edge_codes(senders, receivers)
    gedge, gown, fx, fy, fz, par = layer_call(
        first,
        last,
        code,
        node_latent.reshape(CELLS, H),
        cot_node.reshape(CELLS, H),
        xlo,
        xhi,
        ylo,
        yhi,
        zlo,
        zhi,
        edge_latent.reshape(EDGES, H),
        cot_edge.reshape(EDGES, H),
        w1_edge,
        b1_edge.reshape(1, H),
        w2_edge,
        b2_edge.reshape(1, H),
        w1_node,
        b1_node.reshape(1, H),
        w2_node,
    )
    full = sum_over_devices(par)
    gnode, gw1e, gw2e, gw1n, gw2n, gbias = finish_call(
        gown,
        from_previous(fx[1], "gx"),
        from_next(fx[0], "gx"),
        from_previous(fy[1], "gy"),
        from_next(fy[0], "gy"),
        from_previous(fz[1], "gz"),
        from_next(fz[0], "gz"),
        full,
    )
    return (
        gnode.reshape(node_latent.shape),
        gedge.reshape(edge_latent.shape),
        gw1e,
        gw2e,
        gw1n,
        gw2n,
        gbias,
    )


def solution(mesh):
    cells = P("gx", "gy", "gz", None)
    edges = P("gx", "gy", "gz", None, None)
    return jax.shard_map(
        on_device,
        mesh=mesh,
        in_specs=(cells, edges, cells, cells) + (P(),) * 7 + (cells, edges),
        out_specs=(cells, edges) + (P(),) * 5,
        check_vma=False,
    )
```

time: 523 us -> 127 us (0.24)
  other arithmetic: 259 us -> 3.92 us
  local copies, waits for them, and re-layouts: 154 us -> 7.23 us
  Pallas kernels: 0 us -> 56.9 us
  matrix products: 31.6 us -> 0 us
  waiting for transfers between devices: 38.6 us -> 9.02 us
  blocking collectives: 0 us -> 22.2 us
  between operations: 15.3 us -> 0.87 us
    scatter-add x7 -> x0, other arithmetic: 219 us -> none  [the longest x1 76.2 us: on_device(): jax.ops.segment_sum(d_receiver, receiver_ids, cell_count, indices_are_sor...]
    gather x3 -> x0, local copies, waits for them, and re-layouts: 128 us -> none  [the longest x1 43.7 us: on_device(): sender_rows = jnp.take(flat_pad, sender_ids, axis=0)]
    pallas_call x0 -> x2, Pallas kernels: none -> 56.9 us  [the longest x1 54.2 us: layer_call(): pl.pallas_call(layer_kernel, in_specs=[smem, smem] + [vmem] * 18, out_spe...]
    psum x1 -> x0, waiting for transfers between devices: 33.1 us -> none  [reduce_flat(): return lax.psum(flat_grads, ('gx', 'gy', 'gz'))]
    dot_general x13 -> x0, matrix products: 31.6 us -> none  [the longest x4 10.3 us: transposed_dot(): lax.dot_general(left, right, (((0,), (0,)), ((), ())), preferred_element_...]
    all_to_all x0 -> x1, blocking collectives: none -> 22.2 us  [sum_over_devices(): mine = jnp.sum(lax.all_to_all(chunks, AXES, 0, 0, tiled=True), axis=0)]
    reduce_sum x3 -> x1, other arithmetic: 12.6 us -> 0.14 us  [sum_over_devices(): mine = jnp.sum(lax.all_to_all(chunks, AXES, 0, 0, tiled=True), axis=0)]
    select_n x3 -> x0, other arithmetic: 10.9 us -> none  [the longest x2 10.1 us: on_device(): sender_rows = jnp.take(flat_pad, sender_ids, axis=0)]
  transfers between devices with their start and end apart: 13 -> 13, of which waited for: 2 -> 3; matrix products, arithmetic and copies ran while one was open for 28% -> 6% of each run, Pallas kernels for 0% -> 0%
where the time goes in v1:
time: 127 us
  Pallas kernels  56.9 us (45%)
  starting transfers between devices  26.3 us (21%)
  blocking collectives  22.2 us (17%)
  waiting for transfers between devices  9.02 us (7%)
  local copies, waits for them, and re-layouts  7.23 us (6%)
  other arithmetic  3.92 us (3%)
    pallas_call x1, Pallas kernels, layer_call(): pl.pallas_call(layer_kernel, in_specs=[smem, smem] + [vmem] * 18, out_spe...  54.2 us
    all_to_all x1, blocking collectives, sum_over_devices(): mine = jnp.sum(lax.all_to_all(chunks, AXES, 0, 0, tiled=True), axis=0)  22.2 us
    ppermute x6, starting transfers between devices, from_next(): return lax.ppermute(value, axis, [((k + 1) % n, k) for k in range(n)])  16.1 us
    ppermute x6, waiting for transfers between devices, from_previous(): return lax.ppermute(value, axis, [(k, (k + 1) % n) for k in range(n)])  7.92 us
    ppermute x6, starting transfers between devices, from_previous(): return lax.ppermute(value, axis, [(k, (k + 1) % n) for k in range(n)])  6.34 us
    all_to_all x1, starting transfers between devices, sum_over_devices(): return lax.all_to_all(copies, AXES, 0, 0, tiled=True).reshape(-1, H)  3.89 us
    unnamed x2, other arithmetic  3.12 us
    pallas_call x1, Pallas kernels, finish_call(): pl.pallas_call(finish_kernel, in_specs=[pl.BlockSpec(memory_space=pltpu.V...  2.76 us
  transfers between devices with their start and end apart: 13, of which 3 were waited for; matrix products, arithmetic and copies ran while one was open for 6% of the time, Pallas kernels for 0%

profile of v1, /device:TPU:1, one launch (start us, length us, event | category | flops | bytes accessed | tf_op | source)
XLA Modules:
  0.0 126.5 jit_solution(1989592030168814404)
XLA Ops:
  0.6 0.8 slice_bitcast_fusion.6
  1.4 3.6 %collective-permute-start.1 = (bf16[32,4,128]{2,1,0:T(4,128)(2,1)S(1)}, bf16[32,4,128]{2,1,0:T(4,128)(2,1)S(1)}, u32[]{:S(2)}, u32[]{:S(2)}) collective-permute-start(bf16[32,4,128]{2,1,0:T(4,128)(2,1)S(1)} %get-tuple-element.37), channel_id=1, source_target_pairs={{32,0},{64,32},{96,64},{0,96},{33,1},{65,33},{97,65},{1,97},{34,2}... | collective-permute-start | bytes 98312 | tf_op jit(solution)/shard_map/ppermute | solution.py:497
  5.1 0.8 fusion.1
  5.9 4.8 %collective-permute-start.3 = (bf16[16,2,4,128]{3,2,1,0:T(4,128)(2,1)S(1)}, bf16[16,2,4,128]{3,2,1,0:T(4,128)(2,1)S(1)}, u32[]{:S(2)}, u32[]{:S(2)}) collective-permute-start(bf16[16,2,4,128]{3,2,1,0:T(4,128)(2,1)S(1)} %get-tuple-element.35), channel_id=1, source_target_pairs={{4,0},{8,4},{12,8},{16,12},{20,16},{24,20},{28,24},{0,28},{5,1},{9... | collective-permute-start | bytes 98312 | tf_op jit(solution)/shard_map/ppermute | solution.py:497
  10.6 1.9 %fusion = (bf16[16,32,1,128]{3,2,1,0:T(2,128)(2,1)S(1)}, bf16[16,32,1,128]{3,2,1,0:T(2,128)(2,1)S(1)}) fusion(bf16[16,32,4,128]{3,2,1,0:T(4,128)(2,1)} %param.13), kind=kLoop, calls=%fused_computation.14 | loop fusion | bytes 524288 | tf_op jit(solution)/shard_map/slice | solution.py:536
  12.5 3.6 %collective-permute-start.4 = (bf16[16,32,128]{2,1,0:T(8,128)(2,1)S(1)}, bf16[16,32,128]{2,1,0:T(8,128)(2,1)S(1)}, u32[]{:S(2)}, u32[]{:S(2)}) collective-permute-start(bf16[16,32,128]{2,1,0:T(8,128)(2,1)S(1)} %bitcast.47), channel_id=1, source_target_pairs={{0,1},{1,2},{2,3},{3,0},{4,5},{5,6},{6,7},{7,4},{8,9},{9,10},{10,1... | collective-permute-start | bytes 393224 | tf_op jit(solution)/shard_map/ppermute | solution.py:492
  16.2 0.1 collective-permute-start.5
  16.3 0.5 broadcast.24
  16.8 1.6 %reduce.11 = s32[12288]{0:T(1024)S(1)} reduce(s32[1,1,1,12288]{3,2,1,0:T(1,128)} %param.15, s32[]{:T(128)} %broadcast.24), dimensions={0,1,2}, to_apply=%param.15.reduce_sub_computation.3 | reduce | bytes 98308 | tf_op args[2]
  18.4 1.6 %reduce.10 = s32[12288]{0:T(1024)S(1)} reduce(s32[1,1,1,12288]{3,2,1,0:T(1,128)} %param.16, s32[]{:T(128)} %broadcast.24), dimensions={0,1,2}, to_apply=%param.16.reduce_sub_computation.3 | reduce | bytes 98308 | tf_op args[3]
  19.9 0.7 multiply_add_fusion.code_ref
  20.6 0.8 slice_reduce_fusion
  21.4 4.1 %collective-permute-done.2 = bf16[16,2,4,128]{3,2,1,0:T(4,128)(2,1)S(1)} collective-permute-done((bf16[16,2,4,128]{3,2,1,0:T(4,128)(2,1)S(1)}, bf16[16,2,4,128]{3,2,1,0:T(4,128)(2,1)S(1)}, u32[]{:S(2)}, u32[]{:S(2)}) %collective-permute-start.2) | collective-permute-done | bytes 32800 | tf_op jit(solution)/shard_map/ppermute | solution.py:492
  25.5 0.5 copy-done.15
  26.1 0.1 copy-done.2
  26.2 0.0 copy-done.3
  26.2 54.2 %layer.1 = (bf16[12288,128]{1,0:T(8,128)(2,1)}, f32[2048,128]{1,0:T(8,128)}, bf16[2,128,128]{2,1,0:T(8,128)(2,1)}, bf16[2,128,128]{2,1,0:T(8,128)(2,1)}, bf16[2,...) custom-call(s32[48]{0:T(128)} %get-tuple-element.32.first_ref, s32[48]{0:T(128)} %get-tuple-element.31.last_ref, ...), custom_call_target="tpu_custom_call" | custom-call | tf_op jit(solution)/shard_map/layer/pallas_call | solution.py:397
  80.4 22.2 %all_to_all.10 = f32[128,8,128]{2,1,0:T(8,128)S(1)} all-to-all(f32[128,8,128]{2,1,0:T(8,128)} %bitcast.44), channel_id=1, replica_groups=mesh['gx'=4,'gy'=8,'gz'=4] {'gx','gy','gz'}, dimensions={0} | all-to-all | bytes 1048576 | tf_op jit(solution)/shard_map/all_to_all | solution.py:515
  102.6 0.1 reduce_sum.9
  102.7 0.8 broadcast_in_dim.18
  103.6 3.9 %all-to-all-start.1 = ((f32[128,8,128]{2,1,0:T(8,128)}), f32[128,8,128]{2,1,0:T(8,128)S(1)}, u32[]{:S(2)}, u32[]{:S(2)}) async-start(f32[128,8,128]{2,1,0:T(8,128)} %broadcast_in_dim.18), calls=%async_computation.1 | async-start | bytes 1048576 | tf_op jit(solution)/shard_map/all_to_all | solution.py:517
  107.5 2.8 %collective-permute-start.7 = (bf16[128,128]{1,0:T(8,128)(2,1)S(1)}, bf16[128,128]{1,0:T(8,128)(2,1)S(1)}, u32[]{:S(2)}, u32[]{:S(2)}) collective-permute-start(bf16[128,128]{1,0:T(8,128)(2,1)S(1)} %get-tuple-element.43), channel_id=1, source_target_pairs={{32,0},{64,32},{96,64},{0,96},{33,1},{65,33},{97,65},{1,97},{34,2}... | collective-permute-start | bytes 98312 | tf_op jit(solution)/shard_map/ppermute | solution.py:497
  110.4 0.7 collective-permute-start.11
  111.1 2.7 %collective-permute-start.10 = (bf16[512,128]{1,0:T(8,128)(2,1)S(1)}, bf16[512,128]{1,0:T(8,128)(2,1)S(1)}, u32[]{:S(2)}, u32[]{:S(2)}) collective-permute-start(bf16[512,128]{1,0:T(8,128)(2,1)S(1)} %get-tuple-element.40), channel_id=1, source_target_pairs={{0,1},{1,2},{2,3},{3,0},{4,5},{5,6},{6,7},{7,4},{8,9},{9,10},{10,1... | collective-permute-start | bytes 393224 | tf_op jit(solution)/shard_map/ppermute | solution.py:492
  113.8 4.1 %collective-permute-start.9 = (bf16[128,128]{1,0:T(8,128)(2,1)S(1)}, bf16[128,128]{1,0:T(8,128)(2,1)S(1)}, u32[]{:S(2)}, u32[]{:S(2)}) collective-permute-start(bf16[128,128]{1,0:T(8,128)(2,1)S(1)} %get-tuple-element.41), channel_id=1, source_target_pairs={{4,0},{8,4},{12,8},{16,12},{20,16},{24,20},{28,24},{0,28},{5,1},{9... | collective-permute-start | bytes 98312 | tf_op jit(solution)/shard_map/ppermute | solution.py:497
  117.9 1.1 collective-permute-done.9.yhi_ref
  119.0 3.8 %collective-permute-done.8.ylo_ref = bf16[128,128]{1,0:T(8,128)(2,1)S(1)} collective-permute-done((bf16[128,128]{1,0:T(8,128)(2,1)S(1)}, bf16[128,128]{1,0:T(8,128)(2,1)S(1)}, u32[]{:S(2)}, u32[]{:S(2)}) %collective-permute-start.8) | collective-permute-done | bytes 32800 | tf_op jit(solution)/shard_map/ppermute | solution.py:492
  122.9 0.5 copy-done.14
  123.4 0.1 copy-done.4
  123.5 0.0 copy-done.5
  123.5 0.2 copy-done
  123.7 2.8 %finish.1 = (bf16[2048,128]{1,0:T(8,128)(2,1)}, f32[384,128]{1,0:T(8,128)}, f32[128,128]{1,0:T(8,128)}, f32[256,128]{1,0:T(8,128)}, f32[128,128]{1,0:T(8,128)}, /*index=5*/f32[4,128]{1,0:T(4,128)}) custom-call(f32[2048,128]{1,0:T(8,128)} %get-tuple-element.19.gown_ref, bf16[128,128]{1,0:T(8,128)(2,1)} %copy-done.12, bf16[128,128]{1,0:T(8,128)(2,1)} %copy-done.11, ...), custom_call_target="tpu_custom_call" | custom-call | tf_op jit(solution)/shard_map/finish/pallas_call | solution.py:473
  (46 shorter events, 0.2 us)
Async XLA Ops:
  1.4 19.2 %collective-permute-start.1 = (bf16[32,4,128]{2,1,0:T(4,128)(2,1)S(1)}, bf16[32,4,128]{2,1,0:T(4,128)(2,1)S(1)}, u32[]{:S(2)}, u32[]{:S(2)}) collective-permute-start(bf16[32,4,128]{2,1,0:T(4,128)(2,1)S(1)} %get-tuple-element.37), channel_id=1, source_target_pairs={{32,0},{64,32},{96,64},{0,96},{33,1},{65,33},{97,65},{1,97},{34,2}... | collective-permute-start | bytes 98312 | tf_op jit(solution)/shard_map/ppermute | solution.py:497
  5.1 16.3 %collective-permute-start = (bf16[32,4,128]{2,1,0:T(4,128)(2,1)S(1)}, bf16[32,4,128]{2,1,0:T(4,128)(2,1)S(1)}, u32[]{:S(2)}, u32[]{:S(2)}) collective-permute-start(bf16[32,4,128]{2,1,0:T(4,128)(2,1)S(1)} %get-tuple-element.38), channel_id=1, source_target_pairs={{0,32},{32,64},{64,96},{96,0},{1,33},{33,65},{65,97},{97,1},{2,34}... | collective-permute-start | bytes 98312 | tf_op jit(solution)/shard_map/ppermute | solution.py:492
  5.9 15.5 %collective-permute-start.3 = (bf16[16,2,4,128]{3,2,1,0:T(4,128)(2,1)S(1)}, bf16[16,2,4,128]{3,2,1,0:T(4,128)(2,1)S(1)}, u32[]{:S(2)}, u32[]{:S(2)}) collective-permute-start(bf16[16,2,4,128]{3,2,1,0:T(4,128)(2,1)S(1)} %get-tuple-element.35), channel_id=1, source_target_pairs={{4,0},{8,4},{12,8},{16,12},{20,16},{24,20},{28,24},{0,28},{5,1},{9... | collective-permute-start | bytes 98312 | tf_op jit(solution)/shard_map/ppermute | solution.py:497
  12.5 13.0 %collective-permute-start.4 = (bf16[16,32,128]{2,1,0:T(8,128)(2,1)S(1)}, bf16[16,32,128]{2,1,0:T(8,128)(2,1)S(1)}, u32[]{:S(2)}, u32[]{:S(2)}) collective-permute-start(bf16[16,32,128]{2,1,0:T(8,128)(2,1)S(1)} %bitcast.47), channel_id=1, source_target_pairs={{0,1},{1,2},{2,3},{3,0},{4,5},{5,6},{6,7},{7,4},{8,9},{9,10},{10,1... | collective-permute-start | bytes 393224 | tf_op jit(solution)/shard_map/ppermute | solution.py:492
  16.2 9.3 %collective-permute-start.5 = (bf16[16,32,128]{2,1,0:T(8,128)(2,1)S(1)}, bf16[16,32,128]{2,1,0:T(8,128)(2,1)S(1)}, u32[]{:S(2)}, u32[]{:S(2)}) collective-permute-start(bf16[16,32,128]{2,1,0:T(8,128)(2,1)S(1)} %bitcast.48), channel_id=1, source_target_pairs={{1,0},{2,1},{3,2},{0,3},{5,4},{6,5},{7,6},{4,7},{9,8},{10,9},{11,1... | collective-permute-start | bytes 393224 | tf_op jit(solution)/shard_map/ppermute | solution.py:497
  20.6 4.9 %copy-start.8 = (bf16[32,4,128]{2,1,0:T(4,128)(2,1)}, bf16[32,4,128]{2,1,0:T(4,128)(2,1)S(1)}, u32[]{:S(2)}) copy-start(bf16[32,4,128]{2,1,0:T(4,128)(2,1)S(1)} %collective-permute-done.1) | copy-start | bytes 98308
  20.6 4.9 %collective-permute-start.2 = (bf16[16,2,4,128]{3,2,1,0:T(4,128)(2,1)S(1)}, bf16[16,2,4,128]{3,2,1,0:T(4,128)(2,1)S(1)}, u32[]{:S(2)}, u32[]{:S(2)}) collective-permute-start(bf16[16,2,4,128]{3,2,1,0:T(4,128)(2,1)S(1)} %get-tuple-element.36), channel_id=1, source_target_pairs={{0,4},{4,8},{8,12},{12,16},{16,20},{20,24},{24,28},{28,0},{1,5},{5... | collective-permute-start | bytes 98312 | tf_op jit(solution)/shard_map/ppermute | solution.py:492
  21.4 4.1 %copy-start.9 = (bf16[32,4,128]{2,1,0:T(4,128)(2,1)}, bf16[32,4,128]{2,1,0:T(4,128)(2,1)S(1)}, u32[]{:S(2)}) copy-start(bf16[32,4,128]{2,1,0:T(4,128)(2,1)S(1)} %collective-permute-done) | copy-start | bytes 98308
  21.4 4.1 %copy-start.10 = (bf16[16,2,4,128]{3,2,1,0:T(4,128)(2,1)}, bf16[16,2,4,128]{3,2,1,0:T(4,128)(2,1)S(1)}, u32[]{:S(2)}) copy-start(bf16[16,2,4,128]{3,2,1,0:T(4,128)(2,1)S(1)} %collective-permute-done.3) | copy-start | bytes 98308
  25.5 0.6 copy-start.15
  25.5 0.7 copy-start.2
  25.5 0.7 copy-start.3
  80.4 27.1 %copy-start.7 = (bf16[2,128,128]{2,1,0:T(8,128)(2,1)S(1)}, bf16[2,128,128]{2,1,0:T(8,128)(2,1)}, u32[]{:S(2)}) copy-start(bf16[2,128,128]{2,1,0:T(8,128)(2,1)} %get-tuple-element.20) | copy-start | bytes 196612
  80.4 30.0 %copy-start.1 = (bf16[2,512,128]{2,1,0:T(8,128)(2,1)S(1)}, bf16[2,512,128]{2,1,0:T(8,128)(2,1)}, u32[]{:S(2)}) copy-start(bf16[2,512,128]{2,1,0:T(8,128)(2,1)} %get-tuple-element.22) | copy-start | bytes 786436
  80.4 33.4 %copy-start.6 = (bf16[2,128,128]{2,1,0:T(8,128)(2,1)S(1)}, bf16[2,128,128]{2,1,0:T(8,128)(2,1)}, u32[]{:S(2)}) copy-start(bf16[2,128,128]{2,1,0:T(8,128)(2,1)} %get-tuple-element.21) | copy-start | bytes 196612
  103.6 19.3 %all-to-all-start.1 = ((f32[128,8,128]{2,1,0:T(8,128)}), f32[128,8,128]{2,1,0:T(8,128)S(1)}, u32[]{:S(2)}, u32[]{:S(2)}) async-start(f32[128,8,128]{2,1,0:T(8,128)} %broadcast_in_dim.18), calls=%async_computation.1 | async-start | bytes 1048576 | tf_op jit(solution)/shard_map/all_to_all | solution.py:517
  107.5 10.4 %collective-permute-start.7 = (bf16[128,128]{1,0:T(8,128)(2,1)S(1)}, bf16[128,128]{1,0:T(8,128)(2,1)S(1)}, u32[]{:S(2)}, u32[]{:S(2)}) collective-permute-start(bf16[128,128]{1,0:T(8,128)(2,1)S(1)} %get-tuple-element.43), channel_id=1, source_target_pairs={{32,0},{64,32},{96,64},{0,96},{33,1},{65,33},{97,65},{1,97},{34,2}... | collective-permute-start | bytes 98312 | tf_op jit(solution)/shard_map/ppermute | solution.py:497
  110.3 7.6 %collective-permute-start.6 = (bf16[128,128]{1,0:T(8,128)(2,1)S(1)}, bf16[128,128]{1,0:T(8,128)(2,1)S(1)}, u32[]{:S(2)}, u32[]{:S(2)}) collective-permute-start(bf16[128,128]{1,0:T(8,128)(2,1)S(1)} %get-tuple-element.44), channel_id=1, source_target_pairs={{0,32},{32,64},{64,96},{96,0},{1,33},{33,65},{65,97},{97,1},{2,34}... | collective-permute-start | bytes 98312 | tf_op jit(solution)/shard_map/ppermute | solution.py:492
  110.4 12.5 %collective-permute-start.11 = (bf16[512,128]{1,0:T(8,128)(2,1)S(1)}, bf16[512,128]{1,0:T(8,128)(2,1)S(1)}, u32[]{:S(2)}, u32[]{:S(2)}) collective-permute-start(bf16[512,128]{1,0:T(8,128)(2,1)S(1)} %get-tuple-element.39), channel_id=1, source_target_pairs={{1,0},{2,1},{3,2},{0,3},{5,4},{6,5},{7,6},{4,7},{9,8},{10,9},{11,1... | collective-permute-start | bytes 393224 | tf_op jit(solution)/shard_map/ppermute | solution.py:497
  111.1 11.7 %collective-permute-start.10 = (bf16[512,128]{1,0:T(8,128)(2,1)S(1)}, bf16[512,128]{1,0:T(8,128)(2,1)S(1)}, u32[]{:S(2)}, u32[]{:S(2)}) collective-permute-start(bf16[512,128]{1,0:T(8,128)(2,1)S(1)} %get-tuple-element.40), channel_id=1, source_target_pairs={{0,1},{1,2},{2,3},{3,0},{4,5},{5,6},{6,7},{7,4},{8,9},{9,10},{10,1... | collective-permute-start | bytes 393224 | tf_op jit(solution)/shard_map/ppermute | solution.py:492
  113.8 5.2 %collective-permute-start.9 = (bf16[128,128]{1,0:T(8,128)(2,1)S(1)}, bf16[128,128]{1,0:T(8,128)(2,1)S(1)}, u32[]{:S(2)}, u32[]{:S(2)}) collective-permute-start(bf16[128,128]{1,0:T(8,128)(2,1)S(1)} %get-tuple-element.41), channel_id=1, source_target_pairs={{4,0},{8,4},{12,8},{16,12},{20,16},{24,20},{28,24},{0,28},{5,1},{9... | collective-permute-start | bytes 98312 | tf_op jit(solution)/shard_map/ppermute | solution.py:497
  117.9 5.0 %copy-start.11 = (bf16[128,128]{1,0:T(8,128)(2,1)}, bf16[128,128]{1,0:T(8,128)(2,1)S(1)}, u32[]{:S(2)}) copy-start(bf16[128,128]{1,0:T(8,128)(2,1)S(1)} %collective-permute-done.7.xhi_ref) | copy-start | bytes 98308
  117.9 4.9 %collective-permute-start.8 = (bf16[128,128]{1,0:T(8,128)(2,1)S(1)}, bf16[128,128]{1,0:T(8,128)(2,1)S(1)}, u32[]{:S(2)}, u32[]{:S(2)}) collective-permute-start(bf16[128,128]{1,0:T(8,128)(2,1)S(1)} %get-tuple-element.42), channel_id=1, source_target_pairs={{0,4},{4,8},{8,12},{12,16},{16,20},{20,24},{24,28},{28,0},{1,5},{5... | collective-permute-start | bytes 98312 | tf_op jit(solution)/shard_map/ppermute | solution.py:492
  117.9 5.0 %copy-start.12 = (bf16[128,128]{1,0:T(8,128)(2,1)}, bf16[128,128]{1,0:T(8,128)(2,1)S(1)}, u32[]{:S(2)}) copy-start(bf16[128,128]{1,0:T(8,128)(2,1)S(1)} %collective-permute-done.6.xlo_ref) | copy-start | bytes 98308
  119.0 3.9 %copy-start.13 = (bf16[128,128]{1,0:T(8,128)(2,1)}, bf16[128,128]{1,0:T(8,128)(2,1)S(1)}, u32[]{:S(2)}) copy-start(bf16[128,128]{1,0:T(8,128)(2,1)S(1)} %collective-permute-done.9.yhi_ref) | copy-start | bytes 98308
  122.8 0.6 copy-start.14
  122.8 0.7 copy-start.4
  122.8 0.7 copy-start.5
  122.8 0.9 copy-start

commit v2 on v1

--- a/solution.py
+++ b/solution.py
@@ -13,8 +13,13 @@
 TILE = 256
 TILES = EDGES // TILE
 WIN = 64
+MID = 128
 GROUP = 2
+HALF = TILE // H
+CHUNKS = 4
 ROWS = CELLS + 128
+STRIDE = 208
+GRID = N_PLANE * STRIDE + 128
 PAD_ROWS = CELLS + 3 * PLANE
 PARAM_ROWS = 1024
 AXES = ("gx", "gy", "gz")
@@ -47,9 +52,9 @@
 
 
 def layer_kernel(
-    first_ref,
-    last_ref,
-    code_ref,
+    near_ref,
+    send_ref,
+    recv_ref,
     node_ref,
     cotn_ref,
     xlo_ref,
@@ -58,8 +63,8 @@
     yhi_ref,
     zlo_ref,
     zhi_ref,
-    e_ref,
-    cot_ref,
+    e_hbm,
+    cot_hbm,
     w1e_ref,
     b1e_ref,
     w2e_ref,
@@ -67,17 +72,23 @@
     w1n_ref,
     b1n_ref,
     w2n_ref,
-    gedge_ref,
+    gedge_hbm,
     gown_ref,
     fx_ref,
     fy_ref,
     fz_ref,
     par_ref,
+    e_ref,
+    cot_ref,
+    gedge_ref,
+    dz_ref,
     own_ref,
     zx_ref,
     yx_ref,
     ppad_ref,
-    tab_ref,
+    home_ref,
+    mid_ref,
+    code_ref,
     col_ref,
     u_ref,
     slope_ref,
@@ -85,13 +96,26 @@
     deg_ref,
     dd_ref,
     spad_ref,
-    acc_ref,
+    rsum_ref,
+    smid_ref,
     wide_ref,
     zacc_ref,
     const_ref,
     flip_ref,
     sr_ref,
+    in_sem,
+    out_sem,
 ):
+    copy_e = pltpu.make_async_copy(e_hbm, e_ref, in_sem.at[0])
+    copy_cot = pltpu.make_async_copy(cot_hbm, cot_ref, in_sem.at[1])
+    copy_e.start()
+    copy_cot.start()
+
+    def copy_out(c):
+        size = EDGES // CHUNKS
+        at = pl.ds(pl.multiple_of(c * size, size), size)
+        return pltpu.make_async_copy(gedge_ref.at[at, :], gedge_hbm.at[at, :], out_sem.at[c])
+
     w1a = w1e_ref[0:H]
     w1b = w1e_ref[H : 2 * H]
     w1c = w1e_ref[2 * H : 3 * H]
@@ -99,9 +123,12 @@
     eu_ref[...] = jnp.zeros(eu_ref.shape, F32)
     deg_ref[...] = jnp.zeros(deg_ref.shape, F32)
     spad_ref[...] = jnp.zeros(spad_ref.shape, F32)
-    acc_ref[...] = jnp.zeros(acc_ref.shape, F32)
+    rsum_ref[...] = jnp.zeros(rsum_ref.shape, F32)
+    smid_ref[...] = jnp.zeros(smid_ref.shape, F32)
+    mid_ref[...] = jnp.zeros(mid_ref.shape, F32)
+    wide_ref[...] = jnp.zeros(wide_ref.shape, F32)
     dd_ref[CELLS:ROWS] = jnp.zeros((ROWS - CELLS, 2 * H), BF16)
-    tab_ref[:, CELLS:ROWS] = jnp.zeros((5, ROWS - CELLS, H), BF16)
+    home_ref[CELLS:ROWS] = jnp.zeros((ROWS - CELLS, H), BF16)
     ppad_ref[CELLS + 2 * PLANE :] = jnp.zeros((PAD_ROWS - CELLS - 2 * PLANE, H), BF16)
     const_ref[:, 0:H] = flip(w2e_ref[...])
     const_ref[:, H:] = hot(iota((H, H), 0) == iota((H, H), 1))
@@ -109,79 +136,81 @@
     flip_ref[H : 2 * H] = flip(w1c)
     flip_ref[2 * H : 3 * H] = flip(w1a)
 
+    r = recv_ref[...]
+    s = send_ref[...]
+    delta = s - (((r >> 7) + 1) * 204 + (((r >> 2) & 31) + 1) * 6 + (r & 3) + 1)
+    inside = s - 204 + 4 * (r >> 7)
+    place = jnp.where(delta == 204, r + 4096, jnp.where(delta == -204, r + 8192, inside))
+    code_ref[...] = place * 2048 + r
+
     ppad_ref[0:PLANE] = dot(xlo_ref[...], w1b).astype(BF16)
     ppad_ref[CELLS + PLANE : CELLS + 2 * PLANE] = dot(xhi_ref[...], w1b).astype(BF16)
     yx_ref[0:PLANE] = dot(ylo_ref[...], w1b)
     yx_ref[PLANE : 2 * PLANE] = dot(yhi_ref[...], w1b)
-    zx_ref[pl.ds(0, CELLS // 4, 4), :] = dot(zlo_ref[...], w1b)
-    zx_ref[pl.ds(3, CELLS // 4, 4), :] = dot(zhi_ref[...], w1b)
-    w1bc = jnp.concatenate([w1b, w1c], axis=1)
-    row = iota((PLANE, H), 0)
-    at_low = (row & 3) == 0
-    at_high = (row & 3) == 3
-
-    def prepare(i, carry):
-        base = pl.multiple_of(i * PLANE, PLANE)
-        both = dot(node_ref[pl.ds(base, PLANE), :], w1bc)
-        p = both[:, 0:H]
-        tab_ref[4, pl.ds(base, PLANE), :] = (both[:, H:] + b1e_ref[...]).astype(BF16)
-        ppad_ref[pl.ds(base + PLANE, PLANE), :] = p.astype(BF16)
-        ylow = yx_ref[pl.ds(pl.multiple_of(i * 8, 8), 8), :]
-        yhigh = yx_ref[pl.ds(pl.multiple_of(PLANE + i * 8, 8), 8), :]
-        pad = jnp.zeros((PLANE - 8, H), F32)
-        low_full = jnp.concatenate([ylow, pad], axis=0)
-        high_full = jnp.concatenate([pad, yhigh], axis=0)
-        up = jnp.where(row < PLANE - 4, pltpu.roll(p, PLANE - 4, 0), pltpu.roll(high_full, 4, 0))
-        down = jnp.where(row >= 4, pltpu.roll(p, 4, 0), pltpu.roll(low_full, PLANE - 4, 0))
-        tab_ref[0, pl.ds(base, PLANE), :] = up.astype(BF16)
-        tab_ref[1, pl.ds(base, PLANE), :] = down.astype(BF16)
-        zx = zx_ref[pl.ds(base, PLANE), :]
-        tab_ref[2, pl.ds(base, PLANE), :] = jnp.where(
-            at_high, zx, pltpu.roll(p, PLANE - 1, 0)
-        ).astype(BF16)
-        tab_ref[3, pl.ds(base, PLANE), :] = jnp.where(at_low, zx, pltpu.roll(p, 1, 0)).astype(BF16)
-        return carry
-
-    lax.fori_loop(0, N_PLANE, prepare, 0)
+    zx_ref[0] = dot(zlo_ref[...], w1b)
+    zx_ref[1] = dot(zhi_ref[...], w1b)
+    own_ref[...] = dot(node_ref[...], w1b)
+    for i in range(N_PLANE):
+        at = slice(i * PLANE, (i + 1) * PLANE)
+        base = i * STRIDE
+        ppad_ref[(i + 1) * PLANE : (i + 2) * PLANE] = own_ref[at].astype(BF16)
+        home_ref[at] = (dot(node_ref[at], w1c) + b1e_ref[...]).astype(BF16)
+        for l in range(4):
+            mid_ref[pl.ds(base + 7 + l, 32, 6), :] = own_ref[pl.ds(i * PLANE + l, 32, 4), :]
+        mid_ref[pl.ds(base + 6, 32, 6), :] = zx_ref[0, i * 32 : (i + 1) * 32, :]
+        mid_ref[pl.ds(base + 11, 32, 6), :] = zx_ref[1, i * 32 : (i + 1) * 32, :]
+        mid_ref[base + 1 : base + 5, :] = yx_ref[i * 8 + 4 : i * 8 + 8, :]
+        mid_ref[base + 199 : base + 203, :] = yx_ref[PLANE + i * 8 : PLANE + i * 8 + 4, :]
+    copy_e.wait()
 
     lane = iota((TILE, H), 1)
-    lane_code = (lane >> 6) * 4096 + (lane & 63)
+    lane_x = jnp.where(lane < WIN, 4096 + lane, 8192 - WIN + lane)
     lane_self = jnp.where(lane < WIN, lane, -(1 << 20))
-    srow = iota((H, TILE), 0)
-    srow_code = (srow >> 6) * 4096 + (srow & 63)
-    wrow = iota((WIN, TILE), 0)
+    mrow = iota((MID, H), 0)
+    wrow = iota((WIN, H), 0)
+    far = 1 << 14
 
     def start_of(t):
-        return pl.multiple_of((first_ref[t] >> 4) << 4, 16)
+        return pl.multiple_of((near_ref[HALF * t, 0] >> 4) << 4, 16)
 
     def windows_of(t):
-        return ((last_ref[t] - start_of(t)) >> 6) + 1
+        return ((near_ref[HALF * t + HALF - 1, H - 1] - start_of(t)) >> 6) + 1
+
+    def mid_of(w):
+        return pl.multiple_of((w >> 7) * STRIDE + ((w & 127) >> 4) * 24, 8)
 
     def rows_of(t):
         return pl.ds(pl.multiple_of(t * TILE, TILE), TILE)
 
+    def lines(t):
+        return [code_ref[pl.ds(HALF * t + k, 1), :] for k in range(HALF)]
+
     def columns(t):
-        line = code_ref[pl.ds(t, 1), :].astype(F32)
-        parts = [
-            jnp.broadcast_to(line[:, k * H : (k + 1) * H], (H, H)).T for k in range(TILE // H)
+        parts = [jnp.broadcast_to(line, (H, H)).T for line in lines(t)]
+        return jnp.concatenate(parts, axis=0)
+
+    def split(code, w, guard):
+        place = code >> 11
+        home = (code & 2047) - w
+        if guard:
+            place = jnp.where(jnp.logical_and(home >= 0, home < WIN), place, far)
+        return place, home
+
+    def gather_pre(col, w, rest, weights, guard):
+        place, home = split(col, w, guard)
+        mid = mid_of(w)
+        left = [
+            hot(place - mid == lane),
+            hot(place - w == lane_x),
+            hot(home == lane_self),
         ]
-        return jnp.concatenate(parts, axis=0).astype(jnp.int32)
-
-    def gather_pre(col, w):
-        shifted = col - w
-        inner = (col & 4095) - w
-        parts = [hot(shifted == lane_code + k * 8192) for k in range(3)]
-        left = jnp.concatenate(parts + [hot(inner == lane_self)], axis=1)
-        right = jnp.concatenate(
-            [
-                ppad_ref[pl.ds(w + 2 * PLANE, WIN), :],
-                ppad_ref[pl.ds(w, WIN), :],
-            ]
-            + [tab_ref[k, pl.ds(w, WIN), :] for k in range(5)]
-            + [jnp.zeros((WIN, H), BF16)],
-            axis=0,
-        )
-        return dot(left, right)
+        right = [
+            mid_ref[pl.ds(mid, MID), :].astype(BF16),
+            ppad_ref[pl.ds(w + 2 * PLANE, WIN), :],
+            ppad_ref[pl.ds(w, WIN), :],
+            home_ref[pl.ds(w, MID), :],
+        ]
+        return dot(jnp.concatenate(left + rest, axis=1), jnp.concatenate(right + weights, axis=0))
 
     def activate(t, z):
         s = sigmoid(z)
@@ -192,8 +221,9 @@
         return ub
 
     def collect(t, w, eu):
-        picked = ((code_ref[pl.ds(t, 1), :] & 4095) - w) == wrow
-        ones = jnp.where(picked, 1.0, 0.0)
+        ones = jnp.concatenate(
+            [jnp.where((line & 2047) - w == wrow, 1.0, 0.0) for line in lines(t)], axis=1
+        )
         eu_ref[pl.ds(w, WIN), :] += dot(ones.astype(BF16), eu)
         deg_ref[pl.ds(w, WIN), :] += jnp.broadcast_to(
             jnp.sum(ones, axis=1, keepdims=True), (WIN, H)
@@ -204,7 +234,7 @@
         col_ref[rows_of(t), :] = col
         e = e_ref[rows_of(t), :]
         w = start_of(t)
-        ub = activate(t, gather_pre(col, w) + dot(e, w1a))
+        ub = activate(t, gather_pre(col, w, [e], [w1a], False))
         collect(t, w, jnp.concatenate([e, ub], axis=1))
 
     def forward_slow(t):
@@ -213,7 +243,7 @@
 
         def more(k, carry):
             w = pl.multiple_of(start_of(t) + k * WIN, 16)
-            zacc_ref[:, 0:H] += gather_pre(col_ref[rows_of(t), :], w)
+            zacc_ref[:, 0:H] += gather_pre(col_ref[rows_of(t), :], w, [], [], True)
             return carry
 
         lax.fori_loop(0, windows_of(t), more, 0)
@@ -226,7 +256,7 @@
 
         lax.fori_loop(0, windows_of(t), put, 0)
 
-    def each_group(fast, slow):
+    def each_group(fast, slow, after=None):
         def body(g, carry):
             tiles = [g * GROUP + k for k in range(GROUP)]
             fits = windows_of(tiles[0]) <= 1
@@ -243,6 +273,8 @@
                 for t in tiles:
                     slow(t)
 
+            if after is not None:
+                after(g)
             return carry
 
         lax.fori_loop(0, TILES // GROUP, body, 0)
@@ -280,27 +312,40 @@
         par_ref[7 * H + 3 : 7 * H + 4, :] += jnp.sum(cot32, axis=0, keepdims=True)
         return carry
 
-    lax.fori_loop(0, CELLS // TILE, cells, 0)
+    lax.fori_loop(0, CELLS // TILE, cells, 0, unroll=2)
+    copy_cot.wait()
 
     def spread(col, w, cot):
-        left = jnp.concatenate([hot((col & 4095) - w == lane), cot], axis=1)
+        left = jnp.concatenate([hot((col & 2047) - w == lane), cot], axis=1)
         right = jnp.concatenate([dd_ref[pl.ds(w, H), :], const_ref[...]], axis=0)
         return dot(left, right)
 
-    def scatter(t, w, dz):
-        shifted = code_ref[pl.ds(t, 1), :] - w
-        inner = (code_ref[pl.ds(t, 1), :] & 4095) - w
-        parts = [hot(shifted == srow_code + k * 8192) for k in range(3)]
-        sums = dot(jnp.concatenate(parts + [hot(inner == wrow)], axis=0), dz)
-        spad_ref[pl.ds(w + 2 * PLANE, WIN), :] += sums[0:WIN]
-        spad_ref[pl.ds(w, WIN), :] += sums[WIN : 2 * WIN]
-        for k in range(5):
-            acc_ref[k, pl.ds(w, WIN), :] += sums[(k + 2) * WIN : (k + 3) * WIN]
+    def scatter(t, w, dz, guard):
+        mid = mid_of(w)
+        parts = []
+        for line in lines(t):
+            place, home = split(line, w, guard)
+            across = place - w
+            parts.append(
+                jnp.concatenate(
+                    [
+                        hot(place - mid == mrow),
+                        hot(across - 4096 == wrow),
+                        hot(across - 8192 == wrow),
+                        hot(home == wrow),
+                    ],
+                    axis=0,
+                )
+            )
+        sums = dot(jnp.concatenate(parts, axis=1), dz)
+        smid_ref[pl.ds(mid, MID), :] += sums[0:MID]
+        spad_ref[pl.ds(w + 2 * PLANE, WIN), :] += sums[MID : MID + WIN]
+        spad_ref[pl.ds(w, WIN), :] += sums[MID + WIN : MID + 2 * WIN]
+        rsum_ref[pl.ds(w, WIN), :] += sums[MID + 2 * WIN :]
 
     def finish_edges(t, dd):
         d32 = dd[:, H:]
         d = d32.astype(BF16)
-        d32 = d.astype(F32)
         dz = (dd[:, 0:H] * slope_ref[rows_of(t), :].astype(F32)).astype(BF16)
         gedge_ref[rows_of(t), :] = (d32 + dot(dz, flip_ref[2 * H : 3 * H])).astype(BF16)
         wide_ref[0:H, :] += dot_first(e_ref[rows_of(t), :], dz)
@@ -311,7 +356,7 @@
     def backward_fast(t):
         w = start_of(t)
         dz = finish_edges(t, spread(col_ref[rows_of(t), :], w, cot_ref[rows_of(t), :]))
-        scatter(t, w, dz)
+        scatter(t, w, dz, False)
 
     def backward_slow(t):
         zacc_ref[...] = dot(cot_ref[rows_of(t), :], const_ref[...])
@@ -324,55 +369,58 @@
             return carry
 
         lax.fori_loop(0, (windows_of(t) + 1) >> 1, more, 0)
-        own_ref[...] = finish_edges(t, zacc_ref[...])
+        dz_ref[...] = finish_edges(t, zacc_ref[...])
 
         def put(k, carry):
-            scatter(t, pl.multiple_of(start_of(t) + k * WIN, 16), own_ref[...])
+            scatter(t, pl.multiple_of(start_of(t) + k * WIN, 16), dz_ref[...], True)
             return carry
 
         lax.fori_loop(0, windows_of(t), put, 0)
 
-    wide_ref[...] = jnp.zeros(wide_ref.shape, F32)
-    each_group(backward_fast, backward_slow)
-
-    row8 = iota((8, H), 0)
+    per_chunk = TILES // GROUP // CHUNKS
+
+    def send_out(g):
+        @pl.when(g % per_chunk == per_chunk - 1)
+        def _():
+            copy_out(g // per_chunk).start()
+
+    each_group(backward_fast, backward_slow, send_out)
+
+    for i in range(N_PLANE):
+        at = slice(i * PLANE, (i + 1) * PLANE)
+        base = i * STRIDE
+        for l in range(4):
+            own_ref[pl.ds(i * PLANE + l, 32, 4), :] = smid_ref[pl.ds(base + 7 + l, 32, 6), :]
+        zx_ref[0, i * 32 : (i + 1) * 32, :] = smid_ref[pl.ds(base + 6, 32, 6), :]
+        zx_ref[1, i * 32 : (i + 1) * 32, :] = smid_ref[pl.ds(base + 11, 32, 6), :]
+        nothing = jnp.zeros((4, H), F32)
+        yx_ref[i * 8 : i * 8 + 8, :] = jnp.concatenate(
+            [nothing, smid_ref[base + 1 : base + 5, :]], axis=0
+        )
+        yx_ref[PLANE + i * 8 : PLANE + i * 8 + 8, :] = jnp.concatenate(
+            [smid_ref[base + 199 : base + 203, :], nothing], axis=0
+        )
 
     def gather_cells(i, carry):
-        base = pl.multiple_of(i * PLANE, PLANE)
-        at = pl.ds(base, PLANE)
-        yp = acc_ref[0, at, :]
-        ym = acc_ref[1, at, :]
-        zp = acc_ref[2, at, :]
-        zm = acc_ref[3, at, :]
-        zero = jnp.zeros((PLANE, H), F32)
-        total = spad_ref[pl.ds(base + PLANE, PLANE), :]
-        total += jnp.where(row >= 4, pltpu.roll(yp, 4, 0), zero)
-        total += jnp.where(row < PLANE - 4, pltpu.roll(ym, PLANE - 4, 0), zero)
-        total += jnp.where(at_low, zero, pltpu.roll(zp, 1, 0))
-        total += jnp.where(at_high, zero, pltpu.roll(zm, PLANE - 1, 0))
-        sr = jnp.concatenate([total, acc_ref[4, at, :]], axis=1)
-        par_ref[7 * H : 7 * H + 1, :] += jnp.sum(acc_ref[4, at, :], axis=0, keepdims=True)
-        sr16 = sr.astype(BF16)
+        base = pl.multiple_of(i * TILE, TILE)
+        at = pl.ds(base, TILE)
+        total = spad_ref[pl.ds(base + PLANE, TILE), :] + own_ref[at, :]
+        sums = rsum_ref[at, :]
+        par_ref[7 * H : 7 * H + 1, :] += jnp.sum(sums, axis=0, keepdims=True)
+        sr16 = jnp.concatenate([total, sums], axis=1).astype(BF16)
         sr_ref[at, :] = sr16
         gown_ref[at, :] += dot(sr16, flip_ref[0 : 2 * H])
-        eight = pl.multiple_of(i * 8, 8)
-        yx_ref[pl.ds(eight, 8), :] = jnp.where(row8 >= 4, pltpu.roll(ym[0:8], 4, 0), 0.0)
-        yx_ref[pl.ds(PLANE + eight, 8), :] = jnp.where(
-            row8 < 4, pltpu.roll(yp[PLANE - 8 :], 4, 0), 0.0
-        )
         return carry
 
-    lax.fori_loop(0, N_PLANE, gather_cells, 0)
+    lax.fori_loop(0, CELLS // TILE, gather_cells, 0, unroll=2)
     both = dot_first(node_ref[...], sr_ref[...])
     w1b_flip = flip_ref[0:H]
     sx_lo = spad_ref[0:PLANE].astype(BF16)
     sx_hi = spad_ref[CELLS + PLANE : CELLS + 2 * PLANE].astype(BF16)
     sy_lo = yx_ref[0:PLANE].astype(BF16)
     sy_hi = yx_ref[PLANE : 2 * PLANE].astype(BF16)
-    zx_ref[...] = acc_ref[3, 0:CELLS, :]
-    sz_lo = zx_ref[pl.ds(0, CELLS // 4, 4), :].astype(BF16)
-    zx_ref[...] = acc_ref[2, 0:CELLS, :]
-    sz_hi = zx_ref[pl.ds(3, CELLS // 4, 4), :].astype(BF16)
+    sz_lo = zx_ref[0].astype(BF16)
+    sz_hi = zx_ref[1].astype(BF16)
     fx_ref[0] = dot(sx_lo, w1b_flip).astype(BF16)
     fx_ref[1] = dot(sx_hi, w1b_flip).astype(BF16)
     fy_ref[0] = dot(sy_lo, w1b_flip).astype(BF16)
@@ -389,15 +437,20 @@
     par_ref[7 * H + 1 : 7 * H + 2, :] = jnp.sum(
         wide_ref[2 * H : 2 * H + 8, :], axis=0, keepdims=True
     )
-
-
-def layer_call(first, last, code, *arrays):
+    for c in range(CHUNKS):
+        copy_out(c).wait()
+
+
+def layer_call(senders, receivers, *arrays):
     smem = pl.BlockSpec(memory_space=pltpu.SMEM)
     vmem = pl.BlockSpec(memory_space=pltpu.VMEM)
+    hbm = pl.BlockSpec(memory_space=pl.ANY)
+    senders = senders.reshape(EDGES // H, H)
+    receivers = receivers.reshape(EDGES // H, H)
     return pl.pallas_call(
         layer_kernel,
-        in_specs=[smem, smem] + [vmem] * 18,
-        out_specs=[vmem] * 6,
+        in_specs=[smem] + [vmem] * 10 + [hbm] * 2 + [vmem] * 7,
+        out_specs=[hbm] + [vmem] * 5,
         out_shape=[
             jax.ShapeDtypeStruct((EDGES, H), BF16),
             jax.ShapeDtypeStruct((CELLS, H), F32),
@@ -407,11 +460,17 @@
             jax.ShapeDtypeStruct((PARAM_ROWS, H), F32),
         ],
         scratch_shapes=[
+            pltpu.VMEM((EDGES, H), BF16),
+            pltpu.VMEM((EDGES, H), BF16),
+            pltpu.VMEM((EDGES, H), BF16),
             pltpu.VMEM((TILE, H), BF16),
             pltpu.VMEM((CELLS, H), F32),
+            pltpu.VMEM((2, CELLS // 4, H), F32),
             pltpu.VMEM((2 * PLANE, H), F32),
             pltpu.VMEM((PAD_ROWS, H), BF16),
-            pltpu.VMEM((5, ROWS, H), BF16),
+            pltpu.VMEM((ROWS, H), BF16),
+            pltpu.VMEM((GRID, H), F32),
+            pltpu.VMEM((EDGES // H, H), jnp.int32),
             pltpu.VMEM((EDGES, H), jnp.int32),
             pltpu.VMEM((EDGES, H), BF16),
             pltpu.VMEM((EDGES, H), BF16),
@@ -419,16 +478,19 @@
             pltpu.VMEM((ROWS, H), F32),
             pltpu.VMEM((ROWS, 2 * H), BF16),
             pltpu.VMEM((PAD_ROWS, H), F32),
-            pltpu.VMEM((5, ROWS, H), F32),
+            pltpu.VMEM((ROWS, H), F32),
+            pltpu.VMEM((GRID, H), F32),
             pltpu.VMEM((2 * H + 8, H), F32),
             pltpu.VMEM((TILE, 2 * H), F32),
             pltpu.VMEM((H, 2 * H), BF16),
             pltpu.VMEM((3 * H, H), BF16),
             pltpu.VMEM((CELLS, 2 * H), BF16),
+            pltpu.SemaphoreType.DMA((2,)),
+            pltpu.SemaphoreType.DMA((CHUNKS,)),
         ],
         compiler_params=pltpu.CompilerParams(vmem_limit_bytes=60 * 1024 * 1024),
         name="layer",
-    )(first, last, code, *arrays)
+    )(receivers, senders, receivers, *arrays)
 
 
 def finish_kernel(
@@ -497,16 +559,6 @@
     return lax.ppermute(value, axis, [((k + 1) % n, k) for k in range(n)])
 
 
-def edge_codes(senders, receivers):
-    r = receivers.reshape(TILES, TILE)
-    s = senders.reshape(TILES, TILE)
-    home = ((r >> 7) + 1) * 204 + (((r >> 2) & 31) + 1) * 6 + (r & 3) + 1
-    delta = s - home
-    size = jnp.abs(delta)
-    side = jnp.where(size == 204, 0, jnp.where(size == 6, 2, 4)) + (delta < 0).astype(jnp.int32)
-    return r[:, 0], r[:, -1], side * 4096 + r
-
-
 def sum_over_devices(rows):
     count = 1
     for axis in AXES:
@@ -538,11 +590,9 @@
     yhi = from_next(node_latent[:, 0:2], "gy").reshape(-1, H)
     xlo = from_previous(node_latent[15], "gx").reshape(-1, H)
     xhi = from_next(node_latent[0], "gx").reshape(-1, H)
-    first, last, code = edge_codes(senders, receivers)
     gedge, gown, fx, fy, fz, par = layer_call(
-        first,
-        last,
-        code,
+        senders,
+        receivers,
         node_latent.reshape(CELLS, H),
         cot_node.reshape(CELLS, H),
         xlo,

time: 127 us -> 113 us (0.89)
  Pallas kernels: 56.9 us -> 46.9 us
  other arithmetic: 3.92 us -> 0.14 us
  blocking collectives: 22.2 us -> 24.2 us
  local copies, waits for them, and re-layouts: 7.23 us -> 5.89 us
    pallas_call x1, Pallas kernels: 54.2 us -> 44.2 us  [layer_call(): pl.pallas_call(layer_kernel, in_specs=[smem] + [vmem] * 10 + [hbm] * 2 +...]
    unnamed x2 -> x0, other arithmetic: 3.12 us -> none
    all_to_all x1, blocking collectives: 22.2 us -> 24.2 us  [sum_over_devices(): mine = jnp.sum(lax.all_to_all(chunks, AXES, 0, 0, tiled=True), axis=0)]
  transfers between devices with their start and end apart: 13 -> 13, of which waited for: 3 -> 4; matrix products, arithmetic and copies ran while one was open for 6% -> 2% of each run, Pallas kernels for 0% -> 0%
where the time goes in v2:
time: 113 us
  Pallas kernels  46.9 us (42%)
  starting transfers between devices  25.4 us (22%)
  blocking collectives  24.2 us (21%)
  waiting for transfers between devices  9.78 us (9%)
  local copies, waits for them, and re-layouts  5.89 us (5%)
    pallas_call x1, Pallas kernels, layer_call(): pl.pallas_call(layer_kernel, in_specs=[smem] + [vmem] * 10 + [hbm] * 2 +...  44.2 us
    all_to_all x1, blocking collectives, sum_over_devices(): mine = jnp.sum(lax.all_to_all(chunks, AXES, 0, 0, tiled=True), axis=0)  24.2 us
    ppermute x6, starting transfers between devices, from_next(): return lax.ppermute(value, axis, [((k + 1) % n, k) for k in range(n)])  15.2 us
    ppermute x6, waiting for transfers between devices, from_previous(): return lax.ppermute(value, axis, [(k, (k + 1) % n) for k in range(n)])  7.69 us
    ppermute x6, starting transfers between devices, from_previous(): return lax.ppermute(value, axis, [(k, (k + 1) % n) for k in range(n)])  6.35 us
    all_to_all x1, starting transfers between devices, sum_over_devices(): return lax.all_to_all(copies, AXES, 0, 0, tiled=True).reshape(-1, H)  3.89 us
    pallas_call x1, Pallas kernels, finish_call(): pl.pallas_call(finish_kernel, in_specs=[pl.BlockSpec(memory_space=pltpu.V...  2.76 us
  transfers between devices with their start and end apart: 13, of which 4 were waited for; matrix products, arithmetic and copies ran while one was open for 2% of the time, Pallas kernels for 0%

profile of v2, /device:TPU:1, one launch (start us, length us, event | category | flops | bytes accessed | tf_op | source)
XLA Modules:
  0.0 113.3 jit_solution(11000074220478929058)
XLA Ops:
  0.6 0.8 slice_bitcast_fusion.6
  1.4 3.6 %collective-permute-start.1 = (bf16[32,4,128]{2,1,0:T(4,128)(2,1)S(1)}, bf16[32,4,128]{2,1,0:T(4,128)(2,1)S(1)}, u32[]{:S(2)}, u32[]{:S(2)}) collective-permute-start(bf16[32,4,128]{2,1,0:T(4,128)(2,1)S(1)} %get-tuple-element.35), channel_id=1, source_target_pairs={{32,0},{64,32},{96,64},{0,96},{33,1},{65,33},{97,65},{1,97},{34,2}... | collective-permute-start | bytes 98312 | tf_op jit(solution)/shard_map/ppermute | solution.py:559
  5.1 0.0 collective-permute-start
  5.1 1.9 %fusion = (bf16[16,32,1,128]{3,2,1,0:T(2,128)(2,1)S(1)}, bf16[16,32,1,128]{3,2,1,0:T(2,128)(2,1)S(1)}) fusion(bf16[16,32,4,128]{3,2,1,0:T(4,128)(2,1)} %param.13), kind=kLoop, calls=%fused_computation.10 | loop fusion | bytes 524288 | tf_op jit(solution)/shard_map/slice | solution.py:588
  7.0 3.7 %collective-permute-start.4 = (bf16[16,32,128]{2,1,0:T(8,128)(2,1)S(1)}, bf16[16,32,128]{2,1,0:T(8,128)(2,1)S(1)}, u32[]{:S(2)}, u32[]{:S(2)}) collective-permute-start(bf16[16,32,128]{2,1,0:T(8,128)(2,1)S(1)} %bitcast.51), channel_id=1, source_target_pairs={{0,1},{1,2},{2,3},{3,0},{4,5},{5,6},{6,7},{7,4},{8,9},{9,10},{10,1... | collective-permute-start | bytes 393224 | tf_op jit(solution)/shard_map/ppermute | solution.py:554
  10.6 0.1 collective-permute-start.5
  10.7 0.8 fusion.1
  11.5 3.9 %collective-permute-start.3 = (bf16[16,2,4,128]{3,2,1,0:T(4,128)(2,1)S(1)}, bf16[16,2,4,128]{3,2,1,0:T(4,128)(2,1)S(1)}, u32[]{:S(2)}, u32[]{:S(2)}) collective-permute-start(bf16[16,2,4,128]{3,2,1,0:T(4,128)(2,1)S(1)} %get-tuple-element.33), channel_id=1, source_target_pairs={{4,0},{8,4},{12,8},{16,12},{20,16},{24,20},{28,24},{0,28},{5,1},{9... | collective-permute-start | bytes 98312 | tf_op jit(solution)/shard_map/ppermute | solution.py:559
  15.4 1.0 collective-permute-done.3
  16.4 3.9 %collective-permute-done.2 = bf16[16,2,4,128]{3,2,1,0:T(4,128)(2,1)S(1)} collective-permute-done((bf16[16,2,4,128]{3,2,1,0:T(4,128)(2,1)S(1)}, bf16[16,2,4,128]{3,2,1,0:T(4,128)(2,1)S(1)}, u32[]{:S(2)}, u32[]{:S(2)}) %collective-permute-start.2) | collective-permute-done | bytes 32800 | tf_op jit(solution)/shard_map/ppermute | solution.py:554
  20.3 0.0 copy-start.3
  20.3 0.5 copy-done.15
  20.9 0.1 copy-done.2
  20.9 0.0 copy-done.3
  21.0 44.2 %layer.1 = (bf16[12288,128]{1,0:T(8,128)(2,1)}, f32[2048,128]{1,0:T(8,128)}, bf16[2,128,128]{2,1,0:T(8,128)(2,1)}, bf16[2,128,128]{2,1,0:T(8,128)(2,1)}, bf16[2,...) custom-call(s32[96,128]{1,0:T(8,128)} %bitcast.47, s32[96,128]{1,0:T(8,128)} %bitcast.53, s32[96,128]{1,0:T(8,128)} %bitcast.48, ...), custom_call_target="tpu_custom_call" | custom-call | tf_op jit(solution)/shard_map/layer/pallas_call | solution.py:450
  65.2 0.0 copy-start.7
  65.2 0.0 copy-start.6
  65.2 24.2 %all_to_all.10 = f32[128,8,128]{2,1,0:T(8,128)S(1)} all-to-all(f32[128,8,128]{2,1,0:T(8,128)} %bitcast.46), channel_id=1, replica_groups=mesh['gx'=4,'gy'=8,'gz'=4] {'gx','gy','gz'}, dimensions={0} | all-to-all | bytes 1048576 | tf_op jit(solution)/shard_map/all_to_all | solution.py:567
  89.4 0.1 reduce_sum.9
  89.6 0.8 broadcast_in_dim.2
  90.4 3.9 %all-to-all-start.1 = ((f32[128,8,128]{2,1,0:T(8,128)}), f32[128,8,128]{2,1,0:T(8,128)S(1)}, u32[]{:S(2)}, u32[]{:S(2)}) async-start(f32[128,8,128]{2,1,0:T(8,128)} %broadcast_in_dim.2), calls=%async_computation.1 | async-start | bytes 1048576 | tf_op jit(solution)/shard_map/all_to_all | solution.py:569
  94.3 2.8 %collective-permute-start.7 = (bf16[128,128]{1,0:T(8,128)(2,1)S(1)}, bf16[128,128]{1,0:T(8,128)(2,1)S(1)}, u32[]{:S(2)}, u32[]{:S(2)}) collective-permute-start(bf16[128,128]{1,0:T(8,128)(2,1)S(1)} %get-tuple-element.41), channel_id=1, source_target_pairs={{32,0},{64,32},{96,64},{0,96},{33,1},{65,33},{97,65},{1,97},{34,2}... | collective-permute-start | bytes 98312 | tf_op jit(solution)/shard_map/ppermute | solution.py:559
  97.2 0.7 collective-permute-start.11
  97.9 2.7 %collective-permute-start.10 = (bf16[512,128]{1,0:T(8,128)(2,1)S(1)}, bf16[512,128]{1,0:T(8,128)(2,1)S(1)}, u32[]{:S(2)}, u32[]{:S(2)}) collective-permute-start(bf16[512,128]{1,0:T(8,128)(2,1)S(1)} %get-tuple-element.38), channel_id=1, source_target_pairs={{0,1},{1,2},{2,3},{3,0},{4,5},{5,6},{6,7},{7,4},{8,9},{9,10},{10,1... | collective-permute-start | bytes 393224 | tf_op jit(solution)/shard_map/ppermute | solution.py:554
  100.6 4.1 %collective-permute-start.9 = (bf16[128,128]{1,0:T(8,128)(2,1)S(1)}, bf16[128,128]{1,0:T(8,128)(2,1)S(1)}, u32[]{:S(2)}, u32[]{:S(2)}) collective-permute-start(bf16[128,128]{1,0:T(8,128)(2,1)S(1)} %get-tuple-element.39), channel_id=1, source_target_pairs={{4,0},{8,4},{12,8},{16,12},{20,16},{24,20},{28,24},{0,28},{5,1},{9... | collective-permute-start | bytes 98312 | tf_op jit(solution)/shard_map/ppermute | solution.py:559
  104.7 1.1 collective-permute-done.9.yhi_ref
  105.8 3.8 %collective-permute-done.8.ylo_ref = bf16[128,128]{1,0:T(8,128)(2,1)S(1)} collective-permute-done((bf16[128,128]{1,0:T(8,128)(2,1)S(1)}, bf16[128,128]{1,0:T(8,128)(2,1)S(1)}, u32[]{:S(2)}, u32[]{:S(2)}) %collective-permute-start.8) | collective-permute-done | bytes 32800 | tf_op jit(solution)/shard_map/ppermute | solution.py:554
  109.7 0.5 copy-done.14
  110.2 0.1 copy-done.4
  110.3 0.1 copy-done.5
  110.4 0.2 copy-done
  110.5 2.8 %finish.1 = (bf16[2048,128]{1,0:T(8,128)(2,1)}, f32[384,128]{1,0:T(8,128)}, f32[128,128]{1,0:T(8,128)}, f32[256,128]{1,0:T(8,128)}, f32[128,128]{1,0:T(8,128)}, /*index=5*/f32[4,128]{1,0:T(4,128)}) custom-call(f32[2048,128]{1,0:T(8,128)} %get-tuple-element.19.gown_ref, bf16[128,128]{1,0:T(8,128)(2,1)} %copy-done.9, bf16[128,128]{1,0:T(8,128)(2,1)} %copy-done.8, ...), custom_call_target="tpu_custom_call" | custom-call | tf_op jit(solution)/shard_map/finish/pallas_call | solution.py:535
  (39 shorter events, 0.1 us)
Async XLA Ops:
  1.4 13.9 %collective-permute-start.1 = (bf16[32,4,128]{2,1,0:T(4,128)(2,1)S(1)}, bf16[32,4,128]{2,1,0:T(4,128)(2,1)S(1)}, u32[]{:S(2)}, u32[]{:S(2)}) collective-permute-start(bf16[32,4,128]{2,1,0:T(4,128)(2,1)S(1)} %get-tuple-element.35), channel_id=1, source_target_pairs={{32,0},{64,32},{96,64},{0,96},{33,1},{65,33},{97,65},{1,97},{34,2}... | collective-permute-start | bytes 98312 | tf_op jit(solution)/shard_map/ppermute | solution.py:559
  5.1 10.3 %collective-permute-start = (bf16[32,4,128]{2,1,0:T(4,128)(2,1)S(1)}, bf16[32,4,128]{2,1,0:T(4,128)(2,1)S(1)}, u32[]{:S(2)}, u32[]{:S(2)}) collective-permute-start(bf16[32,4,128]{2,1,0:T(4,128)(2,1)S(1)} %get-tuple-element.36), channel_id=1, source_target_pairs={{0,32},{32,64},{64,96},{96,0},{1,33},{33,65},{65,97},{97,1},{2,34}... | collective-permute-start | bytes 98312 | tf_op jit(solution)/shard_map/ppermute | solution.py:554
  7.0 13.3 %collective-permute-start.4 = (bf16[16,32,128]{2,1,0:T(8,128)(2,1)S(1)}, bf16[16,32,128]{2,1,0:T(8,128)(2,1)S(1)}, u32[]{:S(2)}, u32[]{:S(2)}) collective-permute-start(bf16[16,32,128]{2,1,0:T(8,128)(2,1)S(1)} %bitcast.51), channel_id=1, source_target_pairs={{0,1},{1,2},{2,3},{3,0},{4,5},{5,6},{6,7},{7,4},{8,9},{9,10},{10,1... | collective-permute-start | bytes 393224 | tf_op jit(solution)/shard_map/ppermute | solution.py:554
  10.6 9.6 %collective-permute-start.5 = (bf16[16,32,128]{2,1,0:T(8,128)(2,1)S(1)}, bf16[16,32,128]{2,1,0:T(8,128)(2,1)S(1)}, u32[]{:S(2)}, u32[]{:S(2)}) collective-permute-start(bf16[16,32,128]{2,1,0:T(8,128)(2,1)S(1)} %bitcast.52), channel_id=1, source_target_pairs={{1,0},{2,1},{3,2},{0,3},{5,4},{6,5},{7,6},{4,7},{9,8},{10,9},{11,1... | collective-permute-start | bytes 393224 | tf_op jit(solution)/shard_map/ppermute | solution.py:559
  11.5 4.9 %collective-permute-start.3 = (bf16[16,2,4,128]{3,2,1,0:T(4,128)(2,1)S(1)}, bf16[16,2,4,128]{3,2,1,0:T(4,128)(2,1)S(1)}, u32[]{:S(2)}, u32[]{:S(2)}) collective-permute-start(bf16[16,2,4,128]{3,2,1,0:T(4,128)(2,1)S(1)} %get-tuple-element.33), channel_id=1, source_target_pairs={{4,0},{8,4},{12,8},{16,12},{20,16},{24,20},{28,24},{0,28},{5,1},{9... | collective-permute-start | bytes 98312 | tf_op jit(solution)/shard_map/ppermute | solution.py:559
  15.4 4.9 %copy-start.10 = (bf16[32,4,128]{2,1,0:T(4,128)(2,1)}, bf16[32,4,128]{2,1,0:T(4,128)(2,1)S(1)}, u32[]{:S(2)}) copy-start(bf16[32,4,128]{2,1,0:T(4,128)(2,1)S(1)} %collective-permute-done.1) | copy-start | bytes 98308
  15.4 4.9 %collective-permute-start.2 = (bf16[16,2,4,128]{3,2,1,0:T(4,128)(2,1)S(1)}, bf16[16,2,4,128]{3,2,1,0:T(4,128)(2,1)S(1)}, u32[]{:S(2)}, u32[]{:S(2)}) collective-permute-start(bf16[16,2,4,128]{3,2,1,0:T(4,128)(2,1)S(1)} %get-tuple-element.34), channel_id=1, source_target_pairs={{0,4},{4,8},{8,12},{12,16},{16,20},{20,24},{24,28},{28,0},{1,5},{5... | collective-permute-start | bytes 98312 | tf_op jit(solution)/shard_map/ppermute | solution.py:554
  15.4 4.9 %copy-start.11 = (bf16[32,4,128]{2,1,0:T(4,128)(2,1)}, bf16[32,4,128]{2,1,0:T(4,128)(2,1)S(1)}, u32[]{:S(2)}) copy-start(bf16[32,4,128]{2,1,0:T(4,128)(2,1)S(1)} %collective-permute-done) | copy-start | bytes 98308
  16.4 3.9 %copy-start.13 = (bf16[16,2,4,128]{3,2,1,0:T(4,128)(2,1)}, bf16[16,2,4,128]{3,2,1,0:T(4,128)(2,1)S(1)}, u32[]{:S(2)}) copy-start(bf16[16,2,4,128]{3,2,1,0:T(4,128)(2,1)S(1)} %collective-permute-done.3) | copy-start | bytes 98308
  20.3 0.6 copy-start.15
  20.3 0.7 copy-start.2
  20.3 0.7 copy-start.3
  65.2 29.1 %copy-start.7 = (bf16[2,128,128]{2,1,0:T(8,128)(2,1)S(1)}, bf16[2,128,128]{2,1,0:T(8,128)(2,1)}, u32[]{:S(2)}) copy-start(bf16[2,128,128]{2,1,0:T(8,128)(2,1)} %get-tuple-element.20) | copy-start | bytes 196612
  65.2 32.0 %copy-start.1 = (bf16[2,512,128]{2,1,0:T(8,128)(2,1)S(1)}, bf16[2,512,128]{2,1,0:T(8,128)(2,1)}, u32[]{:S(2)}) copy-start(bf16[2,512,128]{2,1,0:T(8,128)(2,1)} %get-tuple-element.22) | copy-start | bytes 786436
  65.2 35.4 %copy-start.6 = (bf16[2,128,128]{2,1,0:T(8,128)(2,1)S(1)}, bf16[2,128,128]{2,1,0:T(8,128)(2,1)}, u32[]{:S(2)}) copy-start(bf16[2,128,128]{2,1,0:T(8,128)(2,1)} %get-tuple-element.21) | copy-start | bytes 196612
  90.4 19.3 %all-to-all-start.1 = ((f32[128,8,128]{2,1,0:T(8,128)}), f32[128,8,128]{2,1,0:T(8,128)S(1)}, u32[]{:S(2)}, u32[]{:S(2)}) async-start(f32[128,8,128]{2,1,0:T(8,128)} %broadcast_in_dim.2), calls=%async_computation.1 | async-start | bytes 1048576 | tf_op jit(solution)/shard_map/all_to_all | solution.py:569
  94.3 10.4 %collective-permute-start.7 = (bf16[128,128]{1,0:T(8,128)(2,1)S(1)}, bf16[128,128]{1,0:T(8,128)(2,1)S(1)}, u32[]{:S(2)}, u32[]{:S(2)}) collective-permute-start(bf16[128,128]{1,0:T(8,128)(2,1)S(1)} %get-tuple-element.41), channel_id=1, source_target_pairs={{32,0},{64,32},{96,64},{0,96},{33,1},{65,33},{97,65},{1,97},{34,2}... | collective-permute-start | bytes 98312 | tf_op jit(solution)/shard_map/ppermute | solution.py:559
  97.1 7.6 %collective-permute-start.6 = (bf16[128,128]{1,0:T(8,128)(2,1)S(1)}, bf16[128,128]{1,0:T(8,128)(2,1)S(1)}, u32[]{:S(2)}, u32[]{:S(2)}) collective-permute-start(bf16[128,128]{1,0:T(8,128)(2,1)S(1)} %get-tuple-element.42), channel_id=1, source_target_pairs={{0,32},{32,64},{64,96},{96,0},{1,33},{33,65},{65,97},{97,1},{2,34}... | collective-permute-start | bytes 98312 | tf_op jit(solution)/shard_map/ppermute | solution.py:554
  97.2 12.5 %collective-permute-start.11 = (bf16[512,128]{1,0:T(8,128)(2,1)S(1)}, bf16[512,128]{1,0:T(8,128)(2,1)S(1)}, u32[]{:S(2)}, u32[]{:S(2)}) collective-permute-start(bf16[512,128]{1,0:T(8,128)(2,1)S(1)} %get-tuple-element.37), channel_id=1, source_target_pairs={{1,0},{2,1},{3,2},{0,3},{5,4},{6,5},{7,6},{4,7},{9,8},{10,9},{11,1... | collective-permute-start | bytes 393224 | tf_op jit(solution)/shard_map/ppermute | solution.py:559
  97.9 11.7 %collective-permute-start.10 = (bf16[512,128]{1,0:T(8,128)(2,1)S(1)}, bf16[512,128]{1,0:T(8,128)(2,1)S(1)}, u32[]{:S(2)}, u32[]{:S(2)}) collective-permute-start(bf16[512,128]{1,0:T(8,128)(2,1)S(1)} %get-tuple-element.38), channel_id=1, source_target_pairs={{0,1},{1,2},{2,3},{3,0},{4,5},{5,6},{6,7},{7,4},{8,9},{9,10},{10,1... | collective-permute-start | bytes 393224 | tf_op jit(solution)/shard_map/ppermute | solution.py:554
  100.6 5.2 %collective-permute-start.9 = (bf16[128,128]{1,0:T(8,128)(2,1)S(1)}, bf16[128,128]{1,0:T(8,128)(2,1)S(1)}, u32[]{:S(2)}, u32[]{:S(2)}) collective-permute-start(bf16[128,128]{1,0:T(8,128)(2,1)S(1)} %get-tuple-element.39), channel_id=1, source_target_pairs={{4,0},{8,4},{12,8},{16,12},{20,16},{24,20},{28,24},{0,28},{5,1},{9... | collective-permute-start | bytes 98312 | tf_op jit(solution)/shard_map/ppermute | solution.py:559
  104.7 5.0 %copy-start.8 = (bf16[128,128]{1,0:T(8,128)(2,1)}, bf16[128,128]{1,0:T(8,128)(2,1)S(1)}, u32[]{:S(2)}) copy-start(bf16[128,128]{1,0:T(8,128)(2,1)S(1)} %collective-permute-done.7.xhi_ref) | copy-start | bytes 98308
  104.7 4.9 %collective-permute-start.8 = (bf16[128,128]{1,0:T(8,128)(2,1)S(1)}, bf16[128,128]{1,0:T(8,128)(2,1)S(1)}, u32[]{:S(2)}, u32[]{:S(2)}) collective-permute-start(bf16[128,128]{1,0:T(8,128)(2,1)S(1)} %get-tuple-element.40), channel_id=1, source_target_pairs={{0,4},{4,8},{8,12},{12,16},{16,20},{20,24},{24,28},{28,0},{1,5},{5... | collective-permute-start | bytes 98312 | tf_op jit(solution)/shard_map/ppermute | solution.py:554
  104.7 5.0 %copy-start.9 = (bf16[128,128]{1,0:T(8,128)(2,1)}, bf16[128,128]{1,0:T(8,128)(2,1)S(1)}, u32[]{:S(2)}) copy-start(bf16[128,128]{1,0:T(8,128)(2,1)S(1)} %collective-permute-done.6.xlo_ref) | copy-start | bytes 98308
  105.8 3.9 %copy-start.12 = (bf16[128,128]{1,0:T(8,128)(2,1)}, bf16[128,128]{1,0:T(8,128)(2,1)S(1)}, u32[]{:S(2)}) copy-start(bf16[128,128]{1,0:T(8,128)(2,1)S(1)} %collective-permute-done.9.yhi_ref) | copy-start | bytes 98308
  109.6 0.6 copy-start.14
  109.6 0.7 copy-start.4
  109.6 0.7 copy-start.5
  109.7 0.9 copy-start

commit v3 on v2

--- a/solution.py
+++ b/solution.py
@@ -14,9 +14,9 @@
 TILES = EDGES // TILE
 WIN = 64
 MID = 128
-GROUP = 2
+GROUP = 8
 HALF = TILE // H
-CHUNKS = 4
+CHUNKS = 3
 ROWS = CELLS + 128
 STRIDE = 208
 GRID = N_PLANE * STRIDE + 128
@@ -127,9 +127,9 @@
     smid_ref[...] = jnp.zeros(smid_ref.shape, F32)
     mid_ref[...] = jnp.zeros(mid_ref.shape, F32)
     wide_ref[...] = jnp.zeros(wide_ref.shape, F32)
-    dd_ref[CELLS:ROWS] = jnp.zeros((ROWS - CELLS, 2 * H), BF16)
-    home_ref[CELLS:ROWS] = jnp.zeros((ROWS - CELLS, H), BF16)
-    ppad_ref[CELLS + 2 * PLANE :] = jnp.zeros((PAD_ROWS - CELLS - 2 * PLANE, H), BF16)
+    dd_ref[CELLS:ROWS] = jnp.zeros((ROWS - CELLS, 2 * H), F32)
+    home_ref[CELLS:ROWS] = jnp.zeros((ROWS - CELLS, H), F32)
+    ppad_ref[CELLS + 2 * PLANE :] = jnp.zeros((PAD_ROWS - CELLS - 2 * PLANE, H), F32)
     const_ref[:, 0:H] = flip(w2e_ref[...])
     const_ref[:, H:] = hot(iota((H, H), 0) == iota((H, H), 1))
     flip_ref[0:H] = flip(w1b)
@@ -143,8 +143,8 @@
     place = jnp.where(delta == 204, r + 4096, jnp.where(delta == -204, r + 8192, inside))
     code_ref[...] = place * 2048 + r
 
-    ppad_ref[0:PLANE] = dot(xlo_ref[...], w1b).astype(BF16)
-    ppad_ref[CELLS + PLANE : CELLS + 2 * PLANE] = dot(xhi_ref[...], w1b).astype(BF16)
+    ppad_ref[0:PLANE] = dot(xlo_ref[...], w1b)
+    ppad_ref[CELLS + PLANE : CELLS + 2 * PLANE] = dot(xhi_ref[...], w1b)
     yx_ref[0:PLANE] = dot(ylo_ref[...], w1b)
     yx_ref[PLANE : 2 * PLANE] = dot(yhi_ref[...], w1b)
     zx_ref[0] = dot(zlo_ref[...], w1b)
@@ -153,8 +153,8 @@
     for i in range(N_PLANE):
         at = slice(i * PLANE, (i + 1) * PLANE)
         base = i * STRIDE
-        ppad_ref[(i + 1) * PLANE : (i + 2) * PLANE] = own_ref[at].astype(BF16)
-        home_ref[at] = (dot(node_ref[at], w1c) + b1e_ref[...]).astype(BF16)
+        ppad_ref[(i + 1) * PLANE : (i + 2) * PLANE] = own_ref[at]
+        home_ref[at] = dot(node_ref[at], w1c) + b1e_ref[...]
         for l in range(4):
             mid_ref[pl.ds(base + 7 + l, 32, 6), :] = own_ref[pl.ds(i * PLANE + l, 32, 4), :]
         mid_ref[pl.ds(base + 6, 32, 6), :] = zx_ref[0, i * 32 : (i + 1) * 32, :]
@@ -171,13 +171,13 @@
     far = 1 << 14
 
     def start_of(t):
-        return pl.multiple_of((near_ref[HALF * t, 0] >> 4) << 4, 16)
+        return pl.multiple_of((near_ref[HALF * t, 0] >> 3) << 3, 8)
 
     def windows_of(t):
         return ((near_ref[HALF * t + HALF - 1, H - 1] - start_of(t)) >> 6) + 1
 
     def mid_of(w):
-        return pl.multiple_of((w >> 7) * STRIDE + ((w & 127) >> 4) * 24, 8)
+        return pl.multiple_of((w >> 7) * STRIDE + ((w & 127) >> 4) * 24 + (w & 8), 8)
 
     def rows_of(t):
         return pl.ds(pl.multiple_of(t * TILE, TILE), TILE)
@@ -206,9 +206,9 @@
         ]
         right = [
             mid_ref[pl.ds(mid, MID), :].astype(BF16),
-            ppad_ref[pl.ds(w + 2 * PLANE, WIN), :],
-            ppad_ref[pl.ds(w, WIN), :],
-            home_ref[pl.ds(w, MID), :],
+            ppad_ref[pl.ds(w + 2 * PLANE, WIN), :].astype(BF16),
+            ppad_ref[pl.ds(w, WIN), :].astype(BF16),
+            home_ref[pl.ds(w, MID), :].astype(BF16),
         ]
         return dot(jnp.concatenate(left + rest, axis=1), jnp.concatenate(right + weights, axis=0))
 
@@ -242,7 +242,7 @@
         zacc_ref[:, 0:H] = dot(e_ref[rows_of(t), :], w1a)
 
         def more(k, carry):
-            w = pl.multiple_of(start_of(t) + k * WIN, 16)
+            w = pl.multiple_of(start_of(t) + k * WIN, 8)
             zacc_ref[:, 0:H] += gather_pre(col_ref[rows_of(t), :], w, [], [], True)
             return carry
 
@@ -250,7 +250,7 @@
         activate(t, zacc_ref[:, 0:H])
 
         def put(k, carry):
-            w = pl.multiple_of(start_of(t) + k * WIN, 16)
+            w = pl.multiple_of(start_of(t) + k * WIN, 8)
             collect(t, w, jnp.concatenate([e_ref[rows_of(t), :], u_ref[rows_of(t), :]], axis=1))
             return carry
 
@@ -304,20 +304,20 @@
         cot32 = cot.astype(F32)
         gown_ref[at, :] = cot32 + dx[:, 0:H]
         dagg = dx[:, H:].astype(BF16)
-        dd_ref[at, 0:H] = dot(dagg, const_ref[:, 0:H]).astype(BF16)
-        dd_ref[at, H:] = dagg
+        dd_ref[at, 0:H] = dot(dagg, const_ref[:, 0:H])
+        dd_ref[at, H:] = dx[:, H:]
         par_ref[4 * H : 6 * H, :] += dot_first(x, dz)
         par_ref[6 * H : 7 * H, :] += dot_first(u.astype(BF16), cot)
         par_ref[7 * H + 2 : 7 * H + 3, :] += jnp.sum(dz.astype(F32), axis=0, keepdims=True)
         par_ref[7 * H + 3 : 7 * H + 4, :] += jnp.sum(cot32, axis=0, keepdims=True)
         return carry
 
-    lax.fori_loop(0, CELLS // TILE, cells, 0, unroll=2)
+    lax.fori_loop(0, CELLS // TILE, cells, 0, unroll=8)
     copy_cot.wait()
 
     def spread(col, w, cot):
         left = jnp.concatenate([hot((col & 2047) - w == lane), cot], axis=1)
-        right = jnp.concatenate([dd_ref[pl.ds(w, H), :], const_ref[...]], axis=0)
+        right = jnp.concatenate([dd_ref[pl.ds(w, H), :].astype(BF16), const_ref[...]], axis=0)
         return dot(left, right)
 
     def scatter(t, w, dz, guard):
@@ -362,7 +362,7 @@
         zacc_ref[...] = dot(cot_ref[rows_of(t), :], const_ref[...])
 
         def more(k, carry):
-            w = pl.multiple_of(start_of(t) + k * H, 16)
+            w = pl.multiple_of(start_of(t) + k * H, 8)
             zacc_ref[...] += spread(
                 col_ref[rows_of(t), :], w, jnp.zeros((TILE, H), BF16)
             )
@@ -372,7 +372,7 @@
         dz_ref[...] = finish_edges(t, zacc_ref[...])
 
         def put(k, carry):
-            scatter(t, pl.multiple_of(start_of(t) + k * WIN, 16), dz_ref[...], True)
+            scatter(t, pl.multiple_of(start_of(t) + k * WIN, 8), dz_ref[...], True)
             return carry
 
         lax.fori_loop(0, windows_of(t), put, 0)
@@ -412,7 +412,7 @@
         gown_ref[at, :] += dot(sr16, flip_ref[0 : 2 * H])
         return carry
 
-    lax.fori_loop(0, CELLS // TILE, gather_cells, 0, unroll=2)
+    lax.fori_loop(0, CELLS // TILE, gather_cells, 0, unroll=8)
     both = dot_first(node_ref[...], sr_ref[...])
     w1b_flip = flip_ref[0:H]
     sx_lo = spad_ref[0:PLANE].astype(BF16)
@@ -467,8 +467,8 @@
             pltpu.VMEM((CELLS, H), F32),
             pltpu.VMEM((2, CELLS // 4, H), F32),
             pltpu.VMEM((2 * PLANE, H), F32),
-            pltpu.VMEM((PAD_ROWS, H), BF16),
-            pltpu.VMEM((ROWS, H), BF16),
+            pltpu.VMEM((PAD_ROWS, H), F32),
+            pltpu.VMEM((ROWS, H), F32),
             pltpu.VMEM((GRID, H), F32),
             pltpu.VMEM((EDGES // H, H), jnp.int32),
             pltpu.VMEM((EDGES, H), jnp.int32),
@@ -476,7 +476,7 @@
             pltpu.VMEM((EDGES, H), BF16),
             pltpu.VMEM((ROWS, 2 * H), F32),
             pltpu.VMEM((ROWS, H), F32),
-            pltpu.VMEM((ROWS, 2 * H), BF16),
+            pltpu.VMEM((ROWS, 2 * H), F32),
             pltpu.VMEM((PAD_ROWS, H), F32),
             pltpu.VMEM((ROWS, H), F32),
             pltpu.VMEM((GRID, H), F32),

time: 113 us -> 103 us (0.912)
  Pallas kernels: 46.9 us -> 37.3 us
  blocking collectives: 24.2 us -> 23 us
    pallas_call x1, Pallas kernels: 44.2 us -> 34.5 us  [layer_call(): pl.pallas_call(layer_kernel, in_specs=[smem] + [vmem] * 10 + [hbm] * 2 +...]
    all_to_all x1, blocking collectives: 24.2 us -> 23 us  [sum_over_devices(): mine = jnp.sum(lax.all_to_all(chunks, AXES, 0, 0, tiled=True), axis=0)]
  transfers between devices with their start and end apart: 13 -> 13, of which waited for: 4 -> 4; matrix products, arithmetic and copies ran while one was open for 2% -> 3% of each run, Pallas kernels for 0% -> 0%
where the time goes in v3:
time: 103 us; the launch traced here: 102 us
  Pallas kernels  37.3 us (36%)
  starting transfers between devices  25.4 us (25%)
  blocking collectives  23 us (22%)
  waiting for transfers between devices  9.78 us (9%)
  local copies, waits for them, and re-layouts  5.89 us (6%)
    pallas_call x1, Pallas kernels, layer_call(): pl.pallas_call(layer_kernel, in_specs=[smem] + [vmem] * 10 + [hbm] * 2 +...  34.5 us
    all_to_all x1, blocking collectives, sum_over_devices(): mine = jnp.sum(lax.all_to_all(chunks, AXES, 0, 0, tiled=True), axis=0)  23 us
    ppermute x6, starting transfers between devices, from_next(): return lax.ppermute(value, axis, [((k + 1) % n, k) for k in range(n)])  15.2 us
    ppermute x6, waiting for transfers between devices, from_previous(): return lax.ppermute(value, axis, [(k, (k + 1) % n) for k in range(n)])  7.69 us
    ppermute x6, starting transfers between devices, from_previous(): return lax.ppermute(value, axis, [(k, (k + 1) % n) for k in range(n)])  6.35 us
    all_to_all x1, starting transfers between devices, sum_over_devices(): return lax.all_to_all(copies, AXES, 0, 0, tiled=True).reshape(-1, H)  3.89 us
    pallas_call x1, Pallas kernels, finish_call(): pl.pallas_call(finish_kernel, in_specs=[pl.BlockSpec(memory_space=pltpu.V...  2.76 us
    ppermute x6, waiting for transfers between devices, from_next(): return lax.ppermute(value, axis, [((k + 1) % n, k) for k in range(n)])  2.09 us
  transfers between devices with their start and end apart: 13, of which 4 were waited for; matrix products, arithmetic and copies ran while one was open for 3% of the time, Pallas kernels for 0%

profile of v3, /device:TPU:1, one launch (start us, length us, event | category | flops | bytes accessed | tf_op | source)
XLA Modules:
  0.0 102.4 jit_solution(9347961154712182836)
XLA Ops:
  0.6 0.8 slice_bitcast_fusion.6
  1.4 3.6 %collective-permute-start.1 = (bf16[32,4,128]{2,1,0:T(4,128)(2,1)S(1)}, bf16[32,4,128]{2,1,0:T(4,128)(2,1)S(1)}, u32[]{:S(2)}, u32[]{:S(2)}) collective-permute-start(bf16[32,4,128]{2,1,0:T(4,128)(2,1)S(1)} %get-tuple-element.35), channel_id=1, source_target_pairs={{32,0},{64,32},{96,64},{0,96},{33,1},{65,33},{97,65},{1,97},{34,2}... | collective-permute-start | bytes 98312 | tf_op jit(solution)/shard_map/ppermute | solution.py:559
  5.1 0.0 collective-permute-start
  5.1 1.9 %fusion = (bf16[16,32,1,128]{3,2,1,0:T(2,128)(2,1)S(1)}, bf16[16,32,1,128]{3,2,1,0:T(2,128)(2,1)S(1)}) fusion(bf16[16,32,4,128]{3,2,1,0:T(4,128)(2,1)} %param.13), kind=kLoop, calls=%fused_computation.10 | loop fusion | bytes 524288 | tf_op jit(solution)/shard_map/slice | solution.py:588
  7.0 3.7 %collective-permute-start.4 = (bf16[16,32,128]{2,1,0:T(8,128)(2,1)S(1)}, bf16[16,32,128]{2,1,0:T(8,128)(2,1)S(1)}, u32[]{:S(2)}, u32[]{:S(2)}) collective-permute-start(bf16[16,32,128]{2,1,0:T(8,128)(2,1)S(1)} %bitcast.51), channel_id=1, source_target_pairs={{0,1},{1,2},{2,3},{3,0},{4,5},{5,6},{6,7},{7,4},{8,9},{9,10},{10,1... | collective-permute-start | bytes 393224 | tf_op jit(solution)/shard_map/ppermute | solution.py:554
  10.6 0.1 collective-permute-start.5
  10.7 0.8 fusion.1
  11.5 3.9 %collective-permute-start.3 = (bf16[16,2,4,128]{3,2,1,0:T(4,128)(2,1)S(1)}, bf16[16,2,4,128]{3,2,1,0:T(4,128)(2,1)S(1)}, u32[]{:S(2)}, u32[]{:S(2)}) collective-permute-start(bf16[16,2,4,128]{3,2,1,0:T(4,128)(2,1)S(1)} %get-tuple-element.33), channel_id=1, source_target_pairs={{4,0},{8,4},{12,8},{16,12},{20,16},{24,20},{28,24},{0,28},{5,1},{9... | collective-permute-start | bytes 98312 | tf_op jit(solution)/shard_map/ppermute | solution.py:559
  15.4 1.0 collective-permute-done.3
  16.4 3.9 %collective-permute-done.2 = bf16[16,2,4,128]{3,2,1,0:T(4,128)(2,1)S(1)} collective-permute-done((bf16[16,2,4,128]{3,2,1,0:T(4,128)(2,1)S(1)}, bf16[16,2,4,128]{3,2,1,0:T(4,128)(2,1)S(1)}, u32[]{:S(2)}, u32[]{:S(2)}) %collective-permute-start.2) | collective-permute-done | bytes 32800 | tf_op jit(solution)/shard_map/ppermute | solution.py:554
  20.3 0.0 copy-start.3
  20.3 0.5 copy-done.15
  20.9 0.1 copy-done.2
  20.9 0.0 copy-done.3
  21.0 34.5 %layer.1 = (bf16[12288,128]{1,0:T(8,128)(2,1)}, f32[2048,128]{1,0:T(8,128)}, bf16[2,128,128]{2,1,0:T(8,128)(2,1)}, bf16[2,128,128]{2,1,0:T(8,128)(2,1)}, bf16[2,...) custom-call(s32[96,128]{1,0:T(8,128)} %bitcast.47, s32[96,128]{1,0:T(8,128)} %bitcast.53, s32[96,128]{1,0:T(8,128)} %bitcast.48, ...), custom_call_target="tpu_custom_call" | custom-call | tf_op jit(solution)/shard_map/layer/pallas_call | solution.py:450
  55.5 0.0 copy-start.7
  55.5 0.0 copy-start.6
  55.5 23.0 %all_to_all.10 = f32[128,8,128]{2,1,0:T(8,128)S(1)} all-to-all(f32[128,8,128]{2,1,0:T(8,128)} %bitcast.46), channel_id=1, replica_groups=mesh['gx'=4,'gy'=8,'gz'=4] {'gx','gy','gz'}, dimensions={0} | all-to-all | bytes 1048576 | tf_op jit(solution)/shard_map/all_to_all | solution.py:567
  78.5 0.1 reduce_sum.9
  78.7 0.8 broadcast_in_dim.2
  79.5 3.9 %all-to-all-start.1 = ((f32[128,8,128]{2,1,0:T(8,128)}), f32[128,8,128]{2,1,0:T(8,128)S(1)}, u32[]{:S(2)}, u32[]{:S(2)}) async-start(f32[128,8,128]{2,1,0:T(8,128)} %broadcast_in_dim.2), calls=%async_computation.1 | async-start | bytes 1048576 | tf_op jit(solution)/shard_map/all_to_all | solution.py:569
  83.4 2.8 %collective-permute-start.7 = (bf16[128,128]{1,0:T(8,128)(2,1)S(1)}, bf16[128,128]{1,0:T(8,128)(2,1)S(1)}, u32[]{:S(2)}, u32[]{:S(2)}) collective-permute-start(bf16[128,128]{1,0:T(8,128)(2,1)S(1)} %get-tuple-element.41), channel_id=1, source_target_pairs={{32,0},{64,32},{96,64},{0,96},{33,1},{65,33},{97,65},{1,97},{34,2}... | collective-permute-start | bytes 98312 | tf_op jit(solution)/shard_map/ppermute | solution.py:559
  86.3 0.7 collective-permute-start.11
  87.0 2.7 %collective-permute-start.10 = (bf16[512,128]{1,0:T(8,128)(2,1)S(1)}, bf16[512,128]{1,0:T(8,128)(2,1)S(1)}, u32[]{:S(2)}, u32[]{:S(2)}) collective-permute-start(bf16[512,128]{1,0:T(8,128)(2,1)S(1)} %get-tuple-element.38), channel_id=1, source_target_pairs={{0,1},{1,2},{2,3},{3,0},{4,5},{5,6},{6,7},{7,4},{8,9},{9,10},{10,1... | collective-permute-start | bytes 393224 | tf_op jit(solution)/shard_map/ppermute | solution.py:554
  89.7 4.1 %collective-permute-start.9 = (bf16[128,128]{1,0:T(8,128)(2,1)S(1)}, bf16[128,128]{1,0:T(8,128)(2,1)S(1)}, u32[]{:S(2)}, u32[]{:S(2)}) collective-permute-start(bf16[128,128]{1,0:T(8,128)(2,1)S(1)} %get-tuple-element.39), channel_id=1, source_target_pairs={{4,0},{8,4},{12,8},{16,12},{20,16},{24,20},{28,24},{0,28},{5,1},{9... | collective-permute-start | bytes 98312 | tf_op jit(solution)/shard_map/ppermute | solution.py:559
  93.8 1.1 %collective-permute-done.9.yhi_ref = bf16[128,128]{1,0:T(8,128)(2,1)S(1)} collective-permute-done((bf16[128,128]{1,0:T(8,128)(2,1)S(1)}, bf16[128,128]{1,0:T(8,128)(2,1)S(1)}, u32[]{:S(2)}, u32[]{:S(2)}) %collective-permute-start.9) | collective-permute-done | bytes 32800 | tf_op jit(solution)/shard_map/ppermute | solution.py:559
  94.9 3.8 %collective-permute-done.8.ylo_ref = bf16[128,128]{1,0:T(8,128)(2,1)S(1)} collective-permute-done((bf16[128,128]{1,0:T(8,128)(2,1)S(1)}, bf16[128,128]{1,0:T(8,128)(2,1)S(1)}, u32[]{:S(2)}, u32[]{:S(2)}) %collective-permute-start.8) | collective-permute-done | bytes 32800 | tf_op jit(solution)/shard_map/ppermute | solution.py:554
  98.8 0.5 copy-done.14
  99.3 0.1 copy-done.4
  99.4 0.1 copy-done.5
  99.5 0.2 copy-done
  99.6 2.8 %finish.1 = (bf16[2048,128]{1,0:T(8,128)(2,1)}, f32[384,128]{1,0:T(8,128)}, f32[128,128]{1,0:T(8,128)}, f32[256,128]{1,0:T(8,128)}, f32[128,128]{1,0:T(8,128)}, /*index=5*/f32[4,128]{1,0:T(4,128)}) custom-call(f32[2048,128]{1,0:T(8,128)} %get-tuple-element.19.gown_ref, bf16[128,128]{1,0:T(8,128)(2,1)} %copy-done.9, bf16[128,128]{1,0:T(8,128)(2,1)} %copy-done.8, ...), custom_call_target="tpu_custom_call" | custom-call | tf_op jit(solution)/shard_map/finish/pallas_call | solution.py:535
  (39 shorter events, 0.1 us)
Async XLA Ops:
  1.4 13.9 %collective-permute-start.1 = (bf16[32,4,128]{2,1,0:T(4,128)(2,1)S(1)}, bf16[32,4,128]{2,1,0:T(4,128)(2,1)S(1)}, u32[]{:S(2)}, u32[]{:S(2)}) collective-permute-start(bf16[32,4,128]{2,1,0:T(4,128)(2,1)S(1)} %get-tuple-element.35), channel_id=1, source_target_pairs={{32,0},{64,32},{96,64},{0,96},{33,1},{65,33},{97,65},{1,97},{34,2}... | collective-permute-start | bytes 98312 | tf_op jit(solution)/shard_map/ppermute | solution.py:559
  5.1 10.3 %collective-permute-start = (bf16[32,4,128]{2,1,0:T(4,128)(2,1)S(1)}, bf16[32,4,128]{2,1,0:T(4,128)(2,1)S(1)}, u32[]{:S(2)}, u32[]{:S(2)}) collective-permute-start(bf16[32,4,128]{2,1,0:T(4,128)(2,1)S(1)} %get-tuple-element.36), channel_id=1, source_target_pairs={{0,32},{32,64},{64,96},{96,0},{1,33},{33,65},{65,97},{97,1},{2,34}... | collective-permute-start | bytes 98312 | tf_op jit(solution)/shard_map/ppermute | solution.py:554
  7.0 13.3 %collective-permute-start.4 = (bf16[16,32,128]{2,1,0:T(8,128)(2,1)S(1)}, bf16[16,32,128]{2,1,0:T(8,128)(2,1)S(1)}, u32[]{:S(2)}, u32[]{:S(2)}) collective-permute-start(bf16[16,32,128]{2,1,0:T(8,128)(2,1)S(1)} %bitcast.51), channel_id=1, source_target_pairs={{0,1},{1,2},{2,3},{3,0},{4,5},{5,6},{6,7},{7,4},{8,9},{9,10},{10,1... | collective-permute-start | bytes 393224 | tf_op jit(solution)/shard_map/ppermute | solution.py:554
  10.6 9.6 %collective-permute-start.5 = (bf16[16,32,128]{2,1,0:T(8,128)(2,1)S(1)}, bf16[16,32,128]{2,1,0:T(8,128)(2,1)S(1)}, u32[]{:S(2)}, u32[]{:S(2)}) collective-permute-start(bf16[16,32,128]{2,1,0:T(8,128)(2,1)S(1)} %bitcast.52), channel_id=1, source_target_pairs={{1,0},{2,1},{3,2},{0,3},{5,4},{6,5},{7,6},{4,7},{9,8},{10,9},{11,1... | collective-permute-start | bytes 393224 | tf_op jit(solution)/shard_map/ppermute | solution.py:559
  11.5 4.9 %collective-permute-start.3 = (bf16[16,2,4,128]{3,2,1,0:T(4,128)(2,1)S(1)}, bf16[16,2,4,128]{3,2,1,0:T(4,128)(2,1)S(1)}, u32[]{:S(2)}, u32[]{:S(2)}) collective-permute-start(bf16[16,2,4,128]{3,2,1,0:T(4,128)(2,1)S(1)} %get-tuple-element.33), channel_id=1, source_target_pairs={{4,0},{8,4},{12,8},{16,12},{20,16},{24,20},{28,24},{0,28},{5,1},{9... | collective-permute-start | bytes 98312 | tf_op jit(solution)/shard_map/ppermute | solution.py:559
  15.4 4.9 %copy-start.10 = (bf16[32,4,128]{2,1,0:T(4,128)(2,1)}, bf16[32,4,128]{2,1,0:T(4,128)(2,1)S(1)}, u32[]{:S(2)}) copy-start(bf16[32,4,128]{2,1,0:T(4,128)(2,1)S(1)} %collective-permute-done.1) | copy-start | bytes 98308
  15.4 4.9 %collective-permute-start.2 = (bf16[16,2,4,128]{3,2,1,0:T(4,128)(2,1)S(1)}, bf16[16,2,4,128]{3,2,1,0:T(4,128)(2,1)S(1)}, u32[]{:S(2)}, u32[]{:S(2)}) collective-permute-start(bf16[16,2,4,128]{3,2,1,0:T(4,128)(2,1)S(1)} %get-tuple-element.34), channel_id=1, source_target_pairs={{0,4},{4,8},{8,12},{12,16},{16,20},{20,24},{24,28},{28,0},{1,5},{5... | collective-permute-start | bytes 98312 | tf_op jit(solution)/shard_map/ppermute | solution.py:554
  15.4 4.9 %copy-start.11 = (bf16[32,4,128]{2,1,0:T(4,128)(2,1)}, bf16[32,4,128]{2,1,0:T(4,128)(2,1)S(1)}, u32[]{:S(2)}) copy-start(bf16[32,4,128]{2,1,0:T(4,128)(2,1)S(1)} %collective-permute-done) | copy-start | bytes 98308
  16.4 3.9 %copy-start.13 = (bf16[16,2,4,128]{3,2,1,0:T(4,128)(2,1)}, bf16[16,2,4,128]{3,2,1,0:T(4,128)(2,1)S(1)}, u32[]{:S(2)}) copy-start(bf16[16,2,4,128]{3,2,1,0:T(4,128)(2,1)S(1)} %collective-permute-done.3) | copy-start | bytes 98308
  20.3 0.6 copy-start.15
  20.3 0.7 copy-start.2
  20.3 0.7 copy-start.3
  55.5 27.9 %copy-start.7 = (bf16[2,128,128]{2,1,0:T(8,128)(2,1)S(1)}, bf16[2,128,128]{2,1,0:T(8,128)(2,1)}, u32[]{:S(2)}) copy-start(bf16[2,128,128]{2,1,0:T(8,128)(2,1)} %get-tuple-element.20) | copy-start | bytes 196612
  55.5 30.8 %copy-start.1 = (bf16[2,512,128]{2,1,0:T(8,128)(2,1)S(1)}, bf16[2,512,128]{2,1,0:T(8,128)(2,1)}, u32[]{:S(2)}) copy-start(bf16[2,512,128]{2,1,0:T(8,128)(2,1)} %get-tuple-element.22) | copy-start | bytes 786436
  55.5 34.2 %copy-start.6 = (bf16[2,128,128]{2,1,0:T(8,128)(2,1)S(1)}, bf16[2,128,128]{2,1,0:T(8,128)(2,1)}, u32[]{:S(2)}) copy-start(bf16[2,128,128]{2,1,0:T(8,128)(2,1)} %get-tuple-element.21) | copy-start | bytes 196612
  79.5 19.3 %all-to-all-start.1 = ((f32[128,8,128]{2,1,0:T(8,128)}), f32[128,8,128]{2,1,0:T(8,128)S(1)}, u32[]{:S(2)}, u32[]{:S(2)}) async-start(f32[128,8,128]{2,1,0:T(8,128)} %broadcast_in_dim.2), calls=%async_computation.1 | async-start | bytes 1048576 | tf_op jit(solution)/shard_map/all_to_all | solution.py:569
  83.4 10.4 %collective-permute-start.7 = (bf16[128,128]{1,0:T(8,128)(2,1)S(1)}, bf16[128,128]{1,0:T(8,128)(2,1)S(1)}, u32[]{:S(2)}, u32[]{:S(2)}) collective-permute-start(bf16[128,128]{1,0:T(8,128)(2,1)S(1)} %get-tuple-element.41), channel_id=1, source_target_pairs={{32,0},{64,32},{96,64},{0,96},{33,1},{65,33},{97,65},{1,97},{34,2}... | collective-permute-start | bytes 98312 | tf_op jit(solution)/shard_map/ppermute | solution.py:559
  86.3 7.6 %collective-permute-start.6 = (bf16[128,128]{1,0:T(8,128)(2,1)S(1)}, bf16[128,128]{1,0:T(8,128)(2,1)S(1)}, u32[]{:S(2)}, u32[]{:S(2)}) collective-permute-start(bf16[128,128]{1,0:T(8,128)(2,1)S(1)} %get-tuple-element.42), channel_id=1, source_target_pairs={{0,32},{32,64},{64,96},{96,0},{1,33},{33,65},{65,97},{97,1},{2,34}... | collective-permute-start | bytes 98312 | tf_op jit(solution)/shard_map/ppermute | solution.py:554
  86.3 12.5 %collective-permute-start.11 = (bf16[512,128]{1,0:T(8,128)(2,1)S(1)}, bf16[512,128]{1,0:T(8,128)(2,1)S(1)}, u32[]{:S(2)}, u32[]{:S(2)}) collective-permute-start(bf16[512,128]{1,0:T(8,128)(2,1)S(1)} %get-tuple-element.37), channel_id=1, source_target_pairs={{1,0},{2,1},{3,2},{0,3},{5,4},{6,5},{7,6},{4,7},{9,8},{10,9},{11,1... | collective-permute-start | bytes 393224 | tf_op jit(solution)/shard_map/ppermute | solution.py:559
  87.0 11.7 %collective-permute-start.10 = (bf16[512,128]{1,0:T(8,128)(2,1)S(1)}, bf16[512,128]{1,0:T(8,128)(2,1)S(1)}, u32[]{:S(2)}, u32[]{:S(2)}) collective-permute-start(bf16[512,128]{1,0:T(8,128)(2,1)S(1)} %get-tuple-element.38), channel_id=1, source_target_pairs={{0,1},{1,2},{2,3},{3,0},{4,5},{5,6},{6,7},{7,4},{8,9},{9,10},{10,1... | collective-permute-start | bytes 393224 | tf_op jit(solution)/shard_map/ppermute | solution.py:554
  89.7 5.2 %collective-permute-start.9 = (bf16[128,128]{1,0:T(8,128)(2,1)S(1)}, bf16[128,128]{1,0:T(8,128)(2,1)S(1)}, u32[]{:S(2)}, u32[]{:S(2)}) collective-permute-start(bf16[128,128]{1,0:T(8,128)(2,1)S(1)} %get-tuple-element.39), channel_id=1, source_target_pairs={{4,0},{8,4},{12,8},{16,12},{20,16},{24,20},{28,24},{0,28},{5,1},{9... | collective-permute-start | bytes 98312 | tf_op jit(solution)/shard_map/ppermute | solution.py:559
  93.8 5.0 %copy-start.8 = (bf16[128,128]{1,0:T(8,128)(2,1)}, bf16[128,128]{1,0:T(8,128)(2,1)S(1)}, u32[]{:S(2)}) copy-start(bf16[128,128]{1,0:T(8,128)(2,1)S(1)} %collective-permute-done.7.xhi_ref) | copy-start | bytes 98308
  93.8 4.9 %collective-permute-start.8 = (bf16[128,128]{1,0:T(8,128)(2,1)S(1)}, bf16[128,128]{1,0:T(8,128)(2,1)S(1)}, u32[]{:S(2)}, u32[]{:S(2)}) collective-permute-start(bf16[128,128]{1,0:T(8,128)(2,1)S(1)} %get-tuple-element.40), channel_id=1, source_target_pairs={{0,4},{4,8},{8,12},{12,16},{16,20},{20,24},{24,28},{28,0},{1,5},{5... | collective-permute-start | bytes 98312 | tf_op jit(solution)/shard_map/ppermute | solution.py:554
  93.8 5.0 %copy-start.9 = (bf16[128,128]{1,0:T(8,128)(2,1)}, bf16[128,128]{1,0:T(8,128)(2,1)S(1)}, u32[]{:S(2)}) copy-start(bf16[128,128]{1,0:T(8,128)(2,1)S(1)} %collective-permute-done.6.xlo_ref) | copy-start | bytes 98308
  94.9 3.9 %copy-start.12 = (bf16[128,128]{1,0:T(8,128)(2,1)}, bf16[128,128]{1,0:T(8,128)(2,1)S(1)}, u32[]{:S(2)}) copy-start(bf16[128,128]{1,0:T(8,128)(2,1)S(1)} %collective-permute-done.9.yhi_ref) | copy-start | bytes 98308
  98.7 0.6 copy-start.14
  98.8 0.7 copy-start.4
  98.8 0.7 copy-start.5
  98.8 0.9 copy-start

commit v4 on v3

--- a/solution.py
+++ b/solution.py
@@ -4,6 +4,7 @@
 from jax.experimental import pallas as pl
 from jax.experimental.pallas import tpu as pltpu
 from jax.sharding import PartitionSpec as P
+
 
 H = 128
 PLANE = 128
@@ -77,7 +78,7 @@
     fx_ref,
     fy_ref,
     fz_ref,
-    par_ref,
+    par_out,
     e_ref,
     cot_ref,
     gedge_ref,
@@ -88,7 +89,7 @@
     ppad_ref,
     home_ref,
     mid_ref,
-    code_ref,
+    place_ref,
     col_ref,
     u_ref,
     slope_ref,
@@ -103,6 +104,7 @@
     const_ref,
     flip_ref,
     sr_ref,
+    par_ref,
     in_sem,
     out_sem,
 ):
@@ -119,6 +121,9 @@
     w1a = w1e_ref[0:H]
     w1b = w1e_ref[H : 2 * H]
     w1c = w1e_ref[2 * H : 3 * H]
+    w1a_half = (0.5 * w1a.astype(F32)).astype(BF16)
+    w1b_half = (0.5 * w1b.astype(F32)).astype(BF16)
+    w1c_half = (0.5 * w1c.astype(F32)).astype(BF16)
     par_ref[...] = jnp.zeros(par_ref.shape, F32)
     eu_ref[...] = jnp.zeros(eu_ref.shape, F32)
     deg_ref[...] = jnp.zeros(deg_ref.shape, F32)
@@ -130,7 +135,8 @@
     dd_ref[CELLS:ROWS] = jnp.zeros((ROWS - CELLS, 2 * H), F32)
     home_ref[CELLS:ROWS] = jnp.zeros((ROWS - CELLS, H), F32)
     ppad_ref[CELLS + 2 * PLANE :] = jnp.zeros((PAD_ROWS - CELLS - 2 * PLANE, H), F32)
-    const_ref[:, 0:H] = flip(w2e_ref[...])
+    w2_half = (0.5 * w2e_ref[...].astype(F32)).astype(BF16)
+    const_ref[:, 0:H] = flip(w2_half)
     const_ref[:, H:] = hot(iota((H, H), 0) == iota((H, H), 1))
     flip_ref[0:H] = flip(w1b)
     flip_ref[H : 2 * H] = flip(w1c)
@@ -141,20 +147,20 @@
     delta = s - (((r >> 7) + 1) * 204 + (((r >> 2) & 31) + 1) * 6 + (r & 3) + 1)
     inside = s - 204 + 4 * (r >> 7)
     place = jnp.where(delta == 204, r + 4096, jnp.where(delta == -204, r + 8192, inside))
-    code_ref[...] = place * 2048 + r
-
-    ppad_ref[0:PLANE] = dot(xlo_ref[...], w1b)
-    ppad_ref[CELLS + PLANE : CELLS + 2 * PLANE] = dot(xhi_ref[...], w1b)
-    yx_ref[0:PLANE] = dot(ylo_ref[...], w1b)
-    yx_ref[PLANE : 2 * PLANE] = dot(yhi_ref[...], w1b)
-    zx_ref[0] = dot(zlo_ref[...], w1b)
-    zx_ref[1] = dot(zhi_ref[...], w1b)
-    own_ref[...] = dot(node_ref[...], w1b)
+    place_ref[...] = place
+
+    ppad_ref[0:PLANE] = dot(xlo_ref[...], w1b_half)
+    ppad_ref[CELLS + PLANE : CELLS + 2 * PLANE] = dot(xhi_ref[...], w1b_half)
+    yx_ref[0:PLANE] = dot(ylo_ref[...], w1b_half)
+    yx_ref[PLANE : 2 * PLANE] = dot(yhi_ref[...], w1b_half)
+    zx_ref[0] = dot(zlo_ref[...], w1b_half)
+    zx_ref[1] = dot(zhi_ref[...], w1b_half)
+    own_ref[...] = dot(node_ref[...], w1b_half)
     for i in range(N_PLANE):
         at = slice(i * PLANE, (i + 1) * PLANE)
         base = i * STRIDE
         ppad_ref[(i + 1) * PLANE : (i + 2) * PLANE] = own_ref[at]
-        home_ref[at] = dot(node_ref[at], w1c) + b1e_ref[...]
+        home_ref[at] = dot(node_ref[at], w1c_half) + 0.5 * b1e_ref[...]
         for l in range(4):
             mid_ref[pl.ds(base + 7 + l, 32, 6), :] = own_ref[pl.ds(i * PLANE + l, 32, 4), :]
         mid_ref[pl.ds(base + 6, 32, 6), :] = zx_ref[0, i * 32 : (i + 1) * 32, :]
@@ -182,27 +188,24 @@
     def rows_of(t):
         return pl.ds(pl.multiple_of(t * TILE, TILE), TILE)
 
-    def lines(t):
-        return [code_ref[pl.ds(HALF * t + k, 1), :] for k in range(HALF)]
-
-    def columns(t):
-        parts = [jnp.broadcast_to(line, (H, H)).T for line in lines(t)]
-        return jnp.concatenate(parts, axis=0)
-
-    def split(code, w, guard):
-        place = code >> 11
-        home = (code & 2047) - w
-        if guard:
-            place = jnp.where(jnp.logical_and(home >= 0, home < WIN), place, far)
-        return place, home
-
-    def gather_pre(col, w, rest, weights, guard):
-        place, home = split(col, w, guard)
+    def places(t):
+        return [place_ref[pl.ds(HALF * t + k, 1), :] for k in range(HALF)]
+
+    def homes(t):
+        return [recv_ref[pl.ds(HALF * t + k, 1), :] for k in range(HALF)]
+
+    def columns(lines):
+        return jnp.concatenate([jnp.broadcast_to(line, (H, H)).T for line in lines], axis=0)
+
+    def keep_near(place, home, w):
+        return jnp.where(jnp.logical_and(home >= w, home < w + WIN), place, far)
+
+    def gather_pre(place, home, w, rest, weights):
         mid = mid_of(w)
         left = [
-            hot(place - mid == lane),
-            hot(place - w == lane_x),
-            hot(home == lane_self),
+            hot(place == lane + mid),
+            hot(place == lane_x + w),
+            hot(home == lane_self + w),
         ]
         right = [
             mid_ref[pl.ds(mid, MID), :].astype(BF16),
@@ -212,17 +215,18 @@
         ]
         return dot(jnp.concatenate(left + rest, axis=1), jnp.concatenate(right + weights, axis=0))
 
-    def activate(t, z):
-        s = sigmoid(z)
-        u = z * s
+    def activate(t, half):
+        th = jnp.tanh(half)
+        up = 1.0 + th
+        u = half * up
         ub = u.astype(BF16)
         u_ref[rows_of(t), :] = ub
-        slope_ref[rows_of(t), :] = (s + u * (1.0 - s)).astype(BF16)
+        slope_ref[rows_of(t), :] = (up + u * (1.0 - th)).astype(BF16)
         return ub
 
     def collect(t, w, eu):
         ones = jnp.concatenate(
-            [jnp.where((line & 2047) - w == wrow, 1.0, 0.0) for line in lines(t)], axis=1
+            [jnp.where(line == wrow + w, 1.0, 0.0) for line in homes(t)], axis=1
         )
         eu_ref[pl.ds(w, WIN), :] += dot(ones.astype(BF16), eu)
         deg_ref[pl.ds(w, WIN), :] += jnp.broadcast_to(
@@ -230,20 +234,22 @@
         )
 
     def forward_fast(t):
-        col = columns(t)
-        col_ref[rows_of(t), :] = col
+        home = columns(homes(t))
+        col_ref[rows_of(t), :] = home
         e = e_ref[rows_of(t), :]
         w = start_of(t)
-        ub = activate(t, gather_pre(col, w, [e], [w1a], False))
+        ub = activate(t, gather_pre(columns(places(t)), home, w, [e], [w1a_half]))
         collect(t, w, jnp.concatenate([e, ub], axis=1))
 
     def forward_slow(t):
-        col_ref[rows_of(t), :] = columns(t)
-        zacc_ref[:, 0:H] = dot(e_ref[rows_of(t), :], w1a)
+        col_ref[rows_of(t), :] = columns(homes(t))
+        zacc_ref[:, 0:H] = dot(e_ref[rows_of(t), :], w1a_half)
 
         def more(k, carry):
             w = pl.multiple_of(start_of(t) + k * WIN, 8)
-            zacc_ref[:, 0:H] += gather_pre(col_ref[rows_of(t), :], w, [], [], True)
+            home = col_ref[rows_of(t), :]
+            place = keep_near(columns(places(t)), home, w)
+            zacc_ref[:, 0:H] += gather_pre(place, home, w, [], [])
             return carry
 
         lax.fori_loop(0, windows_of(t), more, 0)
@@ -315,24 +321,24 @@
     lax.fori_loop(0, CELLS // TILE, cells, 0, unroll=8)
     copy_cot.wait()
 
-    def spread(col, w, cot):
-        left = jnp.concatenate([hot((col & 2047) - w == lane), cot], axis=1)
+    def spread(home, w, cot):
+        left = jnp.concatenate([hot(home == lane + w), cot], axis=1)
         right = jnp.concatenate([dd_ref[pl.ds(w, H), :].astype(BF16), const_ref[...]], axis=0)
         return dot(left, right)
 
     def scatter(t, w, dz, guard):
         mid = mid_of(w)
         parts = []
-        for line in lines(t):
-            place, home = split(line, w, guard)
-            across = place - w
+        for place, home in zip(places(t), homes(t)):
+            if guard:
+                place = keep_near(place, home, w)
             parts.append(
                 jnp.concatenate(
                     [
-                        hot(place - mid == mrow),
-                        hot(across - 4096 == wrow),
-                        hot(across - 8192 == wrow),
-                        hot(home == wrow),
+                        hot(place == mrow + mid),
+                        hot(place == wrow + (w + 4096)),
+                        hot(place == wrow + (w + 8192)),
+                        hot(home == wrow + w),
                     ],
                     axis=0,
                 )
@@ -437,6 +443,7 @@
     par_ref[7 * H + 1 : 7 * H + 2, :] = jnp.sum(
         wide_ref[2 * H : 2 * H + 8, :], axis=0, keepdims=True
     )
+    par_out[...] = par_ref[...].astype(BF16)
     for c in range(CHUNKS):
         copy_out(c).wait()
 
@@ -457,7 +464,7 @@
             jax.ShapeDtypeStruct((2, PLANE, H), BF16),
             jax.ShapeDtypeStruct((2, PLANE, H), BF16),
             jax.ShapeDtypeStruct((2, CELLS // 4, H), BF16),
-            jax.ShapeDtypeStruct((PARAM_ROWS, H), F32),
+            jax.ShapeDtypeStruct((PARAM_ROWS, H), BF16),
         ],
         scratch_shapes=[
             pltpu.VMEM((EDGES, H), BF16),
@@ -485,6 +492,7 @@
             pltpu.VMEM((H, 2 * H), BF16),
             pltpu.VMEM((3 * H, H), BF16),
             pltpu.VMEM((CELLS, 2 * H), BF16),
+            pltpu.VMEM((PARAM_ROWS, H), F32),
             pltpu.SemaphoreType.DMA((2,)),
             pltpu.SemaphoreType.DMA((CHUNKS,)),
         ],
@@ -493,7 +501,7 @@
     )(receivers, senders, receivers, *arrays)
 
 
-def finish_kernel(
+def node_kernel(
     gown_ref,
     xlo_ref,
     xhi_ref,
@@ -501,23 +509,9 @@
     yhi_ref,
     zlo_ref,
     zhi_ref,
-    par_ref,
     gnode_ref,
-    w1e_ref,
-    w2e_ref,
-    w1n_ref,
-    w2n_ref,
-    bias_ref,
     sum_ref,
 ):
-    par = par_ref[0 : 7 * H + 8, :]
-    square = jnp.sum(par * par)
-    factor = 1.0 / jnp.maximum(1.0, jnp.sqrt(jnp.full((1, H), square / (7 * H * H + 4 * H), F32)))
-    w1e_ref[...] = par_ref[0 : 3 * H, :] * factor
-    w2e_ref[...] = par_ref[3 * H : 4 * H, :] * factor
-    w1n_ref[...] = par_ref[4 * H : 6 * H, :] * factor
-    w2n_ref[...] = par_ref[6 * H : 7 * H, :] * factor
-    bias_ref[...] = par_ref[7 * H : 7 * H + 4, :] * factor
     sum_ref[...] = gown_ref[...]
     sum_ref[0:PLANE] += xlo_ref[...].astype(F32)
     sum_ref[CELLS - PLANE :] += xhi_ref[...].astype(F32)
@@ -531,22 +525,42 @@
     gnode_ref[...] = sum_ref[...].astype(BF16)
 
 
-def finish_call(*arrays):
+def node_call(*arrays):
     return pl.pallas_call(
-        finish_kernel,
-        in_specs=[pl.BlockSpec(memory_space=pltpu.VMEM)] * 8,
-        out_specs=[pl.BlockSpec(memory_space=pltpu.VMEM)] * 6,
+        node_kernel,
+        in_specs=[pl.BlockSpec(memory_space=pltpu.VMEM)] * 7,
+        out_specs=pl.BlockSpec(memory_space=pltpu.VMEM),
+        out_shape=jax.ShapeDtypeStruct((CELLS, H), BF16),
+        scratch_shapes=[pltpu.VMEM((CELLS, H), F32)],
+        name="nodes",
+    )(*arrays)
+
+
+def clip_kernel(par_ref, w1e_ref, w2e_ref, w1n_ref, w2n_ref, bias_ref):
+    par = par_ref[0 : 7 * H + 16, :].astype(F32)
+    square = jnp.sum(par * par)
+    factor = 1.0 / jnp.maximum(1.0, jnp.sqrt(jnp.full((1, H), square / (7 * H * H + 4 * H), F32)))
+    w1e_ref[...] = par[0 : 3 * H] * factor
+    w2e_ref[...] = par[3 * H : 4 * H] * factor
+    w1n_ref[...] = par[4 * H : 6 * H] * factor
+    w2n_ref[...] = par[6 * H : 7 * H] * factor
+    bias_ref[...] = par[7 * H : 7 * H + 4] * factor
+
+
+def clip_call(par):
+    return pl.pallas_call(
+        clip_kernel,
+        in_specs=[pl.BlockSpec(memory_space=pltpu.VMEM)],
+        out_specs=[pl.BlockSpec(memory_space=pltpu.VMEM)] * 5,
         out_shape=[
-            jax.ShapeDtypeStruct((CELLS, H), BF16),
             jax.ShapeDtypeStruct((3 * H, H), F32),
             jax.ShapeDtypeStruct((H, H), F32),
             jax.ShapeDtypeStruct((2 * H, H), F32),
             jax.ShapeDtypeStruct((H, H), F32),
             jax.ShapeDtypeStruct((4, H), F32),
         ],
-        scratch_shapes=[pltpu.VMEM((CELLS, H), F32)],
-        name="finish",
-    )(*arrays)
+        name="clip",
+    )(par)
 
 
 def from_previous(value, axis):
@@ -564,7 +578,8 @@
     for axis in AXES:
         count *= lax.axis_size(axis)
     chunks = rows.reshape(count, -1, H)
-    mine = jnp.sum(lax.all_to_all(chunks, AXES, 0, 0, tiled=True), axis=0)
+    parts = lax.all_to_all(chunks, AXES, 0, 0, tiled=True)
+    mine = jnp.sum(parts.astype(F32), axis=0).astype(BF16)
     copies = jnp.broadcast_to(mine[None], (count,) + mine.shape)
     return lax.all_to_all(copies, AXES, 0, 0, tiled=True).reshape(-1, H)
 
@@ -612,7 +627,7 @@
         w2_node,
     )
     full = sum_over_devices(par)
-    gnode, gw1e, gw2e, gw1n, gw2n, gbias = finish_call(
+    gnode = node_call(
         gown,
         from_previous(fx[1], "gx"),
         from_next(fx[0], "gx"),
@@ -620,8 +635,8 @@
         from_next(fy[0], "gy"),
         from_previous(fz[1], "gz"),
         from_next(fz[0], "gz"),
-        full,
     )
+    gw1e, gw2e, gw1n, gw2n, gbias = clip_call(full)
     return (
         gnode.reshape(node_latent.shape),
         gedge.reshape(edge_latent.shape),

time: 103 us -> 97.2 us (0.944)
  blocking collectives: 23 us -> 0 us
  starting transfers between devices: 25.4 us -> 39.1 us
  local copies, waits for them, and re-layouts: 5.89 us -> 8.83 us
  Pallas kernels: 37.3 us -> 38.4 us
    all_to_all x1 -> x0, blocking collectives: 23 us -> none  [sum_over_devices(): mine = jnp.sum(lax.all_to_all(chunks, AXES, 0, 0, tiled=True), axis=0)]
    all_to_all x0 -> x1, starting transfers between devices: none -> 11.4 us  [sum_over_devices(): parts = lax.all_to_all(chunks, AXES, 0, 0, tiled=True)]
    all_to_all x0 -> x1, waiting for transfers between devices: none -> 7.19 us  [sum_over_devices(): parts = lax.all_to_all(chunks, AXES, 0, 0, tiled=True)]
    ppermute x6, waiting for transfers between devices: 7.69 us -> 0.99 us  [from_previous(): return lax.ppermute(value, axis, [(k, (k + 1) % n) for k in range(n)])]
    ppermute x6, starting transfers between devices: 6.35 us -> 11.8 us  [from_previous(): return lax.ppermute(value, axis, [(k, (k + 1) % n) for k in range(n)])]
    ppermute x6, starting transfers between devices: 15.2 us -> 11.8 us  [from_next(): return lax.ppermute(value, axis, [((k + 1) % n, k) for k in range(n)])]
    pallas_call x1 -> x2, Pallas kernels: 2.76 us -> 4.34 us  [the longest x1 2.37 us: node_call(): pl.pallas_call(node_kernel, in_specs=[pl.BlockSpec(memory_space=pltpu.VME...]
    unnamed x34 -> x28, local copies, waits for them, and re-layouts: 1.56 us -> 2.08 us
  transfers between devices with their start and end apart: 13 -> 14, of which waited for: 4 -> 4; matrix products, arithmetic and copies ran while one was open for 3% -> 5% of each run, Pallas kernels for 0% -> 2%
where the time goes in v4:
time: 97.2 us; the launch traced here: 96.5 us
  starting transfers between devices  39.1 us (40%)
  Pallas kernels  38.4 us (40%)
  waiting for transfers between devices  9.27 us (10%)
  local copies, waits for them, and re-layouts  8.83 us (9%)
    pallas_call x1, Pallas kernels, layer_call(): pl.pallas_call(layer_kernel, in_specs=[smem] + [vmem] * 10 + [hbm] * 2 +...  34 us
    ppermute x6, starting transfers between devices, from_previous(): return lax.ppermute(value, axis, [(k, (k + 1) % n) for k in range(n)])  11.8 us
    ppermute x6, starting transfers between devices, from_next(): return lax.ppermute(value, axis, [((k + 1) % n, k) for k in range(n)])  11.8 us
    all_to_all x1, starting transfers between devices, sum_over_devices(): parts = lax.all_to_all(chunks, AXES, 0, 0, tiled=True)  11.4 us
    all_to_all x1, waiting for transfers between devices, sum_over_devices(): parts = lax.all_to_all(chunks, AXES, 0, 0, tiled=True)  7.19 us
    all_to_all x1, starting transfers between devices, sum_over_devices(): return lax.all_to_all(copies, AXES, 0, 0, tiled=True).reshape(-1, H)  3.99 us
    pallas_call x1, Pallas kernels, node_call(): pl.pallas_call(node_kernel, in_specs=[pl.BlockSpec(memory_space=pltpu.VME...  2.37 us
    unnamed x28, local copies, waits for them, and re-layouts  2.08 us
  transfers between devices with their start and end apart: 14, of which 4 were waited for; matrix products, arithmetic and copies ran while one was open for 5% of the time, Pallas kernels for 2%

profile of v4, /device:TPU:1, one launch (start us, length us, event | category | flops | bytes accessed | tf_op | source)
XLA Modules:
  0.0 96.5 jit_solution(7014739403519008344)
XLA Ops:
  0.6 1.9 %fusion = (bf16[16,32,1,128]{3,2,1,0:T(2,128)(2,1)S(1)}, bf16[16,32,1,128]{3,2,1,0:T(2,128)(2,1)S(1)}) fusion(bf16[16,32,4,128]{3,2,1,0:T(4,128)(2,1)} %param.13), kind=kLoop, calls=%fused_computation.10 | loop fusion | bytes 524288 | tf_op jit(solution)/shard_map/slice | solution.py:603
  2.5 4.2 %collective-permute-start.4 = (bf16[16,32,128]{2,1,0:T(8,128)(2,1)S(1)}, bf16[16,32,128]{2,1,0:T(8,128)(2,1)S(1)}, u32[]{:S(2)}, u32[]{:S(2)}) collective-permute-start(bf16[16,32,128]{2,1,0:T(8,128)(2,1)S(1)} %bitcast.52), channel_id=1, source_target_pairs={{0,1},{1,2},{2,3},{3,0},{4,5},{5,6},{6,7},{7,4},{8,9},{9,10},{10,1... | collective-permute-start | bytes 393224 | tf_op jit(solution)/shard_map/ppermute | solution.py:568
  6.7 0.1 collective-permute-start.5
  6.8 0.8 slice_bitcast_fusion.6
  7.6 1.4 %collective-permute-start = (bf16[32,4,128]{2,1,0:T(4,128)(2,1)S(1)}, bf16[32,4,128]{2,1,0:T(4,128)(2,1)S(1)}, u32[]{:S(2)}, u32[]{:S(2)}) collective-permute-start(bf16[32,4,128]{2,1,0:T(4,128)(2,1)S(1)} %get-tuple-element.34), channel_id=1, source_target_pairs={{0,32},{32,64},{64,96},{96,0},{1,33},{33,65},{65,97},{97,1},{2,34}... | collective-permute-start | bytes 98312 | tf_op jit(solution)/shard_map/ppermute | solution.py:568
  9.0 1.5 %collective-permute-start.1 = (bf16[32,4,128]{2,1,0:T(4,128)(2,1)S(1)}, bf16[32,4,128]{2,1,0:T(4,128)(2,1)S(1)}, u32[]{:S(2)}, u32[]{:S(2)}) collective-permute-start(bf16[32,4,128]{2,1,0:T(4,128)(2,1)S(1)} %get-tuple-element.33), channel_id=1, source_target_pairs={{32,0},{64,32},{96,64},{0,96},{33,1},{65,33},{97,65},{1,97},{34,2}... | collective-permute-start | bytes 98312 | tf_op jit(solution)/shard_map/ppermute | solution.py:573
  10.5 0.8 fusion.1
  11.3 0.4 collective-permute-start.2
  11.7 3.8 %collective-permute-start.3 = (bf16[16,2,4,128]{3,2,1,0:T(4,128)(2,1)S(1)}, bf16[16,2,4,128]{3,2,1,0:T(4,128)(2,1)S(1)}, u32[]{:S(2)}, u32[]{:S(2)}) collective-permute-start(bf16[16,2,4,128]{3,2,1,0:T(4,128)(2,1)S(1)} %get-tuple-element.31), channel_id=1, source_target_pairs={{4,0},{8,4},{12,8},{16,12},{20,16},{24,20},{28,24},{0,28},{5,1},{9... | collective-permute-start | bytes 98312 | tf_op jit(solution)/shard_map/ppermute | solution.py:573
  15.5 0.9 collective-permute-done.2
  16.5 0.1 collective-permute-done.3
  16.6 0.5 copy-done.9
  17.1 0.1 copy-done.11
  17.3 34.0 %layer.1 = (bf16[12288,128]{1,0:T(8,128)(2,1)}, f32[2048,128]{1,0:T(8,128)}, bf16[2,128,128]{2,1,0:T(8,128)(2,1)}, bf16[2,128,128]{2,1,0:T(8,128)(2,1)}, bf16[2,...) custom-call(s32[96,128]{1,0:T(8,128)} %bitcast.48, s32[96,128]{1,0:T(8,128)} %bitcast.54, s32[96,128]{1,0:T(8,128)} %bitcast.49, ...), custom_call_target="tpu_custom_call" | custom-call | tf_op jit(solution)/shard_map/layer/pallas_call | solution.py:457
  51.3 11.4 %all-to-all-start = ((bf16[128,8,128]{2,1,0:T(8,128)(2,1)}), bf16[128,8,128]{2,1,0:T(8,128)(2,1)S(1)}, u32[]{:S(2)}, u32[]{:S(2)}) async-start(bf16[128,8,128]{2,1,0:T(8,128)(2,1)} %bitcast.47), calls=%async_computation | async-start | bytes 524288 | tf_op jit(solution)/shard_map/all_to_all | solution.py:581
  62.7 1.0 %slice_bitcast_fusion = (bf16[512,128]{1,0:T(8,128)(2,1)S(1)}, bf16[512,128]{1,0:T(8,128)(2,1)S(1)}) fusion(bf16[2,512,128]{2,1,0:T(8,128)(2,1)} %get-tuple-element.21), kind=kLoop, calls=%fused_computation.2 | loop fusion | bytes 524288 | tf_op jit(solution)/shard_map/squeeze | solution.py:637
  63.7 3.2 %collective-permute-start.10 = (bf16[512,128]{1,0:T(8,128)(2,1)S(1)}, bf16[512,128]{1,0:T(8,128)(2,1)S(1)}, u32[]{:S(2)}, u32[]{:S(2)}) collective-permute-start(bf16[512,128]{1,0:T(8,128)(2,1)S(1)} %get-tuple-element.36), channel_id=1, source_target_pairs={{0,1},{1,2},{2,3},{3,0},{4,5},{5,6},{6,7},{7,4},{8,9},{9,10},{10,1... | collective-permute-start | bytes 393224 | tf_op jit(solution)/shard_map/ppermute | solution.py:568
  66.9 7.2 %all-to-all-done = bf16[128,8,128]{2,1,0:T(8,128)(2,1)S(1)} async-done(((bf16[128,8,128]{2,1,0:T(8,128)(2,1)}), bf16[128,8,128]{2,1,0:T(8,128)(2,1)S(1)}, u32[]{:S(2)}, u32[]{:S(2)}) %all-to-all-start) | async-done | bytes 262176 | tf_op jit(solution)/shard_map/all_to_all | solution.py:581
  74.1 0.1 reduce_sum.12
  74.3 0.7 broadcast_in_dim.2
  75.0 4.0 %all-to-all-start.1 = ((bf16[128,8,128]{2,1,0:T(8,128)(2,1)}), bf16[128,8,128]{2,1,0:T(8,128)(2,1)S(1)}, u32[]{:S(2)}, u32[]{:S(2)}) async-start(bf16[128,8,128]{2,1,0:T(8,128)(2,1)} %broadcast_in_dim.2), calls=%async_computation.1 | async-start | bytes 524288 | tf_op jit(solution)/shard_map/all_to_all | solution.py:584
  79.0 0.8 slice_bitcast_fusion.4
  79.8 1.4 %collective-permute-start.6 = (bf16[128,128]{1,0:T(8,128)(2,1)S(1)}, bf16[128,128]{1,0:T(8,128)(2,1)S(1)}, u32[]{:S(2)}, u32[]{:S(2)}) collective-permute-start(bf16[128,128]{1,0:T(8,128)(2,1)S(1)} %get-tuple-element.40), channel_id=1, source_target_pairs={{0,32},{32,64},{64,96},{96,0},{1,33},{33,65},{65,97},{97,1},{2,34}... | collective-permute-start | bytes 98312 | tf_op jit(solution)/shard_map/ppermute | solution.py:568
  81.1 1.3 %collective-permute-start.7 = (bf16[128,128]{1,0:T(8,128)(2,1)S(1)}, bf16[128,128]{1,0:T(8,128)(2,1)S(1)}, u32[]{:S(2)}, u32[]{:S(2)}) collective-permute-start(bf16[128,128]{1,0:T(8,128)(2,1)S(1)} %get-tuple-element.39), channel_id=1, source_target_pairs={{32,0},{64,32},{96,64},{0,96},{33,1},{65,33},{97,65},{1,97},{34,2}... | collective-permute-start | bytes 98312 | tf_op jit(solution)/shard_map/ppermute | solution.py:573
  82.5 0.8 slice_bitcast_fusion.2
  83.3 1.3 %collective-permute-start.8 = (bf16[128,128]{1,0:T(8,128)(2,1)S(1)}, bf16[128,128]{1,0:T(8,128)(2,1)S(1)}, u32[]{:S(2)}, u32[]{:S(2)}) collective-permute-start(bf16[128,128]{1,0:T(8,128)(2,1)S(1)} %get-tuple-element.38), channel_id=1, source_target_pairs={{0,4},{4,8},{8,12},{12,16},{16,20},{20,24},{24,28},{28,0},{1,5},{5... | collective-permute-start | bytes 98312 | tf_op jit(solution)/shard_map/ppermute | solution.py:568
  84.6 5.1 %collective-permute-start.9 = (bf16[128,128]{1,0:T(8,128)(2,1)S(1)}, bf16[128,128]{1,0:T(8,128)(2,1)S(1)}, u32[]{:S(2)}, u32[]{:S(2)}) collective-permute-start(bf16[128,128]{1,0:T(8,128)(2,1)S(1)} %get-tuple-element.37), channel_id=1, source_target_pairs={{4,0},{8,4},{12,8},{16,12},{20,16},{24,20},{28,24},{0,28},{5,1},{9... | collective-permute-start | bytes 98312 | tf_op jit(solution)/shard_map/ppermute | solution.py:573
  89.7 1.0 %collective-permute-done.9.yhi_ref = bf16[128,128]{1,0:T(8,128)(2,1)S(1)} collective-permute-done((bf16[128,128]{1,0:T(8,128)(2,1)S(1)}, bf16[128,128]{1,0:T(8,128)(2,1)S(1)}, u32[]{:S(2)}, u32[]{:S(2)}) %collective-permute-start.9) | collective-permute-done | bytes 32800 | tf_op jit(solution)/shard_map/ppermute | solution.py:573
  90.8 0.6 copy-done.12
  91.4 2.4 %nodes.1 = bf16[2048,128]{1,0:T(8,128)(2,1)} custom-call(f32[2048,128]{1,0:T(8,128)} %get-tuple-element.18.gown_ref, bf16[128,128]{1,0:T(8,128)(2,1)} %copy-done.7, bf16[128,128]{1,0:T(8,128)(2,1)} %copy-done.8, bf16[128,128]{1,0:T(8,128)(2,1)} %copy-done.10, bf16[128,128]{1,0:T(8,128)(2,1)} %copy-done.12, bf16[512,128]{1,0:T(8,128)(2,1)} %copy-done.3, ...), custom_call_target="tpu_custom_call" | custom-call | tf_op jit(solution)/shard_map/nodes/pallas_call | solution.py:529
  93.8 0.7 copy-done
  94.5 2.0 %clip.1 = (f32[384,128]{1,0:T(8,128)}, f32[128,128]{1,0:T(8,128)}, f32[256,128]{1,0:T(8,128)}, f32[128,128]{1,0:T(8,128)}, f32[4,128]{1,0:T(4,128)}) custom-call(bf16[1024,128]{1,0:T(8,128)(2,1)} %bitcast.44), custom_call_target="tpu_custom_call" | custom-call | tf_op jit(solution)/shard_map/clip/pallas_call | solution.py:551
  (35 shorter events, 0.3 us)
Async XLA Ops:
  2.5 14.0 %collective-permute-start.4 = (bf16[16,32,128]{2,1,0:T(8,128)(2,1)S(1)}, bf16[16,32,128]{2,1,0:T(8,128)(2,1)S(1)}, u32[]{:S(2)}, u32[]{:S(2)}) collective-permute-start(bf16[16,32,128]{2,1,0:T(8,128)(2,1)S(1)} %bitcast.52), channel_id=1, source_target_pairs={{0,1},{1,2},{2,3},{3,0},{4,5},{5,6},{6,7},{7,4},{8,9},{9,10},{10,1... | collective-permute-start | bytes 393224 | tf_op jit(solution)/shard_map/ppermute | solution.py:568
  6.7 9.8 %collective-permute-start.5 = (bf16[16,32,128]{2,1,0:T(8,128)(2,1)S(1)}, bf16[16,32,128]{2,1,0:T(8,128)(2,1)S(1)}, u32[]{:S(2)}, u32[]{:S(2)}) collective-permute-start(bf16[16,32,128]{2,1,0:T(8,128)(2,1)S(1)} %bitcast.53), channel_id=1, source_target_pairs={{1,0},{2,1},{3,2},{0,3},{5,4},{6,5},{7,6},{4,7},{9,8},{10,9},{11,1... | collective-permute-start | bytes 393224 | tf_op jit(solution)/shard_map/ppermute | solution.py:573
  7.6 4.1 %collective-permute-start = (bf16[32,4,128]{2,1,0:T(4,128)(2,1)S(1)}, bf16[32,4,128]{2,1,0:T(4,128)(2,1)S(1)}, u32[]{:S(2)}, u32[]{:S(2)}) collective-permute-start(bf16[32,4,128]{2,1,0:T(4,128)(2,1)S(1)} %get-tuple-element.34), channel_id=1, source_target_pairs={{0,32},{32,64},{64,96},{96,0},{1,33},{33,65},{65,97},{97,1},{2,34}... | collective-permute-start | bytes 98312 | tf_op jit(solution)/shard_map/ppermute | solution.py:568
  9.0 6.5 %collective-permute-start.1 = (bf16[32,4,128]{2,1,0:T(4,128)(2,1)S(1)}, bf16[32,4,128]{2,1,0:T(4,128)(2,1)S(1)}, u32[]{:S(2)}, u32[]{:S(2)}) collective-permute-start(bf16[32,4,128]{2,1,0:T(4,128)(2,1)S(1)} %get-tuple-element.33), channel_id=1, source_target_pairs={{32,0},{64,32},{96,64},{0,96},{33,1},{65,33},{97,65},{1,97},{34,2}... | collective-permute-start | bytes 98312 | tf_op jit(solution)/shard_map/ppermute | solution.py:573
  11.3 5.2 %collective-permute-start.2 = (bf16[16,2,4,128]{3,2,1,0:T(4,128)(2,1)S(1)}, bf16[16,2,4,128]{3,2,1,0:T(4,128)(2,1)S(1)}, u32[]{:S(2)}, u32[]{:S(2)}) collective-permute-start(bf16[16,2,4,128]{3,2,1,0:T(4,128)(2,1)S(1)} %get-tuple-element.32), channel_id=1, source_target_pairs={{0,4},{4,8},{8,12},{12,16},{16,20},{20,24},{24,28},{28,0},{1,5},{5... | collective-permute-start | bytes 98312 | tf_op jit(solution)/shard_map/ppermute | solution.py:568
  11.7 4.8 %copy-start.5 = (bf16[32,4,128]{2,1,0:T(4,128)(2,1)}, bf16[32,4,128]{2,1,0:T(4,128)(2,1)S(1)}, u32[]{:S(2)}) copy-start(bf16[32,4,128]{2,1,0:T(4,128)(2,1)S(1)} %collective-permute-done) | copy-start | bytes 98308
  11.7 4.8 %collective-permute-start.3 = (bf16[16,2,4,128]{3,2,1,0:T(4,128)(2,1)S(1)}, bf16[16,2,4,128]{3,2,1,0:T(4,128)(2,1)S(1)}, u32[]{:S(2)}, u32[]{:S(2)}) collective-permute-start(bf16[16,2,4,128]{3,2,1,0:T(4,128)(2,1)S(1)} %get-tuple-element.31), channel_id=1, source_target_pairs={{4,0},{8,4},{12,8},{16,12},{20,16},{24,20},{28,24},{0,28},{5,1},{9... | collective-permute-start | bytes 98312 | tf_op jit(solution)/shard_map/ppermute | solution.py:573
  15.5 1.1 %copy-start.6 = (bf16[32,4,128]{2,1,0:T(4,128)(2,1)}, bf16[32,4,128]{2,1,0:T(4,128)(2,1)S(1)}, u32[]{:S(2)}) copy-start(bf16[32,4,128]{2,1,0:T(4,128)(2,1)S(1)} %collective-permute-done.1) | copy-start | bytes 98308
  16.5 0.6 copy-start.9
  16.5 0.6 copy-start.11
  16.6 0.7 copy-start.1
  16.6 0.7 copy-start.2
  51.3 22.8 %all-to-all-start = ((bf16[128,8,128]{2,1,0:T(8,128)(2,1)}), bf16[128,8,128]{2,1,0:T(8,128)(2,1)S(1)}, u32[]{:S(2)}, u32[]{:S(2)}) async-start(bf16[128,8,128]{2,1,0:T(8,128)(2,1)} %bitcast.47), calls=%async_computation | async-start | bytes 524288 | tf_op jit(solution)/shard_map/all_to_all | solution.py:581
  63.7 27.0 %collective-permute-start.10 = (bf16[512,128]{1,0:T(8,128)(2,1)S(1)}, bf16[512,128]{1,0:T(8,128)(2,1)S(1)}, u32[]{:S(2)}, u32[]{:S(2)}) collective-permute-start(bf16[512,128]{1,0:T(8,128)(2,1)S(1)} %get-tuple-element.36), channel_id=1, source_target_pairs={{0,1},{1,2},{2,3},{3,0},{4,5},{5,6},{6,7},{7,4},{8,9},{9,10},{10,1... | collective-permute-start | bytes 393224 | tf_op jit(solution)/shard_map/ppermute | solution.py:568
  66.9 23.8 %collective-permute-start.11 = (bf16[512,128]{1,0:T(8,128)(2,1)S(1)}, bf16[512,128]{1,0:T(8,128)(2,1)S(1)}, u32[]{:S(2)}, u32[]{:S(2)}) collective-permute-start(bf16[512,128]{1,0:T(8,128)(2,1)S(1)} %get-tuple-element.35), channel_id=1, source_target_pairs={{1,0},{2,1},{3,2},{0,3},{5,4},{6,5},{7,6},{4,7},{9,8},{10,9},{11,1... | collective-permute-start | bytes 393224 | tf_op jit(solution)/shard_map/ppermute | solution.py:573
  75.0 18.8 %all-to-all-start.1 = ((bf16[128,8,128]{2,1,0:T(8,128)(2,1)}), bf16[128,8,128]{2,1,0:T(8,128)(2,1)S(1)}, u32[]{:S(2)}, u32[]{:S(2)}) async-start(bf16[128,8,128]{2,1,0:T(8,128)(2,1)} %broadcast_in_dim.2), calls=%async_computation.1 | async-start | bytes 524288 | tf_op jit(solution)/shard_map/all_to_all | solution.py:584
  79.8 4.8 %collective-permute-start.6 = (bf16[128,128]{1,0:T(8,128)(2,1)S(1)}, bf16[128,128]{1,0:T(8,128)(2,1)S(1)}, u32[]{:S(2)}, u32[]{:S(2)}) collective-permute-start(bf16[128,128]{1,0:T(8,128)(2,1)S(1)} %get-tuple-element.40), channel_id=1, source_target_pairs={{0,32},{32,64},{64,96},{96,0},{1,33},{33,65},{65,97},{97,1},{2,34}... | collective-permute-start | bytes 98312 | tf_op jit(solution)/shard_map/ppermute | solution.py:568
  81.1 8.5 %collective-permute-start.7 = (bf16[128,128]{1,0:T(8,128)(2,1)S(1)}, bf16[128,128]{1,0:T(8,128)(2,1)S(1)}, u32[]{:S(2)}, u32[]{:S(2)}) collective-permute-start(bf16[128,128]{1,0:T(8,128)(2,1)S(1)} %get-tuple-element.39), channel_id=1, source_target_pairs={{32,0},{64,32},{96,64},{0,96},{33,1},{65,33},{97,65},{1,97},{34,2}... | collective-permute-start | bytes 98312 | tf_op jit(solution)/shard_map/ppermute | solution.py:573
  83.3 6.4 %collective-permute-start.8 = (bf16[128,128]{1,0:T(8,128)(2,1)S(1)}, bf16[128,128]{1,0:T(8,128)(2,1)S(1)}, u32[]{:S(2)}, u32[]{:S(2)}) collective-permute-start(bf16[128,128]{1,0:T(8,128)(2,1)S(1)} %get-tuple-element.38), channel_id=1, source_target_pairs={{0,4},{4,8},{8,12},{12,16},{16,20},{20,24},{24,28},{28,0},{1,5},{5... | collective-permute-start | bytes 98312 | tf_op jit(solution)/shard_map/ppermute | solution.py:568
  84.6 6.1 %copy-start.7 = (bf16[128,128]{1,0:T(8,128)(2,1)}, bf16[128,128]{1,0:T(8,128)(2,1)S(1)}, u32[]{:S(2)}) copy-start(bf16[128,128]{1,0:T(8,128)(2,1)S(1)} %collective-permute-done.6.xlo_ref) | copy-start | bytes 98308
  84.6 6.1 %collective-permute-start.9 = (bf16[128,128]{1,0:T(8,128)(2,1)S(1)}, bf16[128,128]{1,0:T(8,128)(2,1)S(1)}, u32[]{:S(2)}, u32[]{:S(2)}) collective-permute-start(bf16[128,128]{1,0:T(8,128)(2,1)S(1)} %get-tuple-element.37), channel_id=1, source_target_pairs={{4,0},{8,4},{12,8},{16,12},{20,16},{24,20},{28,24},{0,28},{5,1},{9... | collective-permute-start | bytes 98312 | tf_op jit(solution)/shard_map/ppermute | solution.py:573
  89.7 1.1 %copy-start.8 = (bf16[128,128]{1,0:T(8,128)(2,1)}, bf16[128,128]{1,0:T(8,128)(2,1)S(1)}, u32[]{:S(2)}) copy-start(bf16[128,128]{1,0:T(8,128)(2,1)S(1)} %collective-permute-done.7.xhi_ref) | copy-start | bytes 98308
  89.7 1.1 %copy-start.10 = (bf16[128,128]{1,0:T(8,128)(2,1)}, bf16[128,128]{1,0:T(8,128)(2,1)S(1)}, u32[]{:S(2)}) copy-start(bf16[128,128]{1,0:T(8,128)(2,1)S(1)} %collective-permute-done.8.ylo_ref) | copy-start | bytes 98308
  90.7 0.6 copy-start.12
  90.7 0.7 copy-start.3
  90.7 0.7 copy-start.4
  93.8 0.7 copy-start
